TPU v7x, 256 devices: a whole 4x4x8 slice. The times are simulated.
256 devices in a mesh: loc: 32 (over y, x, core), tm: 8 (over z).
Axes of the slice: x: 4, y: 4, z: 8, core: 2. Of those that a mesh axis runs over, the one named last changes fastest.
Arguments:
- observed: float32 [4096, 1024], P('loc', 'tm'), may hold values from -6 to 6
- observed_mask: int32 [4096, 1024], P('loc', 'tm'), may hold values 0 or 1
- training_site_positions: float32 [2, 4096], replicated, may hold values from 0 to 1
- time_stamps: float32 [1024], replicated, may hold values from 0 to 1
- noise_var: float32 [1024], P('tm'), may hold values from 0.2 to 2
- test_coords: float32 [2, 4096], replicated, may hold values from 0 to 1
- site_order: int32 [4096], replicated, may hold values from 0 to 4095, each once
Outputs:
- solver_estimate: float32 [4096, 1024], P('loc', 'tm')
- posterior_mean_field: float32 [4096, 1024], P('loc', 'tm')
Inputs may be any that keep to these rules, and one draw needn't show every extreme that they name: `site_order`: each test site appears once.
All inputs are finite; a program needn't handle non-finite values. No bound on the sum of `observed_mask` on one device may be relied on, other than what follows from the above.
Results may differ from a plain program's by a relative error of at most 0.00022.
Values sent between devices are 32-bit elements; how exact they have to be, the bound alone decides.
No kernel may reach another device: no remote copies, remote signals or barrier semaphores. Data moves between devices by JAX's collectives and lax.ppermute only.
A program may use at most 64 MiB of HBM per device.

v0:
```python
import functools
import math

import jax
import jax.numpy as jnp
from jax import lax
from jax.experimental import pallas as pl
from jax.experimental.pallas import tpu as pltpu
from jax.sharding import Mesh
from jax.sharding import PartitionSpec as P


LOC = ("loc_0", "loc_1", "loc_2")
EVERYONE = ("loc_0", "loc_1", "loc_2", "tm")

root_three = math.sqrt(3.0)
space_reach = 2.5
time_reach = 5.0
amplitude = 0.1
tiny = 1e-36
TILE = 128
f32, bf16 = jnp.float32, jnp.bfloat16
VMEM = pl.BlockSpec(memory_space=pltpu.VMEM)


def ahead(block, axis, shift):
    size = lax.axis_size(axis)
    return lax.ppermute(block, axis, [((i + shift) % size, i) for i in range(size)])


def gathered(block, axis, order):
    held = {0: block}
    for shift in order:
        held[shift] = ahead(block, axis, shift)
    return [held[shift] for shift in range(len(held))]


def neighbours(block):
    return lax.ppermute(block, "tm", [(i, i ^ 1) for i in range(lax.axis_size("tm"))])


def swapped(block):
    return lax.ppermute(block, "loc_2", [(0, 1), (1, 0)])


def halves(value):
    high = value.astype(bf16)
    return high, (value - high.astype(f32)).astype(bf16)


def product(left, right):
    return jnp.dot(left, right, preferred_element_type=f32)


def call(kernel, outs, *args, flops, scratch=()):
    shapes = [jax.ShapeDtypeStruct(shape, dtype) for shape, dtype in outs]
    moved = sum(math.prod(s.shape) * s.dtype.itemsize for s in list(args) + shapes)
    return pl.pallas_call(
        kernel,
        out_shape=shapes,
        in_specs=[VMEM] * len(args),
        out_specs=[VMEM] * len(shapes),
        scratch_shapes=list(scratch),
        cost_estimate=pl.CostEstimate(flops=flops, bytes_accessed=moved, transcendentals=0),
        compiler_params=pltpu.CompilerParams(vmem_limit_bytes=16 * 1024 * 1024),
    )(*args)


def matern(scaled):
    return (1.0 + scaled) * jnp.exp(-scaled)


def root(square):
    return square * lax.rsqrt(jnp.maximum(square, tiny))


def upright(lines):
    filler = jnp.zeros((TILE - lines.shape[0], TILE), f32)
    return jnp.concatenate([lines, filler], 0).T


def lanes(ref, index):
    return ref[:, pl.ds(pl.multiple_of(index * TILE, TILE), TILE)]


def row_places():
    y, x, c = (lax.axis_index(axis) for axis in LOC)
    return [((((y + s) & 3) * 4) + x) * 2 + c for s in range(4)]


def column_places():
    y, x, c = (lax.axis_index(axis) for axis in LOC)
    return [(y * 4 + ((x + s) & 3)) * 2 + (c ^ other) for other in range(2) for s in range(4)]


def fill(points_ref, at_ref, length, high_ref, low_ref):
    step = 16
    factor = root_three / length

    @pl.loop(0, 4 * TILE // step, unroll=2)
    def _(i):
        rows = pl.ds(pl.multiple_of(i * step, step), step)
        dx = at_ref[rows, 0:1] - points_ref[0:1, :]
        dy = at_ref[rows, 1:2] - points_ref[1:2, :]
        high, low = halves(matern(root(dx * dx + dy * dy) * factor))
        high_ref[rows, :] = high
        low_ref[rows, :] = low


def time_kernel(stamps_ref, high_ref, low_ref, *, length):
    own = lax.axis_index("tm")
    columns = upright(jnp.concatenate([stamps_ref[pl.ds(t, 1), :] for t in (own, own ^ 1)], 0))
    for s in range(2):
        for t in range(4):
            line = stamps_ref[pl.ds((own + 2 * t) & 7, 1), :]
            apart = jnp.abs(columns[:, s : s + 1] - line)
            high, low = halves(matern(apart * (root_three / length)))
            high_ref[s * TILE : (s + 1) * TILE, t * TILE : (t + 1) * TILE] = high
            low_ref[s * TILE : (s + 1) * TILE, t * TILE : (t + 1) * TILE] = low


def set_columns(sites_ref, points_ref):
    for k, place in enumerate(column_places()):
        points_ref[:, k * TILE : (k + 1) * TILE] = lanes(sites_ref, place)


def train_kernel(stamps_ref, sites_ref, noise_ref, *refs, time_length, length):
    time_high_ref, time_low_ref, high_ref, low_ref, noise_out_ref, points_ref, at_ref = refs
    noise_out_ref[...] = noise_ref[...]
    time_kernel(stamps_ref, time_high_ref, time_low_ref, length=time_length)
    set_columns(sites_ref, points_ref)
    lines = jnp.concatenate([lanes(sites_ref, place) for place in row_places()], 0)
    columns = upright(lines)
    for s in range(4):
        at_ref[s * TILE : (s + 1) * TILE, 0:2] = columns[:, 2 * s : 2 * s + 2]
    fill(points_ref, at_ref, length, high_ref, low_ref)


def test_kernel(sites_ref, tests_ref, order_ref, high_ref, low_ref, points_ref, at_ref, *, length):
    set_columns(sites_ref, points_ref)
    coords = tests_ref[...]
    first = coords.astype(bf16)
    rest = coords - first.astype(f32)
    second = rest.astype(bf16)
    third = (rest - second.astype(f32)).astype(bf16)
    parts = jnp.concatenate([first, second, third], 0)
    chunk = 512
    lines = []
    for place in row_places():
        wanted = order_ref[pl.ds(place, 1), :]
        found = jnp.zeros((6, TILE), f32)
        for start in range(0, coords.shape[1], chunk):
            number = lax.broadcasted_iota(jnp.int32, (chunk, TILE), 0) + start
            chosen = jnp.where(number == wanted, 1.0, 0.0).astype(bf16)
            found = found + product(parts[:, start : start + chunk], chosen)
        lines.append(found[0:2] + found[2:4] + found[4:6])
    columns = upright(jnp.concatenate(lines, 0))
    for s in range(4):
        at_ref[s * TILE : (s + 1) * TILE, 0:2] = columns[:, 2 * s : 2 * s + 2]
    fill(points_ref, at_ref, length, high_ref, low_ref)


def fold_kernel(own_ref, other_ref, high_ref, low_ref, *outs):
    pair = jnp.concatenate([own_ref[:TILE, :], other_ref[:TILE, :]], 1)
    high, low = halves(pair)
    for t, out in enumerate(outs):
        part = slice(t * TILE, (t + 1) * TILE)
        kernel_high = high_ref[:, part]
        summed = product(high, kernel_high) + product(high, low_ref[:, part])
        out[:TILE, :] = summed + product(low, kernel_high)
        if out.shape[0] > TILE:
            out[TILE:, :] = own_ref[TILE:, :] + other_ref[TILE:, :]


def stack(blocks, high_ref, low_ref, at=0):
    for k, block in enumerate(blocks):
        high, low = halves(block[:TILE, :])
        high_ref[k * TILE : (k + 1) * TILE, at : at + TILE] = high
        low_ref[k * TILE : (k + 1) * TILE, at : at + TILE] = low


def applied(high_ref, low_ref, rows, right_high, right_low):
    high = high_ref[rows, :]
    return product(high, right_high) + product(high, right_low) + product(low_ref[rows, :], right_high)


def apply_kernel(*refs):
    blocks, starts, noise_ref, high_ref, low_ref = refs[:8], refs[8:12], *refs[12:15]
    outs, right_high, right_low = refs[15:19], *refs[19:]
    stack(blocks, right_high, right_low)
    start = starts[0][...]
    squares = jnp.sum(start * start, 0, keepdims=True)
    first = jnp.zeros((1, TILE), f32)
    for r, out in enumerate(outs):
        rows = slice(r * TILE, (r + 1) * TILE)
        part = applied(high_ref, low_ref, rows, right_high[...], right_low[...])
        out[:TILE, :] = part
        first = first + jnp.sum(starts[r][...] * part, 0, keepdims=True)
    first = first * amplitude + squares * noise_ref[...]
    carry = jnp.concatenate([squares, first, jnp.zeros((6, TILE), f32)], 0)
    for out in outs:
        out[TILE:, :] = carry


def image_kernel(a, b, c, d, mask_ref, start_ref, noise_ref, out_ref):
    parts = (a[...] + b[...]) + (c[...] + d[...])
    start = start_ref[...]
    image = mask_ref[...].astype(f32) * parts[:TILE, :] * amplitude + start * noise_ref[...]
    out_ref[:TILE, :] = image
    out_ref[TILE:, :] = parts[TILE:, :]


def curve_kernel(*refs):
    folds, outers, starts, images = refs[:8], refs[8:12], refs[12:16], refs[16:20]
    noise_ref, high_ref, low_ref, out_ref, known_ref, right_high, right_low = refs[20:]
    sums = sum(fold[TILE:, :] for fold in folds)
    norm = jnp.sum(sums[0:1, :], axis=1, keepdims=True)
    first = jnp.sum(sums[1:2, :], axis=1, keepdims=True)
    step = norm / first
    stack(folds, right_high, right_low)
    curved = jnp.zeros((1, TILE), f32)
    for r in range(4):
        rows = slice(r * TILE, (r + 1) * TILE)
        part = applied(high_ref, low_ref, rows, right_high[...], right_low[...])
        outer = outers[r][:TILE, :] - step * part
        residual = starts[r][...] - step * images[r][:TILE, :]
        curved = curved + jnp.sum(residual * outer, 0, keepdims=True)
    image = images[0][:TILE, :]
    residual = starts[0][...] - step * image
    squares = jnp.sum(residual * residual, 0, keepdims=True)
    curved = curved * amplitude + squares * noise_ref[...]
    crossed = jnp.sum(residual * image, 0, keepdims=True)
    lane = lax.broadcasted_iota(jnp.int32, (1, TILE), 1)

    def side_by_side(values):
        line = jnp.zeros((1, TILE), f32)
        for k, value in enumerate(values):
            line = jnp.where(lane == k, jnp.sum(value, axis=1, keepdims=True), line)
        return line

    line = side_by_side([squares, curved, crossed])
    out_ref[...] = jnp.broadcast_to(line[None], out_ref.shape)
    known_ref[...] = side_by_side([step, norm, first])


def field_kernel(*refs):
    folds, high_ref, low_ref = refs[:8], *refs[8:10]
    outs, right_high, right_low = refs[10:14], *refs[14:]
    stack(folds, right_high, right_low)
    for r, out in enumerate(outs):
        rows = slice(r * TILE, (r + 1) * TILE)
        out[...] = applied(high_ref, low_ref, rows, right_high[...], right_low[...])


def last_kernel(sums_ref, known_ref, start_ref, image_ref, *refs):
    (a, b, c, d), (e, f, g, h), (estimate_ref, field_ref) = refs[:4], refs[4:8], refs[8:]
    sums = jnp.sum(sums_ref[...], axis=0)
    norm_next, curved, crossed = sums[:, 0:1], sums[:, 1:2], sums[:, 2:3]
    step, norm, first = known_ref[:, 0:1], known_ref[:, 1:2], known_ref[:, 2:3]
    follow = norm_next / norm
    step_next = norm_next / (curved + 2.0 * follow * crossed + follow * follow * first)
    start, image = start_ref[...], image_ref[:TILE, :]
    direction = (start - step * image) + follow * start
    estimate_ref[...] = step * start + step_next * direction
    of_start = (a[...] + b[...]) + (c[...] + d[...])
    of_image = (e[...] + f[...]) + (g[...] + h[...])
    turned = (of_start - step * of_image) + follow * of_start
    field_ref[...] = (step * of_start + step_next * turned) * amplitude


def whole(
    observed,
    observed_mask,
    training_site_positions,
    time_stamps,
    noise_var,
    test_coords,
    site_order,
):
    sites = training_site_positions.shape[1]
    times = time_stamps.shape[0]
    space_length = space_reach / math.sqrt(sites)
    wide = (4 * TILE, 8 * TILE)
    split_pair = [(wide, bf16), (wide, bf16)]
    square = ((TILE, TILE), f32)
    points = [pltpu.VMEM((2, 8 * TILE), f32), pltpu.VMEM((4 * TILE, TILE), f32)]
    right = [pltpu.VMEM((8 * TILE, TILE), bf16)] * 2
    one_product = 6 * 4 * TILE * 8 * TILE * TILE

    def exchanged(copies, axes):
        return lax.all_to_all(copies, axes, split_axis=0, concat_axis=0, tiled=True)

    start = observed_mask.astype(f32) * observed
    start_rows = gathered(start, "loc_0", (2, 1, 3))

    time_high, time_low, site_high, site_low, noise = call(
        functools.partial(train_kernel, time_length=time_reach / times, length=space_length),
        [((2 * TILE, 4 * TILE), bf16)] * 2 + split_pair + [((1, TILE), f32)],
        time_stamps.reshape(8, TILE),
        training_site_positions,
        noise_var[None, :],
        flops=400 * 4 * TILE * 8 * TILE,
        scratch=points,
    )

    def folded(block, other):
        parts = call(
            fold_kernel,
            [(block.shape, f32)] * 4,
            block,
            other,
            time_high,
            time_low,
            flops=6 * TILE * 8 * TILE * TILE,
        )
        others = [ahead(parts[k], "tm", -2 * k) for k in (1, 2, 3)]
        mine, second, fourth, sixth = [parts[0]] + others
        return (mine + fourth) + (second + sixth)

    def columns(block):
        held = gathered(block, "loc_1", (2, 1, 3))
        return held + [swapped(piece) for piece in held]

    def to_owners(parts):
        return [parts[0]] + [ahead(parts[s], "loc_0", -s) for s in (1, 2, 3)]

    other = neighbours(start)
    start_fold = folded(start, other)
    start_fold, start_rows = lax.optimization_barrier((start_fold, start_rows))
    start_folds = columns(start_fold)
    outers = call(
        apply_kernel,
        [((TILE + 8, TILE), f32)] * 4,
        *start_folds,
        *start_rows,
        noise,
        site_high,
        site_low,
        flops=one_product,
        scratch=right,
    )
    test_high, test_low = call(
        functools.partial(test_kernel, length=space_length),
        split_pair,
        training_site_positions,
        test_coords,
        site_order.reshape(-1, TILE),
        flops=600 * 4 * TILE * 8 * TILE,
        scratch=points,
    )

    owned = to_owners(outers)
    owned, test_high, test_low = lax.optimization_barrier((owned, test_high, test_low))
    (image,) = call(
        image_kernel,
        [((TILE + 8, TILE), f32)],
        *owned,
        observed_mask,
        start,
        noise,
        flops=10 * TILE * TILE,
    )
    other = neighbours(image)
    image_rows = gathered(image, "loc_0", (2, 1, 3))
    image_fold = folded(image, other)
    start_fields = call(
        field_kernel,
        [square] * 4,
        *start_folds,
        test_high,
        test_low,
        flops=one_product,
        scratch=right,
    )
    image_fold, image_rows, start_fields = lax.optimization_barrier(
        (image_fold, image_rows, start_fields)
    )
    start_fields = to_owners(start_fields)
    image_folds = columns(image_fold)
    size = lax.axis_size(EVERYONE)
    sums, known = call(
        curve_kernel,
        [((size, 1, TILE), f32), ((1, TILE), f32)],
        *image_folds,
        *outers,
        *start_rows,
        *image_rows,
        noise,
        site_high,
        site_low,
        flops=one_product,
        scratch=right,
    )
    sums = exchanged(sums, EVERYONE)
    image_fields = call(
        field_kernel,
        [square] * 4,
        *image_folds,
        test_high,
        test_low,
        flops=one_product,
        scratch=right,
    )
    return tuple(
        call(
            last_kernel,
            [square] * 2,
            sums,
            known,
            start,
            image,
            *start_fields,
            *to_owners(image_fields),
            flops=20 * TILE * TILE,
        )
    )


def solution(mesh):
    split = Mesh(mesh.devices.reshape(4, 4, 2, mesh.shape["tm"]), ("loc_0", "loc_1", "loc_2", "tm"))
    in_specs = (P(LOC, "tm"), P(LOC, "tm"), P(), P(), P("tm"), P(), P())
    out_specs = (P(LOC, "tm"), P(LOC, "tm"))
    return jax.shard_map(whole, mesh=split, in_specs=in_specs, out_specs=out_specs, check_vma=False)
```

profile of v0, /device:TPU:1, one launch (start us, length us, event | category | flops | bytes accessed | tf_op | source)
XLA Modules:
  0.0 101.8 jit_solution(11123325609524004697)
XLA Ops:
  0.6 0.9 convert_multiply_fusion.own_ref.refs_8_.start_ref.refs_12_
  1.5 2.5 %collective-permute-start = (f32[128,128]{1,0:T(8,128)S(1)}, f32[128,128]{1,0:T(8,128)S(1)}, u32[]{:S(2)}, u32[]{:S(2)}) collective-permute-start(f32[128,128]{1,0:T(8,128)S(1)} %convert_multiply_fusion.own_ref.refs_8_.start_ref.refs_12_), channel_id=1, source_target_pairs={{0,1},{1,0},{2,3},{3,2},{4,5},{5,4},{6,7},{7,6},{8,9},{9,8},{10,11... | collective-permute-start | bytes 196616 | tf_op jit(solution)/shard_map/ppermute | solution.py:39
  4.1 0.6 copy-done.5
  4.7 2.9 %shard_map.86 = (bf16[256,512]{1,0:T(8,128)(2,1)S(1)}, bf16[256,512]{1,0:T(8,128)(2,1)S(1)}, bf16[512,1024]{1,0:T(8,128)(2,1)S(1)}, bf16[512,1024]{1,0:T(8,128)(2,1)S(1)}, f32[1,128]{1,0:T(1,128)S(1)}) custom-call(f32[8,128]{1,0:T(8,128)S(1)} %bitcast.4, f32[2,4096]{1,0:T(2,128)S(1)} %copy-done.1, f32[1,128]{1,0:T(1,128)S(1)} %bitcast.5), custom_call_target="tpu_custom_call" | custom-call | flops 209715200 | bytes 2659328 | tf_op jit(solution)/shard_map/pallas_call | solution.py:58
  8.0 3.1 %collective-permute-start.2 = (f32[128,128]{1,0:T(8,128)S(1)}, f32[128,128]{1,0:T(8,128)S(1)}, u32[]{:S(2)}, u32[]{:S(2)}) collective-permute-start(f32[128,128]{1,0:T(8,128)S(1)} %get-tuple-element.55), channel_id=1, source_target_pairs={{6,0},{7,1},{0,2},{1,3},{2,4},{3,5},{4,6},{5,7},{14,8},{15,9},{8,1... | collective-permute-start | bytes 196616 | tf_op jit(solution)/shard_map/ppermute | solution.py:28
  11.0 2.2 %collective-permute-start.3 = (f32[128,128]{1,0:T(8,128)S(1)}, f32[128,128]{1,0:T(8,128)S(1)}, u32[]{:S(2)}, u32[]{:S(2)}) collective-permute-start(f32[128,128]{1,0:T(8,128)S(1)} %get-tuple-element.56), channel_id=1, source_target_pairs={{2,0},{3,1},{4,2},{5,3},{6,4},{7,5},{0,6},{1,7},{10,8},{11,9},{12,... | collective-permute-start | bytes 196616 | tf_op jit(solution)/shard_map/ppermute | solution.py:28
  13.3 4.4 %collective-permute-start.1 = (f32[128,128]{1,0:T(8,128)S(1)}, f32[128,128]{1,0:T(8,128)S(1)}, u32[]{:S(2)}, u32[]{:S(2)}) collective-permute-start(f32[128,128]{1,0:T(8,128)S(1)} %get-tuple-element.54), channel_id=1, source_target_pairs={{4,0},{5,1},{6,2},{7,3},{0,4},{1,5},{2,6},{3,7},{12,8},{13,9},{14,... | collective-permute-start | bytes 196616 | tf_op jit(solution)/shard_map/ppermute | solution.py:28
  17.6 2.7 %collective-permute-start.4 = (f32[128,128]{1,0:T(8,128)S(1)}, f32[128,128]{1,0:T(8,128)S(1)}, u32[]{:S(2)}, u32[]{:S(2)}) collective-permute-start(f32[128,128]{1,0:T(8,128)S(1)} %convert_multiply_fusion.own_ref.refs_8_.start_ref.refs_12_), channel_id=1, source_target_pairs={{64,0},{128,64},{192,128},{0,192},{65,1},{129,65},{193,129},{1,193... | collective-permute-start | bytes 196616 | tf_op jit(solution)/shard_map/ppermute | solution.py:28
  20.7 0.7 collective-permute-start.6
  21.7 3.4 %collective-permute-done.5.refs_10_.refs_14_ = f32[128,128]{1,0:T(8,128)S(1)} collective-permute-done((f32[128,128]{1,0:T(8,128)S(1)}, f32[128,128]{1,0:T(8,128)S(1)}, u32[]{:S(2)}, u32[]{:S(2)}) %collective-permute-start.5) | collective-permute-done | bytes 65568 | tf_op jit(solution)/shard_map/ppermute | solution.py:28
  25.1 0.6 collective-permute-done.6.refs_11_.refs_15_
  25.7 2.5 %collective-permute-start.7 = (f32[128,128]{1,0:T(8,128)S(1)}, f32[128,128]{1,0:T(8,128)S(1)}, u32[]{:S(2)}, u32[]{:S(2)}) collective-permute-start(f32[128,128]{1,0:T(8,128)S(1)} %add_add_fusion.1.refs_0_), channel_id=1, source_target_pairs={{16,0},{32,16},{48,32},{0,48},{17,1},{33,17},{49,33},{1,49},{18,2}... | collective-permute-start | bytes 196616 | tf_op jit(solution)/shard_map/ppermute | solution.py:28
  29.3 4.1 %collective-permute-start.10 = (f32[128,128]{1,0:T(8,128)S(1)}, f32[128,128]{1,0:T(8,128)S(1)}, u32[]{:S(2)}, u32[]{:S(2)}) collective-permute-start(f32[128,128]{1,0:T(8,128)S(1)} %add_add_fusion.1.refs_0_), channel_id=1, source_target_pairs={{0,8},{8,0},{1,9},{9,1},{2,10},{10,2},{3,11},{11,3},{4,12},{12,4},... | collective-permute-start | bytes 196616 | tf_op jit(solution)/shard_map/ppermute | solution.py:43
  33.6 3.9 %collective-permute-start.12 = (f32[128,128]{1,0:T(8,128)S(1)}, f32[128,128]{1,0:T(8,128)S(1)}, u32[]{:S(2)}, u32[]{:S(2)}) collective-permute-start(f32[128,128]{1,0:T(8,128)S(1)} %collective-permute-done.8.refs_2_), channel_id=1, source_target_pairs={{0,8},{8,0},{1,9},{9,1},{2,10},{10,2},{3,11},{11,3},{4,12},{12,4},... | collective-permute-start | bytes 196616 | tf_op jit(solution)/shard_map/ppermute | solution.py:43
  37.5 0.7 collective-permute-start.13
  38.4 0.7 collective-permute-done.13.refs_7_
  39.1 1.1 %shard_map.88 = (f32[136,128]{1,0:T(8,128)S(1)}, f32[136,128]{1,0:T(8,128)S(1)}, f32[136,128]{1,0:T(8,128)S(1)}, f32[136,128]{1,0:T(8,128)S(1)}) custom-call(f32[128,128]{1,0:T(8,128)S(1)} %add_add_fusion.1.refs_0_, f32[128,128]{1,0:T(8,128)S(1)} %collective-permute-done.7.refs_1_, f32[128,128]{1,0:T(8,128)S(1)} %collective-permute-done.8.refs_2_, ...), custom_call_target="tpu_custom_call" | custom-call | flops 402653184 | bytes 3162624 | tf_op jit(solution)/shard_map/pallas_call | solution.py:58
  40.2 1.5 %collective-permute-start.15 = (f32[136,128]{1,0:T(8,128)S(1)}, f32[136,128]{1,0:T(8,128)S(1)}, u32[]{:S(2)}, u32[]{:S(2)}) collective-permute-start(f32[136,128]{1,0:T(8,128)S(1)} %get-tuple-element.67.refs_10_), channel_id=1, source_target_pairs={{128,0},{192,64},{0,128},{64,192},{129,1},{193,65},{1,129},{65,193... | collective-permute-start | bytes 208904 | tf_op jit(solution)/shard_map/ppermute | solution.py:28
  41.7 1.6 %collective-permute-start.16 = (f32[136,128]{1,0:T(8,128)S(1)}, f32[136,128]{1,0:T(8,128)S(1)}, u32[]{:S(2)}, u32[]{:S(2)}) collective-permute-start(f32[136,128]{1,0:T(8,128)S(1)} %get-tuple-element.68.refs_11_), channel_id=1, source_target_pairs={{64,0},{128,64},{192,128},{0,192},{65,1},{129,65},{193,129},{1,193... | collective-permute-start | bytes 208904 | tf_op jit(solution)/shard_map/ppermute | solution.py:28
  43.3 3.5 %shard_map.89 = (bf16[512,1024]{1,0:T(8,128)(2,1)S(1)}, bf16[512,1024]{1,0:T(8,128)(2,1)S(1)}) custom-call(f32[2,4096]{1,0:T(2,128)S(1)} %copy-done.1, f32[2,4096]{1,0:T(2,128)S(1)} %copy-done.2, s32[32,128]{1,0:T(8,128)S(1)} %bitcast.3), custom_call_target="tpu_custom_call" | custom-call | flops 314572800 | bytes 2179072 | tf_op jit(solution)/shard_map/pallas_call | solution.py:58
  46.9 0.8 collective-permute-start.17
  47.7 2.4 %collective-permute-done.17.other_ref = f32[136,128]{1,0:T(8,128)S(1)} collective-permute-done((f32[136,128]{1,0:T(8,128)S(1)}, f32[136,128]{1,0:T(8,128)S(1)}, u32[]{:S(2)}, u32[]{:S(2)}) %collective-permute-start.17) | collective-permute-done | bytes 69664 | tf_op jit(solution)/shard_map/ppermute | solution.py:39
  50.6 3.6 %collective-permute-start.20 = (f32[136,128]{1,0:T(8,128)S(1)}, f32[136,128]{1,0:T(8,128)S(1)}, u32[]{:S(2)}, u32[]{:S(2)}) collective-permute-start(f32[136,128]{1,0:T(8,128)S(1)} %get-tuple-element.78), channel_id=1, source_target_pairs={{2,0},{3,1},{4,2},{5,3},{6,4},{7,5},{0,6},{1,7},{10,8},{11,9},{12,... | collective-permute-start | bytes 208904 | tf_op jit(solution)/shard_map/ppermute | solution.py:28
  54.2 0.7 collective-permute-start.18
  54.9 2.6 %collective-permute-start.21 = (f32[136,128]{1,0:T(8,128)S(1)}, f32[136,128]{1,0:T(8,128)S(1)}, u32[]{:S(2)}, u32[]{:S(2)}) collective-permute-start(f32[136,128]{1,0:T(8,128)S(1)} %shard_map.90.own_ref.refs_16_.image_ref), channel_id=1, source_target_pairs={{64,0},{128,64},{192,128},{0,192},{65,1},{129,65},{193,129},{1,193... | collective-permute-start | bytes 208904 | tf_op jit(solution)/shard_map/ppermute | solution.py:28
  57.6 1.0 %shard_map.92 = (f32[128,128]{1,0:T(8,128)S(1)}, f32[128,128]{1,0:T(8,128)S(1)}, f32[128,128]{1,0:T(8,128)S(1)}, f32[128,128]{1,0:T(8,128)S(1)}) custom-call(f32[128,128]{1,0:T(8,128)S(1)} %add_add_fusion.1.refs_0_, f32[128,128]{1,0:T(8,128)S(1)} %collective-permute-done.7.refs_1_, f32[128,128]{1,0:T(8,128)S(1)} %collective-permute-done.8.refs_2_, ...), custom_call_target="tpu_custom_call" | custom-call | flops 402653184 | bytes 2883584 | tf_op jit(solution)/shard_map/pallas_call | solution.py:58
  58.6 0.6 collective-permute-start.23
  59.2 2.6 %collective-permute-done.18 = f32[136,128]{1,0:T(8,128)S(1)} collective-permute-done((f32[136,128]{1,0:T(8,128)S(1)}, f32[136,128]{1,0:T(8,128)S(1)}, u32[]{:S(2)}, u32[]{:S(2)}) %collective-permute-start.18) | collective-permute-done | bytes 69664 | tf_op jit(solution)/shard_map/ppermute | solution.py:28
  62.2 0.9 collective-permute-done.23.refs_19_
  63.4 0.7 collective-permute-start.25
  64.1 0.9 collective-permute-start.26
  65.0 5.6 %collective-permute-start.27 = (f32[136,128]{1,0:T(8,128)S(1)}, f32[136,128]{1,0:T(8,128)S(1)}, u32[]{:S(2)}, u32[]{:S(2)}) collective-permute-start(f32[136,128]{1,0:T(8,128)S(1)} %add_add_fusion.refs_0_), channel_id=1, source_target_pairs={{0,8},{8,0},{1,9},{9,1},{2,10},{10,2},{3,11},{11,3},{4,12},{12,4},... | collective-permute-start | bytes 208904 | tf_op jit(solution)/shard_map/ppermute | solution.py:43
  70.5 1.6 %collective-permute-start.28 = (f32[136,128]{1,0:T(8,128)S(1)}, f32[136,128]{1,0:T(8,128)S(1)}, u32[]{:S(2)}, u32[]{:S(2)}) collective-permute-start(f32[136,128]{1,0:T(8,128)S(1)} %collective-permute-done.24.refs_1_), channel_id=1, source_target_pairs={{0,8},{8,0},{1,9},{9,1},{2,10},{10,2},{3,11},{11,3},{4,12},{12,4},... | collective-permute-start | bytes 208904 | tf_op jit(solution)/shard_map/ppermute | solution.py:43
  72.1 2.1 %collective-permute-start.29 = (f32[136,128]{1,0:T(8,128)S(1)}, f32[136,128]{1,0:T(8,128)S(1)}, u32[]{:S(2)}, u32[]{:S(2)}) collective-permute-start(f32[136,128]{1,0:T(8,128)S(1)} %collective-permute-done.25.refs_2_), channel_id=1, source_target_pairs={{0,8},{8,0},{1,9},{9,1},{2,10},{10,2},{3,11},{11,3},{4,12},{12,4},... | collective-permute-start | bytes 208904 | tf_op jit(solution)/shard_map/ppermute | solution.py:43
  74.2 0.7 collective-permute-start.30
  75.1 0.7 collective-permute-done.30.refs_7_
  75.8 1.9 %shard_map.93 = (f32[256,1,128]{2,1,0:T(1,128)}, f32[1,128]{1,0:T(1,128)S(1)}) custom-call(f32[136,128]{1,0:T(8,128)S(1)} %add_add_fusion.refs_0_, f32[136,128]{1,0:T(8,128)S(1)} %collective-permute-done.24.refs_1_, f32[136,128]{1,0:T(8,128)S(1)} %collective-permute-done.25.refs_2_, f32[136,128]{1,0:T(8,128)S(1)} %collective-permute-done.26.refs_3_, ...), custom_call_target="tpu_custom_call" | custom-call | flops 402653184 | bytes 3605504 | tf_op jit(solution)/shard_map/pallas_call | solution.py:58
  77.7 9.8 %all-to-all-start = ((f32[256,1,128]{2,1,0:T(1,128)}), f32[256,1,128]{2,1,0:T(1,128)S(1)}, u32[]{:S(2)}, u32[]{:S(2)}) async-start(f32[256,1,128]{2,1,0:T(1,128)} %get-tuple-element.90), calls=%async_computation | async-start | bytes 262144 | tf_op jit(solution)/shard_map/all_to_all | solution.py:291
  87.6 1.4 %collective-permute-start.31 = (f32[128,128]{1,0:T(8,128)S(1)}, f32[128,128]{1,0:T(8,128)S(1)}, u32[]{:S(2)}, u32[]{:S(2)}) collective-permute-start(f32[128,128]{1,0:T(8,128)S(1)} %get-tuple-element.93), channel_id=1, source_target_pairs={{192,0},{0,64},{64,128},{128,192},{193,1},{1,65},{65,129},{129,193... | collective-permute-start | bytes 196616 | tf_op jit(solution)/shard_map/ppermute | solution.py:28
  89.0 2.5 %collective-permute-start.32 = (f32[128,128]{1,0:T(8,128)S(1)}, f32[128,128]{1,0:T(8,128)S(1)}, u32[]{:S(2)}, u32[]{:S(2)}) collective-permute-start(f32[128,128]{1,0:T(8,128)S(1)} %get-tuple-element.94), channel_id=1, source_target_pairs={{128,0},{192,64},{0,128},{64,192},{129,1},{193,65},{1,129},{65,193... | collective-permute-start | bytes 196616 | tf_op jit(solution)/shard_map/ppermute | solution.py:28
  91.4 1.1 %collective-permute-start.33 = (f32[128,128]{1,0:T(8,128)S(1)}, f32[128,128]{1,0:T(8,128)S(1)}, u32[]{:S(2)}, u32[]{:S(2)}) collective-permute-start(f32[128,128]{1,0:T(8,128)S(1)} %get-tuple-element.95), channel_id=1, source_target_pairs={{64,0},{128,64},{192,128},{0,192},{65,1},{129,65},{193,129},{1,193... | collective-permute-start | bytes 196616 | tf_op jit(solution)/shard_map/ppermute | solution.py:28
  92.6 1.0 shard_map.94
  94.0 0.8 collective-permute-start.35
  94.9 1.6 %collective-permute-start.36 = (f32[128,128]{1,0:T(8,128)S(1)}, f32[128,128]{1,0:T(8,128)S(1)}, u32[]{:S(2)}, u32[]{:S(2)}) collective-permute-start(f32[128,128]{1,0:T(8,128)S(1)} %get-tuple-element.99), channel_id=1, source_target_pairs={{64,0},{128,64},{192,128},{0,192},{65,1},{129,65},{193,129},{1,193... | collective-permute-start | bytes 196616 | tf_op jit(solution)/shard_map/ppermute | solution.py:28
  96.5 2.1 %collective-permute-done.34.refs_5_ = f32[128,128]{1,0:T(8,128)S(1)} collective-permute-done((f32[128,128]{1,0:T(8,128)S(1)}, f32[128,128]{1,0:T(8,128)S(1)}, u32[]{:S(2)}, u32[]{:S(2)}) %collective-permute-start.34) | collective-permute-done | bytes 65568 | tf_op jit(solution)/shard_map/ppermute | solution.py:28
  98.6 1.2 %collective-permute-done.35.refs_6_ = f32[128,128]{1,0:T(8,128)S(1)} collective-permute-done((f32[128,128]{1,0:T(8,128)S(1)}, f32[128,128]{1,0:T(8,128)S(1)}, u32[]{:S(2)}, u32[]{:S(2)}) %collective-permute-start.35) | collective-permute-done | bytes 65568 | tf_op jit(solution)/shard_map/ppermute | solution.py:28
  99.8 0.8 all-to-all-done.sums_ref
  100.6 1.2 %shard_map.95 = (f32[128,128]{1,0:T(8,128)}, f32[128,128]{1,0:T(8,128)}) custom-call(f32[256,1,128]{2,1,0:T(1,128)S(1)} %all-to-all-done.sums_ref, f32[1,128]{1,0:T(1,128)S(1)} %get-tuple-element.91.known_ref, f32[128,128]{1,0:T(8,128)S(1)} %convert_multiply_fusion.own_ref.refs_8_.start_ref.refs_12_, f32[136,128]{1,0:T(8,128)S(1)} %shard_map.90.own_ref.refs_16_.image_ref, ...), custom_call_target="tpu_custom_call" | custom-call | flops 327680 | bytes 922112 | tf_op jit(solution)/shard_map/pallas_call | solution.py:58
  (53 shorter events, 4.5 us)
Async XLA Ops:
  0.6 3.5 %copy-start.4 = (f32[1024]{0:T(1024)S(1)}, f32[1024]{0:T(1024)}, u32[]{:S(2)}) copy-start(f32[1024]{0:T(1024)} %param.10) | copy-start | bytes 12292
  0.6 3.5 %copy-start.1 = (f32[2,4096]{1,0:T(2,128)S(1)}, f32[2,4096]{1,0:T(2,128)}, u32[]{:S(2)}) copy-start(f32[2,4096]{1,0:T(2,128)} %sites_ref.3) | copy-start | bytes 98308
  1.5 6.1 %collective-permute-start = (f32[128,128]{1,0:T(8,128)S(1)}, f32[128,128]{1,0:T(8,128)S(1)}, u32[]{:S(2)}, u32[]{:S(2)}) collective-permute-start(f32[128,128]{1,0:T(8,128)S(1)} %convert_multiply_fusion.own_ref.refs_8_.start_ref.refs_12_), channel_id=1, source_target_pairs={{0,1},{1,0},{2,3},{3,2},{4,5},{5,4},{6,7},{7,6},{8,9},{9,8},{10,11... | collective-permute-start | bytes 196616 | tf_op jit(solution)/shard_map/ppermute | solution.py:39
  4.1 0.7 copy-start.5
  8.0 12.8 %collective-permute-start.2 = (f32[128,128]{1,0:T(8,128)S(1)}, f32[128,128]{1,0:T(8,128)S(1)}, u32[]{:S(2)}, u32[]{:S(2)}) collective-permute-start(f32[128,128]{1,0:T(8,128)S(1)} %get-tuple-element.55), channel_id=1, source_target_pairs={{6,0},{7,1},{0,2},{1,3},{2,4},{3,5},{4,6},{5,7},{14,8},{15,9},{8,1... | collective-permute-start | bytes 196616 | tf_op jit(solution)/shard_map/ppermute | solution.py:28
  11.0 10.4 %collective-permute-start.3 = (f32[128,128]{1,0:T(8,128)S(1)}, f32[128,128]{1,0:T(8,128)S(1)}, u32[]{:S(2)}, u32[]{:S(2)}) collective-permute-start(f32[128,128]{1,0:T(8,128)S(1)} %get-tuple-element.56), channel_id=1, source_target_pairs={{2,0},{3,1},{4,2},{5,3},{6,4},{7,5},{0,6},{1,7},{10,8},{11,9},{12,... | collective-permute-start | bytes 196616 | tf_op jit(solution)/shard_map/ppermute | solution.py:28
  13.3 8.2 %collective-permute-start.1 = (f32[128,128]{1,0:T(8,128)S(1)}, f32[128,128]{1,0:T(8,128)S(1)}, u32[]{:S(2)}, u32[]{:S(2)}) collective-permute-start(f32[128,128]{1,0:T(8,128)S(1)} %get-tuple-element.54), channel_id=1, source_target_pairs={{4,0},{5,1},{6,2},{7,3},{0,4},{1,5},{2,6},{3,7},{12,8},{13,9},{14,... | collective-permute-start | bytes 196616 | tf_op jit(solution)/shard_map/ppermute | solution.py:28
  17.6 4.1 %collective-permute-start.4 = (f32[128,128]{1,0:T(8,128)S(1)}, f32[128,128]{1,0:T(8,128)S(1)}, u32[]{:S(2)}, u32[]{:S(2)}) collective-permute-start(f32[128,128]{1,0:T(8,128)S(1)} %convert_multiply_fusion.own_ref.refs_8_.start_ref.refs_12_), channel_id=1, source_target_pairs={{64,0},{128,64},{192,128},{0,192},{65,1},{129,65},{193,129},{1,193... | collective-permute-start | bytes 196616 | tf_op jit(solution)/shard_map/ppermute | solution.py:28
  20.4 4.7 %collective-permute-start.5 = (f32[128,128]{1,0:T(8,128)S(1)}, f32[128,128]{1,0:T(8,128)S(1)}, u32[]{:S(2)}, u32[]{:S(2)}) collective-permute-start(f32[128,128]{1,0:T(8,128)S(1)} %convert_multiply_fusion.own_ref.refs_8_.start_ref.refs_12_), channel_id=1, source_target_pairs={{128,0},{192,64},{0,128},{64,192},{129,1},{193,65},{1,129},{65,193... | collective-permute-start | bytes 196616 | tf_op jit(solution)/shard_map/ppermute | solution.py:28
  20.7 5.0 %collective-permute-start.6 = (f32[128,128]{1,0:T(8,128)S(1)}, f32[128,128]{1,0:T(8,128)S(1)}, u32[]{:S(2)}, u32[]{:S(2)}) collective-permute-start(f32[128,128]{1,0:T(8,128)S(1)} %convert_multiply_fusion.own_ref.refs_8_.start_ref.refs_12_), channel_id=1, source_target_pairs={{192,0},{0,64},{64,128},{128,192},{193,1},{1,65},{65,129},{129,193... | collective-permute-start | bytes 196616 | tf_op jit(solution)/shard_map/ppermute | solution.py:28
  25.7 7.7 %collective-permute-start.7 = (f32[128,128]{1,0:T(8,128)S(1)}, f32[128,128]{1,0:T(8,128)S(1)}, u32[]{:S(2)}, u32[]{:S(2)}) collective-permute-start(f32[128,128]{1,0:T(8,128)S(1)} %add_add_fusion.1.refs_0_), channel_id=1, source_target_pairs={{16,0},{32,16},{48,32},{0,48},{17,1},{33,17},{49,33},{1,49},{18,2}... | collective-permute-start | bytes 196616 | tf_op jit(solution)/shard_map/ppermute | solution.py:28
  28.2 5.4 %collective-permute-start.8 = (f32[128,128]{1,0:T(8,128)S(1)}, f32[128,128]{1,0:T(8,128)S(1)}, u32[]{:S(2)}, u32[]{:S(2)}) collective-permute-start(f32[128,128]{1,0:T(8,128)S(1)} %add_add_fusion.1.refs_0_), channel_id=1, source_target_pairs={{32,0},{48,16},{0,32},{16,48},{33,1},{49,17},{1,33},{17,49},{34,2}... | collective-permute-start | bytes 196616 | tf_op jit(solution)/shard_map/ppermute | solution.py:28
  28.7 8.8 %collective-permute-start.9 = (f32[128,128]{1,0:T(8,128)S(1)}, f32[128,128]{1,0:T(8,128)S(1)}, u32[]{:S(2)}, u32[]{:S(2)}) collective-permute-start(f32[128,128]{1,0:T(8,128)S(1)} %add_add_fusion.1.refs_0_), channel_id=1, source_target_pairs={{48,0},{0,16},{16,32},{32,48},{49,1},{1,17},{17,33},{33,49},{50,2}... | collective-permute-start | bytes 196616 | tf_op jit(solution)/shard_map/ppermute | solution.py:28
  29.3 8.9 %collective-permute-start.10 = (f32[128,128]{1,0:T(8,128)S(1)}, f32[128,128]{1,0:T(8,128)S(1)}, u32[]{:S(2)}, u32[]{:S(2)}) collective-permute-start(f32[128,128]{1,0:T(8,128)S(1)} %add_add_fusion.1.refs_0_), channel_id=1, source_target_pairs={{0,8},{8,0},{1,9},{9,1},{2,10},{10,2},{3,11},{11,3},{4,12},{12,4},... | collective-permute-start | bytes 196616 | tf_op jit(solution)/shard_map/ppermute | solution.py:43
  33.4 4.8 %collective-permute-start.11 = (f32[128,128]{1,0:T(8,128)S(1)}, f32[128,128]{1,0:T(8,128)S(1)}, u32[]{:S(2)}, u32[]{:S(2)}) collective-permute-start(f32[128,128]{1,0:T(8,128)S(1)} %collective-permute-done.7.refs_1_), channel_id=1, source_target_pairs={{0,8},{8,0},{1,9},{9,1},{2,10},{10,2},{3,11},{11,3},{4,12},{12,4},... | collective-permute-start | bytes 196616 | tf_op jit(solution)/shard_map/ppermute | solution.py:43
  33.6 4.8 %collective-permute-start.12 = (f32[128,128]{1,0:T(8,128)S(1)}, f32[128,128]{1,0:T(8,128)S(1)}, u32[]{:S(2)}, u32[]{:S(2)}) collective-permute-start(f32[128,128]{1,0:T(8,128)S(1)} %collective-permute-done.8.refs_2_), channel_id=1, source_target_pairs={{0,8},{8,0},{1,9},{9,1},{2,10},{10,2},{3,11},{11,3},{4,12},{12,4},... | collective-permute-start | bytes 196616 | tf_op jit(solution)/shard_map/ppermute | solution.py:43
  37.5 1.6 %collective-permute-start.13 = (f32[128,128]{1,0:T(8,128)S(1)}, f32[128,128]{1,0:T(8,128)S(1)}, u32[]{:S(2)}, u32[]{:S(2)}) collective-permute-start(f32[128,128]{1,0:T(8,128)S(1)} %collective-permute-done.9.refs_3_), channel_id=1, source_target_pairs={{0,8},{8,0},{1,9},{9,1},{2,10},{10,2},{3,11},{11,3},{4,12},{12,4},... | collective-permute-start | bytes 196616 | tf_op jit(solution)/shard_map/ppermute | solution.py:43
  39.1 4.3 %copy-start.2 = (f32[2,4096]{1,0:T(2,128)S(1)}, f32[2,4096]{1,0:T(2,128)}, u32[]{:S(2)}) copy-start(f32[2,4096]{1,0:T(2,128)} %tests_ref.1) | copy-start | bytes 98308
  39.1 4.3 %copy-start.3 = (s32[4096]{0:T(1024)S(1)}, s32[4096]{0:T(1024)}, u32[]{:S(2)}) copy-start(s32[4096]{0:T(1024)} %param.13) | copy-start | bytes 49156
  40.1 6.7 %collective-permute-start.14 = (f32[136,128]{1,0:T(8,128)S(1)}, f32[136,128]{1,0:T(8,128)S(1)}, u32[]{:S(2)}, u32[]{:S(2)}) collective-permute-start(f32[136,128]{1,0:T(8,128)S(1)} %get-tuple-element.66.refs_9_), channel_id=1, source_target_pairs={{192,0},{0,64},{64,128},{128,192},{193,1},{1,65},{65,129},{129,193... | collective-permute-start | bytes 208904 | tf_op jit(solution)/shard_map/ppermute | solution.py:28
  40.2 6.6 %collective-permute-start.15 = (f32[136,128]{1,0:T(8,128)S(1)}, f32[136,128]{1,0:T(8,128)S(1)}, u32[]{:S(2)}, u32[]{:S(2)}) collective-permute-start(f32[136,128]{1,0:T(8,128)S(1)} %get-tuple-element.67.refs_10_), channel_id=1, source_target_pairs={{128,0},{192,64},{0,128},{64,192},{129,1},{193,65},{1,129},{65,193... | collective-permute-start | bytes 208904 | tf_op jit(solution)/shard_map/ppermute | solution.py:28
  41.7 5.2 %collective-permute-start.16 = (f32[136,128]{1,0:T(8,128)S(1)}, f32[136,128]{1,0:T(8,128)S(1)}, u32[]{:S(2)}, u32[]{:S(2)}) collective-permute-start(f32[136,128]{1,0:T(8,128)S(1)} %get-tuple-element.68.refs_11_), channel_id=1, source_target_pairs={{64,0},{128,64},{192,128},{0,192},{65,1},{129,65},{193,129},{1,193... | collective-permute-start | bytes 208904 | tf_op jit(solution)/shard_map/ppermute | solution.py:28
  43.3 3.5 %copy-start = (s32[128,128]{1,0:T(8,128)S(1)}, s32[128,128]{1,0:T(8,128)}, u32[]{:S(2)}) copy-start(s32[128,128]{1,0:T(8,128)} %mask_ref.1) | copy-start | bytes 196612
  46.9 3.2 %collective-permute-start.17 = (f32[136,128]{1,0:T(8,128)S(1)}, f32[136,128]{1,0:T(8,128)S(1)}, u32[]{:S(2)}, u32[]{:S(2)}) collective-permute-start(f32[136,128]{1,0:T(8,128)S(1)} %shard_map.90.own_ref.refs_16_.image_ref), channel_id=1, source_target_pairs={{0,1},{1,0},{2,3},{3,2},{4,5},{5,4},{6,7},{7,6},{8,9},{9,8},{10,11... | collective-permute-start | bytes 208904 | tf_op jit(solution)/shard_map/ppermute | solution.py:39
  50.5 8.1 %collective-permute-start.19 = (f32[136,128]{1,0:T(8,128)S(1)}, f32[136,128]{1,0:T(8,128)S(1)}, u32[]{:S(2)}, u32[]{:S(2)}) collective-permute-start(f32[136,128]{1,0:T(8,128)S(1)} %get-tuple-element.77), channel_id=1, source_target_pairs={{6,0},{7,1},{0,2},{1,3},{2,4},{3,5},{4,6},{5,7},{14,8},{15,9},{8,1... | collective-permute-start | bytes 208904 | tf_op jit(solution)/shard_map/ppermute | solution.py:28
  50.6 8.6 %collective-permute-start.20 = (f32[136,128]{1,0:T(8,128)S(1)}, f32[136,128]{1,0:T(8,128)S(1)}, u32[]{:S(2)}, u32[]{:S(2)}) collective-permute-start(f32[136,128]{1,0:T(8,128)S(1)} %get-tuple-element.78), channel_id=1, source_target_pairs={{2,0},{3,1},{4,2},{5,3},{6,4},{7,5},{0,6},{1,7},{10,8},{11,9},{12,... | collective-permute-start | bytes 208904 | tf_op jit(solution)/shard_map/ppermute | solution.py:28
  54.2 7.6 %collective-permute-start.18 = (f32[136,128]{1,0:T(8,128)S(1)}, f32[136,128]{1,0:T(8,128)S(1)}, u32[]{:S(2)}, u32[]{:S(2)}) collective-permute-start(f32[136,128]{1,0:T(8,128)S(1)} %get-tuple-element.76), channel_id=1, source_target_pairs={{4,0},{5,1},{6,2},{7,3},{0,4},{1,5},{2,6},{3,7},{12,8},{13,9},{14,... | collective-permute-start | bytes 208904 | tf_op jit(solution)/shard_map/ppermute | solution.py:28
  54.9 6.9 %collective-permute-start.21 = (f32[136,128]{1,0:T(8,128)S(1)}, f32[136,128]{1,0:T(8,128)S(1)}, u32[]{:S(2)}, u32[]{:S(2)}) collective-permute-start(f32[136,128]{1,0:T(8,128)S(1)} %shard_map.90.own_ref.refs_16_.image_ref), channel_id=1, source_target_pairs={{64,0},{128,64},{192,128},{0,192},{65,1},{129,65},{193,129},{1,193... | collective-permute-start | bytes 208904 | tf_op jit(solution)/shard_map/ppermute | solution.py:28
  57.5 4.7 %collective-permute-start.22 = (f32[136,128]{1,0:T(8,128)S(1)}, f32[136,128]{1,0:T(8,128)S(1)}, u32[]{:S(2)}, u32[]{:S(2)}) collective-permute-start(f32[136,128]{1,0:T(8,128)S(1)} %shard_map.90.own_ref.refs_16_.image_ref), channel_id=1, source_target_pairs={{128,0},{192,64},{0,128},{64,192},{129,1},{193,65},{1,129},{65,193... | collective-permute-start | bytes 208904 | tf_op jit(solution)/shard_map/ppermute | solution.py:28
  58.6 4.4 %collective-permute-start.23 = (f32[136,128]{1,0:T(8,128)S(1)}, f32[136,128]{1,0:T(8,128)S(1)}, u32[]{:S(2)}, u32[]{:S(2)}) collective-permute-start(f32[136,128]{1,0:T(8,128)S(1)} %shard_map.90.own_ref.refs_16_.image_ref), channel_id=1, source_target_pairs={{192,0},{0,64},{64,128},{128,192},{193,1},{1,65},{65,129},{129,193... | collective-permute-start | bytes 208904 | tf_op jit(solution)/shard_map/ppermute | solution.py:28
  63.1 7.5 %collective-permute-start.24 = (f32[136,128]{1,0:T(8,128)S(1)}, f32[136,128]{1,0:T(8,128)S(1)}, u32[]{:S(2)}, u32[]{:S(2)}) collective-permute-start(f32[136,128]{1,0:T(8,128)S(1)} %add_add_fusion.refs_0_), channel_id=1, source_target_pairs={{16,0},{32,16},{48,32},{0,48},{17,1},{33,17},{49,33},{1,49},{18,2}... | collective-permute-start | bytes 208904 | tf_op jit(solution)/shard_map/ppermute | solution.py:28
  63.4 8.7 %collective-permute-start.25 = (f32[136,128]{1,0:T(8,128)S(1)}, f32[136,128]{1,0:T(8,128)S(1)}, u32[]{:S(2)}, u32[]{:S(2)}) collective-permute-start(f32[136,128]{1,0:T(8,128)S(1)} %add_add_fusion.refs_0_), channel_id=1, source_target_pairs={{32,0},{48,16},{0,32},{16,48},{33,1},{49,17},{1,33},{17,49},{34,2}... | collective-permute-start | bytes 208904 | tf_op jit(solution)/shard_map/ppermute | solution.py:28
  64.1 10.1 %collective-permute-start.26 = (f32[136,128]{1,0:T(8,128)S(1)}, f32[136,128]{1,0:T(8,128)S(1)}, u32[]{:S(2)}, u32[]{:S(2)}) collective-permute-start(f32[136,128]{1,0:T(8,128)S(1)} %add_add_fusion.refs_0_), channel_id=1, source_target_pairs={{48,0},{0,16},{16,32},{32,48},{49,1},{1,17},{17,33},{33,49},{50,2}... | collective-permute-start | bytes 208904 | tf_op jit(solution)/shard_map/ppermute | solution.py:28
  65.0 10.0 %collective-permute-start.27 = (f32[136,128]{1,0:T(8,128)S(1)}, f32[136,128]{1,0:T(8,128)S(1)}, u32[]{:S(2)}, u32[]{:S(2)}) collective-permute-start(f32[136,128]{1,0:T(8,128)S(1)} %add_add_fusion.refs_0_), channel_id=1, source_target_pairs={{0,8},{8,0},{1,9},{9,1},{2,10},{10,2},{3,11},{11,3},{4,12},{12,4},... | collective-permute-start | bytes 208904 | tf_op jit(solution)/shard_map/ppermute | solution.py:43
  70.5 4.4 %collective-permute-start.28 = (f32[136,128]{1,0:T(8,128)S(1)}, f32[136,128]{1,0:T(8,128)S(1)}, u32[]{:S(2)}, u32[]{:S(2)}) collective-permute-start(f32[136,128]{1,0:T(8,128)S(1)} %collective-permute-done.24.refs_1_), channel_id=1, source_target_pairs={{0,8},{8,0},{1,9},{9,1},{2,10},{10,2},{3,11},{11,3},{4,12},{12,4},... | collective-permute-start | bytes 208904 | tf_op jit(solution)/shard_map/ppermute | solution.py:43
  72.1 3.0 %collective-permute-start.29 = (f32[136,128]{1,0:T(8,128)S(1)}, f32[136,128]{1,0:T(8,128)S(1)}, u32[]{:S(2)}, u32[]{:S(2)}) collective-permute-start(f32[136,128]{1,0:T(8,128)S(1)} %collective-permute-done.25.refs_2_), channel_id=1, source_target_pairs={{0,8},{8,0},{1,9},{9,1},{2,10},{10,2},{3,11},{11,3},{4,12},{12,4},... | collective-permute-start | bytes 208904 | tf_op jit(solution)/shard_map/ppermute | solution.py:43
  74.2 1.7 %collective-permute-start.30 = (f32[136,128]{1,0:T(8,128)S(1)}, f32[136,128]{1,0:T(8,128)S(1)}, u32[]{:S(2)}, u32[]{:S(2)}) collective-permute-start(f32[136,128]{1,0:T(8,128)S(1)} %collective-permute-done.26.refs_3_), channel_id=1, source_target_pairs={{0,8},{8,0},{1,9},{9,1},{2,10},{10,2},{3,11},{11,3},{4,12},{12,4},... | collective-permute-start | bytes 208904 | tf_op jit(solution)/shard_map/ppermute | solution.py:43
  77.7 22.9 %all-to-all-start = ((f32[256,1,128]{2,1,0:T(1,128)}), f32[256,1,128]{2,1,0:T(1,128)S(1)}, u32[]{:S(2)}, u32[]{:S(2)}) async-start(f32[256,1,128]{2,1,0:T(1,128)} %get-tuple-element.90), calls=%async_computation | async-start | bytes 262144 | tf_op jit(solution)/shard_map/all_to_all | solution.py:291
  87.6 7.3 %collective-permute-start.31 = (f32[128,128]{1,0:T(8,128)S(1)}, f32[128,128]{1,0:T(8,128)S(1)}, u32[]{:S(2)}, u32[]{:S(2)}) collective-permute-start(f32[128,128]{1,0:T(8,128)S(1)} %get-tuple-element.93), channel_id=1, source_target_pairs={{192,0},{0,64},{64,128},{128,192},{193,1},{1,65},{65,129},{129,193... | collective-permute-start | bytes 196616 | tf_op jit(solution)/shard_map/ppermute | solution.py:28
  89.0 7.5 %collective-permute-start.32 = (f32[128,128]{1,0:T(8,128)S(1)}, f32[128,128]{1,0:T(8,128)S(1)}, u32[]{:S(2)}, u32[]{:S(2)}) collective-permute-start(f32[128,128]{1,0:T(8,128)S(1)} %get-tuple-element.94), channel_id=1, source_target_pairs={{128,0},{192,64},{0,128},{64,192},{129,1},{193,65},{1,129},{65,193... | collective-permute-start | bytes 196616 | tf_op jit(solution)/shard_map/ppermute | solution.py:28
  91.4 5.1 %collective-permute-start.33 = (f32[128,128]{1,0:T(8,128)S(1)}, f32[128,128]{1,0:T(8,128)S(1)}, u32[]{:S(2)}, u32[]{:S(2)}) collective-permute-start(f32[128,128]{1,0:T(8,128)S(1)} %get-tuple-element.95), channel_id=1, source_target_pairs={{64,0},{128,64},{192,128},{0,192},{65,1},{129,65},{193,129},{1,193... | collective-permute-start | bytes 196616 | tf_op jit(solution)/shard_map/ppermute | solution.py:28
  93.6 5.0 %collective-permute-start.34 = (f32[128,128]{1,0:T(8,128)S(1)}, f32[128,128]{1,0:T(8,128)S(1)}, u32[]{:S(2)}, u32[]{:S(2)}) collective-permute-start(f32[128,128]{1,0:T(8,128)S(1)} %get-tuple-element.97), channel_id=1, source_target_pairs={{192,0},{0,64},{64,128},{128,192},{193,1},{1,65},{65,129},{129,193... | collective-permute-start | bytes 196616 | tf_op jit(solution)/shard_map/ppermute | solution.py:28
  94.0 5.8 %collective-permute-start.35 = (f32[128,128]{1,0:T(8,128)S(1)}, f32[128,128]{1,0:T(8,128)S(1)}, u32[]{:S(2)}, u32[]{:S(2)}) collective-permute-start(f32[128,128]{1,0:T(8,128)S(1)} %get-tuple-element.98), channel_id=1, source_target_pairs={{128,0},{192,64},{0,128},{64,192},{129,1},{193,65},{1,129},{65,193... | collective-permute-start | bytes 196616 | tf_op jit(solution)/shard_map/ppermute | solution.py:28
  94.9 5.0 %collective-permute-start.36 = (f32[128,128]{1,0:T(8,128)S(1)}, f32[128,128]{1,0:T(8,128)S(1)}, u32[]{:S(2)}, u32[]{:S(2)}) collective-permute-start(f32[128,128]{1,0:T(8,128)S(1)} %get-tuple-element.99), channel_id=1, source_target_pairs={{64,0},{128,64},{192,128},{0,192},{65,1},{129,65},{193,129},{1,193... | collective-permute-start | bytes 196616 | tf_op jit(solution)/shard_map/ppermute | solution.py:28
where the time goes:
time: 102 us
  starting transfers between devices  69.7 us (68%)
  waiting for transfers between devices  16.4 us (16%)
  Pallas kernels  13.2 us (13%)
    ppermute x27, starting transfers between devices, ahead(): lax.ppermute(block, axis, [((i + shift) % size, i) for i in range(size)])  37.7 us
    ppermute x8, starting transfers between devices, swapped(): return lax.ppermute(block, 'loc_2', [(0, 1), (1, 0)])  18.8 us
    pallas_call x10, Pallas kernels, call(): pl.pallas_call(kernel, out_shape=shapes, in_specs=[VMEM] * len(args), out...  13.2 us
    ppermute x27, waiting for transfers between devices, ahead(): lax.ppermute(block, axis, [((i + shift) % size, i) for i in range(size)])  11.4 us
    all_to_all x1, starting transfers between devices, exchanged(): return lax.all_to_all(copies, axes, split_axis=0, concat_axis=0, tiled=True)  9.84 us
    ppermute x2, starting transfers between devices, neighbours(): lax.ppermute(block, 'tm', [(i, i ^ 1) for i in range(lax.axis_size('tm'))])  3.35 us
    ppermute x2, waiting for transfers between devices, neighbours(): lax.ppermute(block, 'tm', [(i, i ^ 1) for i in range(lax.axis_size('tm'))])  2.44 us
  transfers between devices with their start and end apart: 38, of which 14 were waited for; matrix products, arithmetic and copies ran while one was open for 0% of the time, Pallas kernels for 8%

commit v1 on v0

--- a/solution.py
+++ b/solution.py
@@ -11,7 +11,8 @@
 
 
 LOC = ("loc_0", "loc_1", "loc_2")
-EVERYONE = ("loc_0", "loc_1", "loc_2", "tm")
+TM = ("tm_0", "tm_1")
+EVERYONE = LOC + TM
 
 root_three = math.sqrt(3.0)
 space_reach = 2.5
@@ -36,7 +37,7 @@
 
 
 def neighbours(block):
-    return lax.ppermute(block, "tm", [(i, i ^ 1) for i in range(lax.axis_size("tm"))])
+    return lax.ppermute(block, "tm_1", [(0, 1), (1, 0)])
 
 
 def swapped(block):
@@ -107,12 +108,13 @@
         low_ref[rows, :] = low
 
 
-def time_kernel(stamps_ref, high_ref, low_ref, *, length):
-    own = lax.axis_index("tm")
+def time_kernel(stamps_ref, first, high_ref, low_ref, *, length):
+    parity = lax.axis_index("tm_1")
+    own = 2 * lax.axis_index("tm_0") + parity
     columns = upright(jnp.concatenate([stamps_ref[pl.ds(t, 1), :] for t in (own, own ^ 1)], 0))
     for s in range(2):
         for t in range(4):
-            line = stamps_ref[pl.ds((own + 2 * t) & 7, 1), :]
+            line = stamps_ref[pl.ds(((first + 2 * t) & 7) + parity, 1), :]
             apart = jnp.abs(columns[:, s : s + 1] - line)
             high, low = halves(matern(apart * (root_three / length)))
             high_ref[s * TILE : (s + 1) * TILE, t * TILE : (t + 1) * TILE] = high
@@ -124,10 +126,14 @@
         points_ref[:, k * TILE : (k + 1) * TILE] = lanes(sites_ref, place)
 
 
-def train_kernel(stamps_ref, sites_ref, noise_ref, *refs, time_length, length):
-    time_high_ref, time_low_ref, high_ref, low_ref, noise_out_ref, points_ref, at_ref = refs
+def times_kernel(stamps_ref, noise_ref, *refs, length):
+    by_place, by_shift, noise_out_ref = refs[:2], refs[2:4], refs[4]
     noise_out_ref[...] = noise_ref[...]
-    time_kernel(stamps_ref, time_high_ref, time_low_ref, length=time_length)
+    time_kernel(stamps_ref, 0, *by_place, length=length)
+    time_kernel(stamps_ref, 2 * lax.axis_index("tm_0"), *by_shift, length=length)
+
+
+def site_kernel(sites_ref, high_ref, low_ref, points_ref, at_ref, *, length):
     set_columns(sites_ref, points_ref)
     lines = jnp.concatenate([lanes(sites_ref, place) for place in row_places()], 0)
     columns = upright(lines)
@@ -163,13 +169,16 @@
 def fold_kernel(own_ref, other_ref, high_ref, low_ref, *outs):
     pair = jnp.concatenate([own_ref[:TILE, :], other_ref[:TILE, :]], 1)
     high, low = halves(pair)
-    for t, out in enumerate(outs):
+    for t in range(4):
         part = slice(t * TILE, (t + 1) * TILE)
         kernel_high = high_ref[:, part]
         summed = product(high, kernel_high) + product(high, low_ref[:, part])
-        out[:TILE, :] = summed + product(low, kernel_high)
-        if out.shape[0] > TILE:
-            out[TILE:, :] = own_ref[TILE:, :] + other_ref[TILE:, :]
+        summed = summed + product(low, kernel_high)
+        if len(outs) == 1:
+            outs[0][t] = summed
+        else:
+            outs[t][:TILE, :] = summed
+            outs[t][TILE:, :] = own_ref[TILE:, :] + other_ref[TILE:, :]
 
 
 def stack(blocks, high_ref, low_ref, at=0):
@@ -252,8 +261,18 @@
         out[...] = applied(high_ref, low_ref, rows, right_high[...], right_low[...])
 
 
+def both_kernel(*refs):
+    folds, befores, high_ref, low_ref = refs[:8], refs[8:12], *refs[12:14]
+    outs, right_high, right_low = refs[14:18], *refs[18:]
+    stack(folds, right_high, right_low)
+    for r, out in enumerate(outs):
+        rows = slice(r * TILE, (r + 1) * TILE)
+        out[:, :TILE] = befores[r][...]
+        out[:, TILE:] = applied(high_ref, low_ref, rows, right_high[...], right_low[...])
+
+
 def last_kernel(sums_ref, known_ref, start_ref, image_ref, *refs):
-    (a, b, c, d), (e, f, g, h), (estimate_ref, field_ref) = refs[:4], refs[4:8], refs[8:]
+    (a, b, c, d), (estimate_ref, field_ref) = refs[:4], refs[4:]
     sums = jnp.sum(sums_ref[...], axis=0)
     norm_next, curved, crossed = sums[:, 0:1], sums[:, 1:2], sums[:, 2:3]
     step, norm, first = known_ref[:, 0:1], known_ref[:, 1:2], known_ref[:, 2:3]
@@ -262,8 +281,8 @@
     start, image = start_ref[...], image_ref[:TILE, :]
     direction = (start - step * image) + follow * start
     estimate_ref[...] = step * start + step_next * direction
-    of_start = (a[...] + b[...]) + (c[...] + d[...])
-    of_image = (e[...] + f[...]) + (g[...] + h[...])
+    fields = (a[...] + b[...]) + (c[...] + d[...])
+    of_start, of_image = fields[:, :TILE], fields[:, TILE:]
     turned = (of_start - step * of_image) + follow * of_start
     field_ref[...] = (step * of_start + step_next * turned) * amplitude
 
@@ -293,29 +312,26 @@
     start = observed_mask.astype(f32) * observed
     start_rows = gathered(start, "loc_0", (2, 1, 3))
 
-    time_high, time_low, site_high, site_low, noise = call(
-        functools.partial(train_kernel, time_length=time_reach / times, length=space_length),
-        [((2 * TILE, 4 * TILE), bf16)] * 2 + split_pair + [((1, TILE), f32)],
+    *time_parts, noise = call(
+        functools.partial(times_kernel, length=time_reach / times),
+        [((2 * TILE, 4 * TILE), bf16)] * 4 + [((1, TILE), f32)],
         time_stamps.reshape(8, TILE),
+        noise_var[None, :],
+        flops=20 * 16 * TILE * TILE,
+    )
+    site_high, site_low = call(
+        functools.partial(site_kernel, length=space_length),
+        split_pair,
         training_site_positions,
-        noise_var[None, :],
         flops=400 * 4 * TILE * 8 * TILE,
         scratch=points,
     )
-
-    def folded(block, other):
-        parts = call(
-            fold_kernel,
-            [(block.shape, f32)] * 4,
-            block,
-            other,
-            time_high,
-            time_low,
-            flops=6 * TILE * 8 * TILE * TILE,
+    time_by_place, time_by_shift = time_parts[:2], time_parts[2:]
+
+    def folded(block, other, outs, high, low):
+        return call(
+            fold_kernel, outs, block, other, high, low, flops=6 * TILE * 8 * TILE * TILE
         )
-        others = [ahead(parts[k], "tm", -2 * k) for k in (1, 2, 3)]
-        mine, second, fourth, sixth = [parts[0]] + others
-        return (mine + fourth) + (second + sixth)
 
     def columns(block):
         held = gathered(block, "loc_1", (2, 1, 3))
@@ -325,8 +341,9 @@
         return [parts[0]] + [ahead(parts[s], "loc_0", -s) for s in (1, 2, 3)]
 
     other = neighbours(start)
-    start_fold = folded(start, other)
-    start_fold, start_rows = lax.optimization_barrier((start_fold, start_rows))
+    (start_parts,) = folded(start, other, [((4, TILE, TILE), f32)], *time_by_place)
+    start_parts = exchanged(start_parts, "tm_0")
+    start_fold = start_parts.sum(axis=0)
     start_folds = columns(start_fold)
     outers = call(
         apply_kernel,
@@ -362,7 +379,9 @@
     )
     other = neighbours(image)
     image_rows = gathered(image, "loc_0", (2, 1, 3))
-    image_fold = folded(image, other)
+    parts = folded(image, other, [((TILE + 8, TILE), f32)] * 4, *time_by_shift)
+    parts = [parts[0]] + [ahead(parts[k], "tm_0", -k) for k in (2, 3, 1)]
+    image_fold = (parts[0] + parts[1]) + (parts[2] + parts[3])
     start_fields = call(
         field_kernel,
         [square] * 4,
@@ -372,10 +391,6 @@
         flops=one_product,
         scratch=right,
     )
-    image_fold, image_rows, start_fields = lax.optimization_barrier(
-        (image_fold, image_rows, start_fields)
-    )
-    start_fields = to_owners(start_fields)
     image_folds = columns(image_fold)
     size = lax.axis_size(EVERYONE)
     sums, known = call(
@@ -392,10 +407,11 @@
         scratch=right,
     )
     sums = exchanged(sums, EVERYONE)
-    image_fields = call(
-        field_kernel,
-        [square] * 4,
+    fields = call(
+        both_kernel,
+        [((TILE, 2 * TILE), f32)] * 4,
         *image_folds,
+        *start_fields,
         test_high,
         test_low,
         flops=one_product,
@@ -409,15 +425,16 @@
             known,
             start,
             image,
-            *start_fields,
-            *to_owners(image_fields),
+            *to_owners(fields),
             flops=20 * TILE * TILE,
         )
     )
 
 
 def solution(mesh):
-    split = Mesh(mesh.devices.reshape(4, 4, 2, mesh.shape["tm"]), ("loc_0", "loc_1", "loc_2", "tm"))
-    in_specs = (P(LOC, "tm"), P(LOC, "tm"), P(), P(), P("tm"), P(), P())
-    out_specs = (P(LOC, "tm"), P(LOC, "tm"))
-    return jax.shard_map(whole, mesh=split, in_specs=in_specs, out_specs=out_specs, check_vma=False)
+    split = Mesh(mesh.devices.reshape(4, 4, 2, 4, 2), EVERYONE)
+    in_specs = (P(LOC, TM), P(LOC, TM), P(), P(), P(TM), P(), P())
+    out_specs = (P(LOC, TM), P(LOC, TM))
+    return jax.shard_map(
+        whole, mesh=split, in_specs=in_specs, out_specs=out_specs, check_vma=False
+    )

time: 102 us -> 99 us (0.971)
  starting transfers between devices: 69.7 us -> 64.5 us
    ppermute x27 -> x21, starting transfers between devices: 37.7 us -> 28 us  [ahead(): lax.ppermute(block, axis, [((i + shift) % size, i) for i in range(size)])]
    all_to_all x1 -> x2, starting transfers between devices: 9.84 us -> 16.7 us  [exchanged(): return lax.all_to_all(copies, axes, split_axis=0, concat_axis=0, tiled=True)]
    all_to_all x1 -> x2, waiting for transfers between devices: 0.77 us -> 5.07 us  [exchanged(): return lax.all_to_all(copies, axes, split_axis=0, concat_axis=0, tiled=True)]
    ppermute x8, starting transfers between devices: 18.8 us -> 15.9 us  [swapped(): return lax.ppermute(block, 'loc_2', [(0, 1), (1, 0)])]
    ppermute x27 -> x21, waiting for transfers between devices: 11.4 us -> 9.11 us  [ahead(): lax.ppermute(block, axis, [((i + shift) % size, i) for i in range(size)])]
    pallas_call x10 -> x11, Pallas kernels: 13.2 us -> 13.7 us  [call(): pl.pallas_call(kernel, out_shape=shapes, in_specs=[VMEM] * len(args), out...]
  transfers between devices with their start and end apart: 38 -> 33, of which waited for: 14 -> 8; matrix products, arithmetic and copies ran while one was open for 0% -> 0% of each run, Pallas kernels for 8% -> 9%
where the time goes in v1:
time: 99 us; the launch traced here: 98.7 us
  starting transfers between devices  64.5 us (65%)
  waiting for transfers between devices  17.4 us (18%)
  Pallas kernels  13.7 us (14%)
  local copies, waits for them, and re-layouts  1.33 us (1%)
    ppermute x21, starting transfers between devices, ahead(): lax.ppermute(block, axis, [((i + shift) % size, i) for i in range(size)])  28 us
    all_to_all x2, starting transfers between devices, exchanged(): return lax.all_to_all(copies, axes, split_axis=0, concat_axis=0, tiled=True)  16.7 us
    ppermute x8, starting transfers between devices, swapped(): return lax.ppermute(block, 'loc_2', [(0, 1), (1, 0)])  15.9 us
    pallas_call x11, Pallas kernels, call(): pl.pallas_call(kernel, out_shape=shapes, in_specs=[VMEM] * len(args), out...  13.7 us
    ppermute x21, waiting for transfers between devices, ahead(): lax.ppermute(block, axis, [((i + shift) % size, i) for i in range(size)])  9.11 us
    all_to_all x2, waiting for transfers between devices, exchanged(): return lax.all_to_all(copies, axes, split_axis=0, concat_axis=0, tiled=True)  5.07 us
    ppermute x2, starting transfers between devices, neighbours(): return lax.ppermute(block, 'tm_1', [(0, 1), (1, 0)])  3.91 us
    ppermute x2, waiting for transfers between devices, neighbours(): return lax.ppermute(block, 'tm_1', [(0, 1), (1, 0)])  2.3 us
  transfers between devices with their start and end apart: 33, of which 8 were waited for; matrix products, arithmetic and copies ran while one was open for 0% of the time, Pallas kernels for 9%

profile of v1, /device:TPU:1, one launch (start us, length us, event | category | flops | bytes accessed | tf_op | source)
XLA Modules:
  0.0 98.7 jit_solution(12626283027210181448)
XLA Ops:
  0.6 0.9 convert_multiply_fusion.own_ref.refs_8_.start_ref.refs_12_
  1.5 2.5 %collective-permute-start = (f32[128,128]{1,0:T(8,128)S(1)}, f32[128,128]{1,0:T(8,128)S(1)}, u32[]{:S(2)}, u32[]{:S(2)}) collective-permute-start(f32[128,128]{1,0:T(8,128)S(1)} %convert_multiply_fusion.own_ref.refs_8_.start_ref.refs_12_), channel_id=1, source_target_pairs={{0,1},{1,0},{2,3},{3,2},{4,5},{5,4},{6,7},{7,6},{8,9},{9,8},{10,11... | collective-permute-start | bytes 196616 | tf_op jit(solution)/shard_map/ppermute | solution.py:40
  4.1 0.7 copy-done.8
  4.7 0.6 shard_map.86
  5.3 0.4 collective-permute-done.other_ref
  5.7 1.1 %shard_map.87 = f32[4,128,128]{2,1,0:T(8,128)} custom-call(f32[128,128]{1,0:T(8,128)S(1)} %convert_multiply_fusion.own_ref.refs_8_.start_ref.refs_12_, f32[128,128]{1,0:T(8,128)S(1)} %collective-permute-done.other_ref, bf16[256,512]{1,0:T(8,128)(2,1)S(1)} %get-tuple-element.35.high_ref, bf16[256,512]{1,0:T(8,128)(2,1)S(1)} %get-tuple-element.36.low_ref), custom_call_target="tpu_custom_call" | custom-call | flops 100663296 | bytes 917504 | tf_op jit(solution)/shard_map/pallas_call | solution.py:59
  6.8 8.0 %all-to-all-start = ((f32[4,128,128]{2,1,0:T(8,128)}), f32[4,128,128]{2,1,0:T(8,128)S(1)}, u32[]{:S(2)}, u32[]{:S(2)}) async-start(f32[4,128,128]{2,1,0:T(8,128)} %shard_map.87), calls=%async_computation | async-start | bytes 524288 | tf_op jit(solution)/shard_map/all_to_all | solution.py:310
  14.8 2.7 %collective-permute-start.8 = (f32[128,128]{1,0:T(8,128)S(1)}, f32[128,128]{1,0:T(8,128)S(1)}, u32[]{:S(2)}, u32[]{:S(2)}) collective-permute-start(f32[128,128]{1,0:T(8,128)S(1)} %convert_multiply_fusion.own_ref.refs_8_.start_ref.refs_12_), channel_id=1, source_target_pairs={{64,0},{128,64},{192,128},{0,192},{65,1},{129,65},{193,129},{1,193... | collective-permute-start | bytes 196616 | tf_op jit(solution)/shard_map/ppermute | solution.py:29
  17.9 5.1 %all-to-all-done = f32[4,128,128]{2,1,0:T(8,128)S(1)} async-done(((f32[4,128,128]{2,1,0:T(8,128)}), f32[4,128,128]{2,1,0:T(8,128)S(1)}, u32[]{:S(2)}, u32[]{:S(2)}) %all-to-all-start) | async-done | bytes 262176 | tf_op jit(solution)/shard_map/all_to_all | solution.py:310
  23.0 2.6 %collective-permute-start.1 = (f32[128,128]{1,0:T(8,128)S(1)}, f32[128,128]{1,0:T(8,128)S(1)}, u32[]{:S(2)}, u32[]{:S(2)}) collective-permute-start(f32[128,128]{1,0:T(8,128)S(1)} %reduce_sum.9.refs_0_), channel_id=1, source_target_pairs={{16,0},{32,16},{48,32},{0,48},{17,1},{33,17},{49,33},{1,49},{18,2}... | collective-permute-start | bytes 196616 | tf_op jit(solution)/shard_map/ppermute | solution.py:29
  25.6 0.6 collective-permute-start.2
  26.1 0.6 collective-permute-start.3
  26.8 1.3 %collective-permute-start.10 = (f32[128,128]{1,0:T(8,128)S(1)}, f32[128,128]{1,0:T(8,128)S(1)}, u32[]{:S(2)}, u32[]{:S(2)}) collective-permute-start(f32[128,128]{1,0:T(8,128)S(1)} %convert_multiply_fusion.own_ref.refs_8_.start_ref.refs_12_), channel_id=1, source_target_pairs={{192,0},{0,64},{64,128},{128,192},{193,1},{1,65},{65,129},{129,193... | collective-permute-start | bytes 196616 | tf_op jit(solution)/shard_map/ppermute | solution.py:29
  28.1 4.5 %collective-permute-start.4 = (f32[128,128]{1,0:T(8,128)S(1)}, f32[128,128]{1,0:T(8,128)S(1)}, u32[]{:S(2)}, u32[]{:S(2)}) collective-permute-start(f32[128,128]{1,0:T(8,128)S(1)} %reduce_sum.9.refs_0_), channel_id=1, source_target_pairs={{0,8},{8,0},{1,9},{9,1},{2,10},{10,2},{3,11},{11,3},{4,12},{12,4},... | collective-permute-start | bytes 196616 | tf_op jit(solution)/shard_map/ppermute | solution.py:44
  32.7 2.4 %collective-permute-start.6 = (f32[128,128]{1,0:T(8,128)S(1)}, f32[128,128]{1,0:T(8,128)S(1)}, u32[]{:S(2)}, u32[]{:S(2)}) collective-permute-start(f32[128,128]{1,0:T(8,128)S(1)} %collective-permute-done.2.refs_2_), channel_id=1, source_target_pairs={{0,8},{8,0},{1,9},{9,1},{2,10},{10,2},{3,11},{11,3},{4,12},{12,4},... | collective-permute-start | bytes 196616 | tf_op jit(solution)/shard_map/ppermute | solution.py:44
  35.1 0.7 collective-permute-start.7
  35.8 2.7 %shard_map.88 = (bf16[512,1024]{1,0:T(8,128)(2,1)S(1)}, bf16[512,1024]{1,0:T(8,128)(2,1)S(1)}) custom-call(f32[2,4096]{1,0:T(2,128)S(1)} %copy-done.4), custom_call_target="tpu_custom_call" | custom-call | flops 209715200 | bytes 2129920 | tf_op jit(solution)/shard_map/pallas_call | solution.py:59
  38.6 1.1 %shard_map.89 = (f32[136,128]{1,0:T(8,128)S(1)}, f32[136,128]{1,0:T(8,128)S(1)}, f32[136,128]{1,0:T(8,128)S(1)}, f32[136,128]{1,0:T(8,128)S(1)}) custom-call(f32[128,128]{1,0:T(8,128)S(1)} %reduce_sum.9.refs_0_, f32[128,128]{1,0:T(8,128)S(1)} %collective-permute-done.1.refs_1_, f32[128,128]{1,0:T(8,128)S(1)} %collective-permute-done.2.refs_2_, ...), custom_call_target="tpu_custom_call" | custom-call | flops 402653184 | bytes 3162624 | tf_op jit(solution)/shard_map/pallas_call | solution.py:59
  39.6 1.4 %collective-permute-start.11 = (f32[136,128]{1,0:T(8,128)S(1)}, f32[136,128]{1,0:T(8,128)S(1)}, u32[]{:S(2)}, u32[]{:S(2)}) collective-permute-start(f32[136,128]{1,0:T(8,128)S(1)} %get-tuple-element.41.refs_9_), channel_id=1, source_target_pairs={{192,0},{0,64},{64,128},{128,192},{193,1},{1,65},{65,129},{129,193... | collective-permute-start | bytes 208904 | tf_op jit(solution)/shard_map/ppermute | solution.py:29
  41.0 2.6 %collective-permute-start.12 = (f32[136,128]{1,0:T(8,128)S(1)}, f32[136,128]{1,0:T(8,128)S(1)}, u32[]{:S(2)}, u32[]{:S(2)}) collective-permute-start(f32[136,128]{1,0:T(8,128)S(1)} %get-tuple-element.42.refs_10_), channel_id=1, source_target_pairs={{128,0},{192,64},{0,128},{64,192},{129,1},{193,65},{1,129},{65,193... | collective-permute-start | bytes 208904 | tf_op jit(solution)/shard_map/ppermute | solution.py:29
  43.6 1.1 %collective-permute-start.13 = (f32[136,128]{1,0:T(8,128)S(1)}, f32[136,128]{1,0:T(8,128)S(1)}, u32[]{:S(2)}, u32[]{:S(2)}) collective-permute-start(f32[136,128]{1,0:T(8,128)S(1)} %get-tuple-element.43.refs_11_), channel_id=1, source_target_pairs={{64,0},{128,64},{192,128},{0,192},{65,1},{129,65},{193,129},{1,193... | collective-permute-start | bytes 208904 | tf_op jit(solution)/shard_map/ppermute | solution.py:29
  44.7 3.5 %shard_map.90 = (bf16[512,1024]{1,0:T(8,128)(2,1)S(1)}, bf16[512,1024]{1,0:T(8,128)(2,1)S(1)}) custom-call(f32[2,4096]{1,0:T(2,128)S(1)} %copy-done.4, f32[2,4096]{1,0:T(2,128)S(1)} %copy-done.5, s32[32,128]{1,0:T(8,128)S(1)} %bitcast.3), custom_call_target="tpu_custom_call" | custom-call | flops 314572800 | bytes 2179072 | tf_op jit(solution)/shard_map/pallas_call | solution.py:59
  48.3 1.4 %collective-permute-start.14 = (f32[136,128]{1,0:T(8,128)S(1)}, f32[136,128]{1,0:T(8,128)S(1)}, u32[]{:S(2)}, u32[]{:S(2)}) collective-permute-start(f32[136,128]{1,0:T(8,128)S(1)} %shard_map.91.own_ref.refs_16_.image_ref), channel_id=1, source_target_pairs={{0,1},{1,0},{2,3},{3,2},{4,5},{5,4},{6,7},{7,6},{8,9},{9,8},{10,11... | collective-permute-start | bytes 208904 | tf_op jit(solution)/shard_map/ppermute | solution.py:40
  49.7 1.9 %collective-permute-done.14.other_ref = f32[136,128]{1,0:T(8,128)S(1)} collective-permute-done((f32[136,128]{1,0:T(8,128)S(1)}, f32[136,128]{1,0:T(8,128)S(1)}, u32[]{:S(2)}, u32[]{:S(2)}) %collective-permute-start.14) | collective-permute-done | bytes 69664 | tf_op jit(solution)/shard_map/ppermute | solution.py:40
  51.9 1.3 %collective-permute-start.16 = (f32[136,128]{1,0:T(8,128)S(1)}, f32[136,128]{1,0:T(8,128)S(1)}, u32[]{:S(2)}, u32[]{:S(2)}) collective-permute-start(f32[136,128]{1,0:T(8,128)S(1)} %get-tuple-element.54), channel_id=1, source_target_pairs={{2,0},{4,2},{6,4},{0,6},{3,1},{5,3},{7,5},{1,7},{10,8},{12,10},{14... | collective-permute-start | bytes 208904 | tf_op jit(solution)/shard_map/ppermute | solution.py:29
  53.2 1.1 %collective-permute-start.17 = (f32[136,128]{1,0:T(8,128)S(1)}, f32[136,128]{1,0:T(8,128)S(1)}, u32[]{:S(2)}, u32[]{:S(2)}) collective-permute-start(f32[136,128]{1,0:T(8,128)S(1)} %get-tuple-element.55), channel_id=1, source_target_pairs={{6,0},{0,2},{2,4},{4,6},{7,1},{1,3},{3,5},{5,7},{14,8},{8,10},{10,... | collective-permute-start | bytes 208904 | tf_op jit(solution)/shard_map/ppermute | solution.py:29
  54.3 2.8 %collective-permute-start.15 = (f32[136,128]{1,0:T(8,128)S(1)}, f32[136,128]{1,0:T(8,128)S(1)}, u32[]{:S(2)}, u32[]{:S(2)}) collective-permute-start(f32[136,128]{1,0:T(8,128)S(1)} %get-tuple-element.53), channel_id=1, source_target_pairs={{4,0},{6,2},{0,4},{2,6},{5,1},{7,3},{1,5},{3,7},{12,8},{14,10},{8,... | collective-permute-start | bytes 208904 | tf_op jit(solution)/shard_map/ppermute | solution.py:29
  57.2 0.8 collective-permute-start.25
  58.0 1.4 %collective-permute-start.26 = (f32[136,128]{1,0:T(8,128)S(1)}, f32[136,128]{1,0:T(8,128)S(1)}, u32[]{:S(2)}, u32[]{:S(2)}) collective-permute-start(f32[136,128]{1,0:T(8,128)S(1)} %shard_map.91.own_ref.refs_16_.image_ref), channel_id=1, source_target_pairs={{128,0},{192,64},{0,128},{64,192},{129,1},{193,65},{1,129},{65,193... | collective-permute-start | bytes 208904 | tf_op jit(solution)/shard_map/ppermute | solution.py:29
  59.3 3.1 %collective-permute-done.15 = f32[136,128]{1,0:T(8,128)S(1)} collective-permute-done((f32[136,128]{1,0:T(8,128)S(1)}, f32[136,128]{1,0:T(8,128)S(1)}, u32[]{:S(2)}, u32[]{:S(2)}) %collective-permute-start.15) | collective-permute-done | bytes 69664 | tf_op jit(solution)/shard_map/ppermute | solution.py:29
  62.8 0.9 collective-permute-start.19
  63.7 0.8 collective-permute-start.20
  64.9 4.5 %collective-permute-start.21 = (f32[136,128]{1,0:T(8,128)S(1)}, f32[136,128]{1,0:T(8,128)S(1)}, u32[]{:S(2)}, u32[]{:S(2)}) collective-permute-start(f32[136,128]{1,0:T(8,128)S(1)} %add_add_fusion.refs_0_), channel_id=1, source_target_pairs={{0,8},{8,0},{1,9},{9,1},{2,10},{10,2},{3,11},{11,3},{4,12},{12,4},... | collective-permute-start | bytes 208904 | tf_op jit(solution)/shard_map/ppermute | solution.py:44
  69.3 0.9 collective-permute-start.22
  70.2 2.1 %collective-permute-start.23 = (f32[136,128]{1,0:T(8,128)S(1)}, f32[136,128]{1,0:T(8,128)S(1)}, u32[]{:S(2)}, u32[]{:S(2)}) collective-permute-start(f32[136,128]{1,0:T(8,128)S(1)} %collective-permute-done.19.refs_2_), channel_id=1, source_target_pairs={{0,8},{8,0},{1,9},{9,1},{2,10},{10,2},{3,11},{11,3},{4,12},{12,4},... | collective-permute-start | bytes 208904 | tf_op jit(solution)/shard_map/ppermute | solution.py:44
  72.3 0.7 collective-permute-start.24
  73.2 0.7 collective-permute-done.24.refs_7_
  74.0 1.2 %shard_map.93 = (f32[256,1,128]{2,1,0:T(1,128)S(1)}, f32[1,128]{1,0:T(1,128)S(1)}) custom-call(f32[136,128]{1,0:T(8,128)S(1)} %add_add_fusion.refs_0_, f32[136,128]{1,0:T(8,128)S(1)} %collective-permute-done.18.refs_1_, f32[136,128]{1,0:T(8,128)S(1)} %collective-permute-done.19.refs_2_, f32[136,128]{1,0:T(8,128)S(1)} %collective-permute-done.20.refs_3_, ...), custom_call_target="tpu_custom_call" | custom-call | flops 402653184 | bytes 3605504 | tf_op jit(solution)/shard_map/pallas_call | solution.py:59
  75.2 0.6 copy-done.3
  75.9 8.6 %all-to-all-start.1 = ((f32[256,1,128]{2,1,0:T(1,128)}), f32[256,1,128]{2,1,0:T(1,128)S(1)}, u32[]{:S(2)}, u32[]{:S(2)}) async-start(f32[256,1,128]{2,1,0:T(1,128)} %copy-done.3), calls=%async_computation.1 | async-start | bytes 262144 | tf_op jit(solution)/shard_map/all_to_all | solution.py:310
  84.5 1.0 %shard_map.94 = (f32[128,128]{1,0:T(8,128)S(1)}, f32[128,128]{1,0:T(8,128)S(1)}, f32[128,128]{1,0:T(8,128)S(1)}, f32[128,128]{1,0:T(8,128)S(1)}) custom-call(f32[128,128]{1,0:T(8,128)S(1)} %reduce_sum.9.refs_0_, f32[128,128]{1,0:T(8,128)S(1)} %collective-permute-done.1.refs_1_, f32[128,128]{1,0:T(8,128)S(1)} %collective-permute-done.2.refs_2_, ...), custom_call_target="tpu_custom_call" | custom-call | flops 402653184 | bytes 2883584 | tf_op jit(solution)/shard_map/pallas_call | solution.py:59
  85.6 1.0 %shard_map.95 = (f32[128,256]{1,0:T(8,128)S(1)}, f32[128,256]{1,0:T(8,128)S(1)}, f32[128,256]{1,0:T(8,128)S(1)}, f32[128,256]{1,0:T(8,128)S(1)}) custom-call(f32[136,128]{1,0:T(8,128)S(1)} %add_add_fusion.refs_0_, f32[136,128]{1,0:T(8,128)S(1)} %collective-permute-done.18.refs_1_, f32[136,128]{1,0:T(8,128)S(1)} %collective-permute-done.19.refs_2_, ...), custom_call_target="tpu_custom_call" | custom-call | flops 402653184 | bytes 3440640 | tf_op jit(solution)/shard_map/pallas_call | solution.py:59
  86.6 1.4 %collective-permute-start.28 = (f32[128,256]{1,0:T(8,128)S(1)}, f32[128,256]{1,0:T(8,128)S(1)}, u32[]{:S(2)}, u32[]{:S(2)}) collective-permute-start(f32[128,256]{1,0:T(8,128)S(1)} %get-tuple-element.65), channel_id=1, source_target_pairs={{192,0},{0,64},{64,128},{128,192},{193,1},{1,65},{65,129},{129,193... | collective-permute-start | bytes 393224 | tf_op jit(solution)/shard_map/ppermute | solution.py:29
  88.0 2.5 %collective-permute-start.29 = (f32[128,256]{1,0:T(8,128)S(1)}, f32[128,256]{1,0:T(8,128)S(1)}, u32[]{:S(2)}, u32[]{:S(2)}) collective-permute-start(f32[128,256]{1,0:T(8,128)S(1)} %get-tuple-element.66), channel_id=1, source_target_pairs={{128,0},{192,64},{0,128},{64,192},{129,1},{193,65},{1,129},{65,193... | collective-permute-start | bytes 393224 | tf_op jit(solution)/shard_map/ppermute | solution.py:29
  90.5 1.1 %collective-permute-start.30 = (f32[128,256]{1,0:T(8,128)S(1)}, f32[128,256]{1,0:T(8,128)S(1)}, u32[]{:S(2)}, u32[]{:S(2)}) collective-permute-start(f32[128,256]{1,0:T(8,128)S(1)} %get-tuple-element.67), channel_id=1, source_target_pairs={{64,0},{128,64},{192,128},{0,192},{65,1},{129,65},{193,129},{1,193... | collective-permute-start | bytes 393224 | tf_op jit(solution)/shard_map/ppermute | solution.py:29
  91.6 0.6 collective-permute-done.28.refs_1_
  92.2 5.3 %collective-permute-done.29.refs_2_ = f32[128,256]{1,0:T(8,128)S(1)} collective-permute-done((f32[128,256]{1,0:T(8,128)S(1)}, f32[128,256]{1,0:T(8,128)S(1)}, u32[]{:S(2)}, u32[]{:S(2)}) %collective-permute-start.29) | collective-permute-done | bytes 131104 | tf_op jit(solution)/shard_map/ppermute | solution.py:29
  97.6 1.2 %shard_map.96 = (f32[128,128]{1,0:T(8,128)}, f32[128,128]{1,0:T(8,128)}) custom-call(f32[256,1,128]{2,1,0:T(1,128)S(1)} %all-to-all-done.1.sums_ref, f32[1,128]{1,0:T(1,128)S(1)} %get-tuple-element.57.known_ref, f32[128,128]{1,0:T(8,128)S(1)} %convert_multiply_fusion.own_ref.refs_8_.start_ref.refs_12_, f32[136,128]{1,0:T(8,128)S(1)} %shard_map.91.own_ref.refs_16_.image_ref, ...), custom_call_target="tpu_custom_call" | custom-call | flops 327680 | bytes 922112 | tf_op jit(solution)/shard_map/pallas_call | solution.py:59
  (50 shorter events, 1.9 us)
Async XLA Ops:
  0.6 3.4 %copy-start.7 = (f32[1024]{0:T(1024)S(1)}, f32[1024]{0:T(1024)}, u32[]{:S(2)}) copy-start(f32[1024]{0:T(1024)} %param.10) | copy-start | bytes 12292
  1.5 4.2 %collective-permute-start = (f32[128,128]{1,0:T(8,128)S(1)}, f32[128,128]{1,0:T(8,128)S(1)}, u32[]{:S(2)}, u32[]{:S(2)}) collective-permute-start(f32[128,128]{1,0:T(8,128)S(1)} %convert_multiply_fusion.own_ref.refs_8_.start_ref.refs_12_), channel_id=1, source_target_pairs={{0,1},{1,0},{2,3},{3,2},{4,5},{5,4},{6,7},{7,6},{8,9},{9,8},{10,11... | collective-permute-start | bytes 196616 | tf_op jit(solution)/shard_map/ppermute | solution.py:40
  4.1 0.7 copy-start.8
  5.3 1.5 %copy-start.1 = (bf16[256,512]{1,0:T(8,128)(2,1)}, bf16[256,512]{1,0:T(8,128)(2,1)S(1)}, u32[]{:S(2)}) copy-start(bf16[256,512]{1,0:T(8,128)(2,1)S(1)} %get-tuple-element.51.low_ref) | copy-start | bytes 786436
  6.8 16.2 %all-to-all-start = ((f32[4,128,128]{2,1,0:T(8,128)}), f32[4,128,128]{2,1,0:T(8,128)S(1)}, u32[]{:S(2)}, u32[]{:S(2)}) async-start(f32[4,128,128]{2,1,0:T(8,128)} %shard_map.87), calls=%async_computation | async-start | bytes 524288 | tf_op jit(solution)/shard_map/all_to_all | solution.py:310
  14.8 21.0 %copy-start.4 = (f32[2,4096]{1,0:T(2,128)S(1)}, f32[2,4096]{1,0:T(2,128)}, u32[]{:S(2)}) copy-start(f32[2,4096]{1,0:T(2,128)} %sites_ref.3) | copy-start | bytes 98308
  14.8 11.9 %collective-permute-start.8 = (f32[128,128]{1,0:T(8,128)S(1)}, f32[128,128]{1,0:T(8,128)S(1)}, u32[]{:S(2)}, u32[]{:S(2)}) collective-permute-start(f32[128,128]{1,0:T(8,128)S(1)} %convert_multiply_fusion.own_ref.refs_8_.start_ref.refs_12_), channel_id=1, source_target_pairs={{64,0},{128,64},{192,128},{0,192},{65,1},{129,65},{193,129},{1,193... | collective-permute-start | bytes 196616 | tf_op jit(solution)/shard_map/ppermute | solution.py:29
  17.6 10.5 %collective-permute-start.9 = (f32[128,128]{1,0:T(8,128)S(1)}, f32[128,128]{1,0:T(8,128)S(1)}, u32[]{:S(2)}, u32[]{:S(2)}) collective-permute-start(f32[128,128]{1,0:T(8,128)S(1)} %convert_multiply_fusion.own_ref.refs_8_.start_ref.refs_12_), channel_id=1, source_target_pairs={{128,0},{192,64},{0,128},{64,192},{129,1},{193,65},{1,129},{65,193... | collective-permute-start | bytes 196616 | tf_op jit(solution)/shard_map/ppermute | solution.py:29
  23.0 9.6 %collective-permute-start.1 = (f32[128,128]{1,0:T(8,128)S(1)}, f32[128,128]{1,0:T(8,128)S(1)}, u32[]{:S(2)}, u32[]{:S(2)}) collective-permute-start(f32[128,128]{1,0:T(8,128)S(1)} %reduce_sum.9.refs_0_), channel_id=1, source_target_pairs={{16,0},{32,16},{48,32},{0,48},{17,1},{33,17},{49,33},{1,49},{18,2}... | collective-permute-start | bytes 196616 | tf_op jit(solution)/shard_map/ppermute | solution.py:29
  25.6 7.1 %collective-permute-start.2 = (f32[128,128]{1,0:T(8,128)S(1)}, f32[128,128]{1,0:T(8,128)S(1)}, u32[]{:S(2)}, u32[]{:S(2)}) collective-permute-start(f32[128,128]{1,0:T(8,128)S(1)} %reduce_sum.9.refs_0_), channel_id=1, source_target_pairs={{32,0},{48,16},{0,32},{16,48},{33,1},{49,17},{1,33},{17,49},{34,2}... | collective-permute-start | bytes 196616 | tf_op jit(solution)/shard_map/ppermute | solution.py:29
  26.1 9.0 %collective-permute-start.3 = (f32[128,128]{1,0:T(8,128)S(1)}, f32[128,128]{1,0:T(8,128)S(1)}, u32[]{:S(2)}, u32[]{:S(2)}) collective-permute-start(f32[128,128]{1,0:T(8,128)S(1)} %reduce_sum.9.refs_0_), channel_id=1, source_target_pairs={{48,0},{0,16},{16,32},{32,48},{49,1},{1,17},{17,33},{33,49},{50,2}... | collective-permute-start | bytes 196616 | tf_op jit(solution)/shard_map/ppermute | solution.py:29
  26.8 11.7 %collective-permute-start.10 = (f32[128,128]{1,0:T(8,128)S(1)}, f32[128,128]{1,0:T(8,128)S(1)}, u32[]{:S(2)}, u32[]{:S(2)}) collective-permute-start(f32[128,128]{1,0:T(8,128)S(1)} %convert_multiply_fusion.own_ref.refs_8_.start_ref.refs_12_), channel_id=1, source_target_pairs={{192,0},{0,64},{64,128},{128,192},{193,1},{1,65},{65,129},{129,193... | collective-permute-start | bytes 196616 | tf_op jit(solution)/shard_map/ppermute | solution.py:29
  28.1 10.4 %collective-permute-start.4 = (f32[128,128]{1,0:T(8,128)S(1)}, f32[128,128]{1,0:T(8,128)S(1)}, u32[]{:S(2)}, u32[]{:S(2)}) collective-permute-start(f32[128,128]{1,0:T(8,128)S(1)} %reduce_sum.9.refs_0_), channel_id=1, source_target_pairs={{0,8},{8,0},{1,9},{9,1},{2,10},{10,2},{3,11},{11,3},{4,12},{12,4},... | collective-permute-start | bytes 196616 | tf_op jit(solution)/shard_map/ppermute | solution.py:44
  32.6 5.9 %collective-permute-start.5 = (f32[128,128]{1,0:T(8,128)S(1)}, f32[128,128]{1,0:T(8,128)S(1)}, u32[]{:S(2)}, u32[]{:S(2)}) collective-permute-start(f32[128,128]{1,0:T(8,128)S(1)} %collective-permute-done.1.refs_1_), channel_id=1, source_target_pairs={{0,8},{8,0},{1,9},{9,1},{2,10},{10,2},{3,11},{11,3},{4,12},{12,4},... | collective-permute-start | bytes 196616 | tf_op jit(solution)/shard_map/ppermute | solution.py:44
  32.7 5.8 %collective-permute-start.6 = (f32[128,128]{1,0:T(8,128)S(1)}, f32[128,128]{1,0:T(8,128)S(1)}, u32[]{:S(2)}, u32[]{:S(2)}) collective-permute-start(f32[128,128]{1,0:T(8,128)S(1)} %collective-permute-done.2.refs_2_), channel_id=1, source_target_pairs={{0,8},{8,0},{1,9},{9,1},{2,10},{10,2},{3,11},{11,3},{4,12},{12,4},... | collective-permute-start | bytes 196616 | tf_op jit(solution)/shard_map/ppermute | solution.py:44
  35.1 3.4 %collective-permute-start.7 = (f32[128,128]{1,0:T(8,128)S(1)}, f32[128,128]{1,0:T(8,128)S(1)}, u32[]{:S(2)}, u32[]{:S(2)}) collective-permute-start(f32[128,128]{1,0:T(8,128)S(1)} %collective-permute-done.3.refs_3_), channel_id=1, source_target_pairs={{0,8},{8,0},{1,9},{9,1},{2,10},{10,2},{3,11},{11,3},{4,12},{12,4},... | collective-permute-start | bytes 196616 | tf_op jit(solution)/shard_map/ppermute | solution.py:44
  38.5 6.2 %copy-start.5 = (f32[2,4096]{1,0:T(2,128)S(1)}, f32[2,4096]{1,0:T(2,128)}, u32[]{:S(2)}) copy-start(f32[2,4096]{1,0:T(2,128)} %tests_ref.1) | copy-start | bytes 98308
  38.5 6.1 %copy-start.6 = (s32[4096]{0:T(1024)S(1)}, s32[4096]{0:T(1024)}, u32[]{:S(2)}) copy-start(s32[4096]{0:T(1024)} %param.13) | copy-start | bytes 49156
  39.6 8.6 %collective-permute-start.11 = (f32[136,128]{1,0:T(8,128)S(1)}, f32[136,128]{1,0:T(8,128)S(1)}, u32[]{:S(2)}, u32[]{:S(2)}) collective-permute-start(f32[136,128]{1,0:T(8,128)S(1)} %get-tuple-element.41.refs_9_), channel_id=1, source_target_pairs={{192,0},{0,64},{64,128},{128,192},{193,1},{1,65},{65,129},{129,193... | collective-permute-start | bytes 208904 | tf_op jit(solution)/shard_map/ppermute | solution.py:29
  41.0 7.2 %collective-permute-start.12 = (f32[136,128]{1,0:T(8,128)S(1)}, f32[136,128]{1,0:T(8,128)S(1)}, u32[]{:S(2)}, u32[]{:S(2)}) collective-permute-start(f32[136,128]{1,0:T(8,128)S(1)} %get-tuple-element.42.refs_10_), channel_id=1, source_target_pairs={{128,0},{192,64},{0,128},{64,192},{129,1},{193,65},{1,129},{65,193... | collective-permute-start | bytes 208904 | tf_op jit(solution)/shard_map/ppermute | solution.py:29
  43.6 4.6 %collective-permute-start.13 = (f32[136,128]{1,0:T(8,128)S(1)}, f32[136,128]{1,0:T(8,128)S(1)}, u32[]{:S(2)}, u32[]{:S(2)}) collective-permute-start(f32[136,128]{1,0:T(8,128)S(1)} %get-tuple-element.43.refs_11_), channel_id=1, source_target_pairs={{64,0},{128,64},{192,128},{0,192},{65,1},{129,65},{193,129},{1,193... | collective-permute-start | bytes 208904 | tf_op jit(solution)/shard_map/ppermute | solution.py:29
  44.7 3.5 %copy-start = (s32[128,128]{1,0:T(8,128)S(1)}, s32[128,128]{1,0:T(8,128)}, u32[]{:S(2)}) copy-start(s32[128,128]{1,0:T(8,128)} %mask_ref.1) | copy-start | bytes 196612
  48.2 3.3 %copy-start.2 = (bf16[256,512]{1,0:T(8,128)(2,1)S(1)}, bf16[256,512]{1,0:T(8,128)(2,1)}, u32[]{:S(2)}) copy-start(bf16[256,512]{1,0:T(8,128)(2,1)} %copy-done.1) | copy-start | bytes 786436
  48.3 3.2 %collective-permute-start.14 = (f32[136,128]{1,0:T(8,128)S(1)}, f32[136,128]{1,0:T(8,128)S(1)}, u32[]{:S(2)}, u32[]{:S(2)}) collective-permute-start(f32[136,128]{1,0:T(8,128)S(1)} %shard_map.91.own_ref.refs_16_.image_ref), channel_id=1, source_target_pairs={{0,1},{1,0},{2,3},{3,2},{4,5},{5,4},{6,7},{7,6},{8,9},{9,8},{10,11... | collective-permute-start | bytes 208904 | tf_op jit(solution)/shard_map/ppermute | solution.py:40
  51.9 7.4 %collective-permute-start.16 = (f32[136,128]{1,0:T(8,128)S(1)}, f32[136,128]{1,0:T(8,128)S(1)}, u32[]{:S(2)}, u32[]{:S(2)}) collective-permute-start(f32[136,128]{1,0:T(8,128)S(1)} %get-tuple-element.54), channel_id=1, source_target_pairs={{2,0},{4,2},{6,4},{0,6},{3,1},{5,3},{7,5},{1,7},{10,8},{12,10},{14... | collective-permute-start | bytes 208904 | tf_op jit(solution)/shard_map/ppermute | solution.py:29
  53.2 6.2 %collective-permute-start.17 = (f32[136,128]{1,0:T(8,128)S(1)}, f32[136,128]{1,0:T(8,128)S(1)}, u32[]{:S(2)}, u32[]{:S(2)}) collective-permute-start(f32[136,128]{1,0:T(8,128)S(1)} %get-tuple-element.55), channel_id=1, source_target_pairs={{6,0},{0,2},{2,4},{4,6},{7,1},{1,3},{3,5},{5,7},{14,8},{8,10},{10,... | collective-permute-start | bytes 208904 | tf_op jit(solution)/shard_map/ppermute | solution.py:29
  54.3 8.1 %collective-permute-start.15 = (f32[136,128]{1,0:T(8,128)S(1)}, f32[136,128]{1,0:T(8,128)S(1)}, u32[]{:S(2)}, u32[]{:S(2)}) collective-permute-start(f32[136,128]{1,0:T(8,128)S(1)} %get-tuple-element.53), channel_id=1, source_target_pairs={{4,0},{6,2},{0,4},{2,6},{5,1},{7,3},{1,5},{3,7},{12,8},{14,10},{8,... | collective-permute-start | bytes 208904 | tf_op jit(solution)/shard_map/ppermute | solution.py:29
  57.2 7.3 %collective-permute-start.25 = (f32[136,128]{1,0:T(8,128)S(1)}, f32[136,128]{1,0:T(8,128)S(1)}, u32[]{:S(2)}, u32[]{:S(2)}) collective-permute-start(f32[136,128]{1,0:T(8,128)S(1)} %shard_map.91.own_ref.refs_16_.image_ref), channel_id=1, source_target_pairs={{64,0},{128,64},{192,128},{0,192},{65,1},{129,65},{193,129},{1,193... | collective-permute-start | bytes 208904 | tf_op jit(solution)/shard_map/ppermute | solution.py:29
  58.0 6.9 %collective-permute-start.26 = (f32[136,128]{1,0:T(8,128)S(1)}, f32[136,128]{1,0:T(8,128)S(1)}, u32[]{:S(2)}, u32[]{:S(2)}) collective-permute-start(f32[136,128]{1,0:T(8,128)S(1)} %shard_map.91.own_ref.refs_16_.image_ref), channel_id=1, source_target_pairs={{128,0},{192,64},{0,128},{64,192},{129,1},{193,65},{1,129},{65,193... | collective-permute-start | bytes 208904 | tf_op jit(solution)/shard_map/ppermute | solution.py:29
  62.5 6.9 %collective-permute-start.18 = (f32[136,128]{1,0:T(8,128)S(1)}, f32[136,128]{1,0:T(8,128)S(1)}, u32[]{:S(2)}, u32[]{:S(2)}) collective-permute-start(f32[136,128]{1,0:T(8,128)S(1)} %add_add_fusion.refs_0_), channel_id=1, source_target_pairs={{16,0},{32,16},{48,32},{0,48},{17,1},{33,17},{49,33},{1,49},{18,2}... | collective-permute-start | bytes 208904 | tf_op jit(solution)/shard_map/ppermute | solution.py:29
  62.8 7.4 %collective-permute-start.19 = (f32[136,128]{1,0:T(8,128)S(1)}, f32[136,128]{1,0:T(8,128)S(1)}, u32[]{:S(2)}, u32[]{:S(2)}) collective-permute-start(f32[136,128]{1,0:T(8,128)S(1)} %add_add_fusion.refs_0_), channel_id=1, source_target_pairs={{32,0},{48,16},{0,32},{16,48},{33,1},{49,17},{1,33},{17,49},{34,2}... | collective-permute-start | bytes 208904 | tf_op jit(solution)/shard_map/ppermute | solution.py:29
  63.7 8.6 %collective-permute-start.20 = (f32[136,128]{1,0:T(8,128)S(1)}, f32[136,128]{1,0:T(8,128)S(1)}, u32[]{:S(2)}, u32[]{:S(2)}) collective-permute-start(f32[136,128]{1,0:T(8,128)S(1)} %add_add_fusion.refs_0_), channel_id=1, source_target_pairs={{48,0},{0,16},{16,32},{32,48},{49,1},{1,17},{17,33},{33,49},{50,2}... | collective-permute-start | bytes 208904 | tf_op jit(solution)/shard_map/ppermute | solution.py:29
  64.5 8.6 %collective-permute-start.27 = (f32[136,128]{1,0:T(8,128)S(1)}, f32[136,128]{1,0:T(8,128)S(1)}, u32[]{:S(2)}, u32[]{:S(2)}) collective-permute-start(f32[136,128]{1,0:T(8,128)S(1)} %shard_map.91.own_ref.refs_16_.image_ref), channel_id=1, source_target_pairs={{192,0},{0,64},{64,128},{128,192},{193,1},{1,65},{65,129},{129,193... | collective-permute-start | bytes 208904 | tf_op jit(solution)/shard_map/ppermute | solution.py:29
  64.9 8.2 %collective-permute-start.21 = (f32[136,128]{1,0:T(8,128)S(1)}, f32[136,128]{1,0:T(8,128)S(1)}, u32[]{:S(2)}, u32[]{:S(2)}) collective-permute-start(f32[136,128]{1,0:T(8,128)S(1)} %add_add_fusion.refs_0_), channel_id=1, source_target_pairs={{0,8},{8,0},{1,9},{9,1},{2,10},{10,2},{3,11},{11,3},{4,12},{12,4},... | collective-permute-start | bytes 208904 | tf_op jit(solution)/shard_map/ppermute | solution.py:44
  69.3 3.8 %collective-permute-start.22 = (f32[136,128]{1,0:T(8,128)S(1)}, f32[136,128]{1,0:T(8,128)S(1)}, u32[]{:S(2)}, u32[]{:S(2)}) collective-permute-start(f32[136,128]{1,0:T(8,128)S(1)} %collective-permute-done.18.refs_1_), channel_id=1, source_target_pairs={{0,8},{8,0},{1,9},{9,1},{2,10},{10,2},{3,11},{11,3},{4,12},{12,4},... | collective-permute-start | bytes 208904 | tf_op jit(solution)/shard_map/ppermute | solution.py:44
  70.2 3.0 %collective-permute-start.23 = (f32[136,128]{1,0:T(8,128)S(1)}, f32[136,128]{1,0:T(8,128)S(1)}, u32[]{:S(2)}, u32[]{:S(2)}) collective-permute-start(f32[136,128]{1,0:T(8,128)S(1)} %collective-permute-done.19.refs_2_), channel_id=1, source_target_pairs={{0,8},{8,0},{1,9},{9,1},{2,10},{10,2},{3,11},{11,3},{4,12},{12,4},... | collective-permute-start | bytes 208904 | tf_op jit(solution)/shard_map/ppermute | solution.py:44
  72.3 1.6 %collective-permute-start.24 = (f32[136,128]{1,0:T(8,128)S(1)}, f32[136,128]{1,0:T(8,128)S(1)}, u32[]{:S(2)}, u32[]{:S(2)}) collective-permute-start(f32[136,128]{1,0:T(8,128)S(1)} %collective-permute-done.20.refs_3_), channel_id=1, source_target_pairs={{0,8},{8,0},{1,9},{9,1},{2,10},{10,2},{3,11},{11,3},{4,12},{12,4},... | collective-permute-start | bytes 208904 | tf_op jit(solution)/shard_map/ppermute | solution.py:44
  75.2 0.7 copy-start.3
  75.9 21.7 %all-to-all-start.1 = ((f32[256,1,128]{2,1,0:T(1,128)}), f32[256,1,128]{2,1,0:T(1,128)S(1)}, u32[]{:S(2)}, u32[]{:S(2)}) async-start(f32[256,1,128]{2,1,0:T(1,128)} %copy-done.3), calls=%async_computation.1 | async-start | bytes 262144 | tf_op jit(solution)/shard_map/all_to_all | solution.py:310
  86.6 5.6 %collective-permute-start.28 = (f32[128,256]{1,0:T(8,128)S(1)}, f32[128,256]{1,0:T(8,128)S(1)}, u32[]{:S(2)}, u32[]{:S(2)}) collective-permute-start(f32[128,256]{1,0:T(8,128)S(1)} %get-tuple-element.65), channel_id=1, source_target_pairs={{192,0},{0,64},{64,128},{128,192},{193,1},{1,65},{65,129},{129,193... | collective-permute-start | bytes 393224 | tf_op jit(solution)/shard_map/ppermute | solution.py:29
  88.0 9.5 %collective-permute-start.29 = (f32[128,256]{1,0:T(8,128)S(1)}, f32[128,256]{1,0:T(8,128)S(1)}, u32[]{:S(2)}, u32[]{:S(2)}) collective-permute-start(f32[128,256]{1,0:T(8,128)S(1)} %get-tuple-element.66), channel_id=1, source_target_pairs={{128,0},{192,64},{0,128},{64,192},{129,1},{193,65},{1,129},{65,193... | collective-permute-start | bytes 393224 | tf_op jit(solution)/shard_map/ppermute | solution.py:29
  90.5 7.1 %collective-permute-start.30 = (f32[128,256]{1,0:T(8,128)S(1)}, f32[128,256]{1,0:T(8,128)S(1)}, u32[]{:S(2)}, u32[]{:S(2)}) collective-permute-start(f32[128,256]{1,0:T(8,128)S(1)} %get-tuple-element.67), channel_id=1, source_target_pairs={{64,0},{128,64},{192,128},{0,192},{65,1},{129,65},{193,129},{1,193... | collective-permute-start | bytes 393224 | tf_op jit(solution)/shard_map/ppermute | solution.py:29

commit v2 on v1

--- a/solution.py
+++ b/solution.py
@@ -108,13 +108,13 @@
         low_ref[rows, :] = low
 
 
-def time_kernel(stamps_ref, first, high_ref, low_ref, *, length):
-    parity = lax.axis_index("tm_1")
-    own = 2 * lax.axis_index("tm_0") + parity
+def time_kernel(stamps_ref, noise_ref, high_ref, low_ref, noise_out_ref, *, length):
+    noise_out_ref[...] = noise_ref[...]
+    own = 2 * lax.axis_index("tm_0") + lax.axis_index("tm_1")
     columns = upright(jnp.concatenate([stamps_ref[pl.ds(t, 1), :] for t in (own, own ^ 1)], 0))
     for s in range(2):
         for t in range(4):
-            line = stamps_ref[pl.ds(((first + 2 * t) & 7) + parity, 1), :]
+            line = stamps_ref[pl.ds((own + 2 * t) & 7, 1), :]
             apart = jnp.abs(columns[:, s : s + 1] - line)
             high, low = halves(matern(apart * (root_three / length)))
             high_ref[s * TILE : (s + 1) * TILE, t * TILE : (t + 1) * TILE] = high
@@ -124,13 +124,6 @@
 def set_columns(sites_ref, points_ref):
     for k, place in enumerate(column_places()):
         points_ref[:, k * TILE : (k + 1) * TILE] = lanes(sites_ref, place)
-
-
-def times_kernel(stamps_ref, noise_ref, *refs, length):
-    by_place, by_shift, noise_out_ref = refs[:2], refs[2:4], refs[4]
-    noise_out_ref[...] = noise_ref[...]
-    time_kernel(stamps_ref, 0, *by_place, length=length)
-    time_kernel(stamps_ref, 2 * lax.axis_index("tm_0"), *by_shift, length=length)
 
 
 def site_kernel(sites_ref, high_ref, low_ref, points_ref, at_ref, *, length):
@@ -169,16 +162,13 @@
 def fold_kernel(own_ref, other_ref, high_ref, low_ref, *outs):
     pair = jnp.concatenate([own_ref[:TILE, :], other_ref[:TILE, :]], 1)
     high, low = halves(pair)
-    for t in range(4):
+    for t, out in enumerate(outs):
         part = slice(t * TILE, (t + 1) * TILE)
         kernel_high = high_ref[:, part]
         summed = product(high, kernel_high) + product(high, low_ref[:, part])
-        summed = summed + product(low, kernel_high)
-        if len(outs) == 1:
-            outs[0][t] = summed
-        else:
-            outs[t][:TILE, :] = summed
-            outs[t][TILE:, :] = own_ref[TILE:, :] + other_ref[TILE:, :]
+        out[:TILE, :] = summed + product(low, kernel_high)
+        if out.shape[0] > TILE:
+            out[TILE:, :] = own_ref[TILE:, :] + other_ref[TILE:, :]
 
 
 def stack(blocks, high_ref, low_ref, at=0):
@@ -312,12 +302,12 @@
     start = observed_mask.astype(f32) * observed
     start_rows = gathered(start, "loc_0", (2, 1, 3))
 
-    *time_parts, noise = call(
-        functools.partial(times_kernel, length=time_reach / times),
-        [((2 * TILE, 4 * TILE), bf16)] * 4 + [((1, TILE), f32)],
+    time_high, time_low, noise = call(
+        functools.partial(time_kernel, length=time_reach / times),
+        [((2 * TILE, 4 * TILE), bf16)] * 2 + [((1, TILE), f32)],
         time_stamps.reshape(8, TILE),
         noise_var[None, :],
-        flops=20 * 16 * TILE * TILE,
+        flops=20 * 8 * TILE * TILE,
     )
     site_high, site_low = call(
         functools.partial(site_kernel, length=space_length),
@@ -326,12 +316,19 @@
         flops=400 * 4 * TILE * 8 * TILE,
         scratch=points,
     )
-    time_by_place, time_by_shift = time_parts[:2], time_parts[2:]
-
-    def folded(block, other, outs, high, low):
-        return call(
-            fold_kernel, outs, block, other, high, low, flops=6 * TILE * 8 * TILE * TILE
+
+    def folded(block, other):
+        parts = call(
+            fold_kernel,
+            [(block.shape, f32)] * 4,
+            block,
+            other,
+            time_high,
+            time_low,
+            flops=6 * TILE * 8 * TILE * TILE,
         )
+        parts = [parts[0]] + [ahead(parts[k], "tm_0", -k) for k in (2, 3, 1)]
+        return (parts[0] + parts[1]) + (parts[2] + parts[3])
 
     def columns(block):
         held = gathered(block, "loc_1", (2, 1, 3))
@@ -341,9 +338,7 @@
         return [parts[0]] + [ahead(parts[s], "loc_0", -s) for s in (1, 2, 3)]
 
     other = neighbours(start)
-    (start_parts,) = folded(start, other, [((4, TILE, TILE), f32)], *time_by_place)
-    start_parts = exchanged(start_parts, "tm_0")
-    start_fold = start_parts.sum(axis=0)
+    start_fold = folded(start, other)
     start_folds = columns(start_fold)
     outers = call(
         apply_kernel,
@@ -367,7 +362,6 @@
     )
 
     owned = to_owners(outers)
-    owned, test_high, test_low = lax.optimization_barrier((owned, test_high, test_low))
     (image,) = call(
         image_kernel,
         [((TILE + 8, TILE), f32)],
@@ -379,9 +373,7 @@
     )
     other = neighbours(image)
     image_rows = gathered(image, "loc_0", (2, 1, 3))
-    parts = folded(image, other, [((TILE + 8, TILE), f32)] * 4, *time_by_shift)
-    parts = [parts[0]] + [ahead(parts[k], "tm_0", -k) for k in (2, 3, 1)]
-    image_fold = (parts[0] + parts[1]) + (parts[2] + parts[3])
+    image_fold = folded(image, other)
     start_fields = call(
         field_kernel,
         [square] * 4,

time: 99 us -> 99.7 us (level)
  starting transfers between devices: 64.5 us -> 68.2 us
  waiting for transfers between devices: 17.4 us -> 15.4 us
    ppermute x21 -> x24, starting transfers between devices: 28 us -> 39 us  [ahead(): lax.ppermute(block, axis, [((i + shift) % size, i) for i in range(size)])]
    all_to_all x2 -> x1, starting transfers between devices: 16.7 us -> 10.2 us  [exchanged(): return lax.all_to_all(copies, axes, split_axis=0, concat_axis=0, tiled=True)]
    all_to_all x2 -> x1, waiting for transfers between devices: 5.07 us -> 0.01 us  [exchanged(): return lax.all_to_all(copies, axes, split_axis=0, concat_axis=0, tiled=True)]
    ppermute x21 -> x24, waiting for transfers between devices: 9.11 us -> 11.4 us  [ahead(): lax.ppermute(block, axis, [((i + shift) % size, i) for i in range(size)])]
  transfers between devices with their start and end apart: 33 -> 35, of which waited for: 8 -> 11; matrix products, arithmetic and copies ran while one was open for 0% -> 0% of each run, Pallas kernels for 9% -> 9%
where the time goes in v2:
time: 99.7 us; the launch traced here: 99.4 us
  starting transfers between devices  68.2 us (68%)
  waiting for transfers between devices  15.4 us (15%)
  Pallas kernels  13.4 us (13%)
    ppermute x24, starting transfers between devices, ahead(): lax.ppermute(block, axis, [((i + shift) % size, i) for i in range(size)])  39 us
    ppermute x8, starting transfers between devices, swapped(): return lax.ppermute(block, 'loc_2', [(0, 1), (1, 0)])  15.6 us
    pallas_call x11, Pallas kernels, call(): pl.pallas_call(kernel, out_shape=shapes, in_specs=[VMEM] * len(args), out...  13.4 us
    ppermute x24, waiting for transfers between devices, ahead(): lax.ppermute(block, axis, [((i + shift) % size, i) for i in range(size)])  11.4 us
    all_to_all x1, starting transfers between devices, exchanged(): return lax.all_to_all(copies, axes, split_axis=0, concat_axis=0, tiled=True)  10.2 us
    ppermute x2, starting transfers between devices, neighbours(): return lax.ppermute(block, 'tm_1', [(0, 1), (1, 0)])  3.37 us
    ppermute x2, waiting for transfers between devices, neighbours(): return lax.ppermute(block, 'tm_1', [(0, 1), (1, 0)])  3.06 us
  transfers between devices with their start and end apart: 35, of which 11 were waited for; matrix products, arithmetic and copies ran while one was open for 0% of the time, Pallas kernels for 9%

profile of v2, /device:TPU:1, one launch (start us, length us, event | category | flops | bytes accessed | tf_op | source)
XLA Modules:
  0.0 99.4 jit_solution(1512481390675417517)
XLA Ops:
  0.6 0.9 convert_multiply_fusion.own_ref.refs_8_.start_ref.refs_12_
  1.5 2.5 %collective-permute-start = (f32[128,128]{1,0:T(8,128)S(1)}, f32[128,128]{1,0:T(8,128)S(1)}, u32[]{:S(2)}, u32[]{:S(2)}) collective-permute-start(f32[128,128]{1,0:T(8,128)S(1)} %convert_multiply_fusion.own_ref.refs_8_.start_ref.refs_12_), channel_id=1, source_target_pairs={{0,1},{1,0},{2,3},{3,2},{4,5},{5,4},{6,7},{7,6},{8,9},{9,8},{10,11... | collective-permute-start | bytes 196616 | tf_op jit(solution)/shard_map/ppermute | solution.py:40
  4.1 0.7 copy-done.5
  5.1 0.6 collective-permute-done.other_ref
  5.7 0.4 shard_map.87
  6.1 5.9 %collective-permute-start.2 = (f32[128,128]{1,0:T(8,128)S(1)}, f32[128,128]{1,0:T(8,128)S(1)}, u32[]{:S(2)}, u32[]{:S(2)}) collective-permute-start(f32[128,128]{1,0:T(8,128)S(1)} %get-tuple-element.35), channel_id=1, source_target_pairs={{2,0},{4,2},{6,4},{0,6},{3,1},{5,3},{7,5},{1,7},{10,8},{12,10},{14... | collective-permute-start | bytes 196616 | tf_op jit(solution)/shard_map/ppermute | solution.py:29
  12.0 3.3 %collective-permute-start.1 = (f32[128,128]{1,0:T(8,128)S(1)}, f32[128,128]{1,0:T(8,128)S(1)}, u32[]{:S(2)}, u32[]{:S(2)}) collective-permute-start(f32[128,128]{1,0:T(8,128)S(1)} %get-tuple-element.34), channel_id=1, source_target_pairs={{4,0},{6,2},{0,4},{2,6},{5,1},{7,3},{1,5},{3,7},{12,8},{14,10},{8,... | collective-permute-start | bytes 196616 | tf_op jit(solution)/shard_map/ppermute | solution.py:29
  15.3 2.7 %collective-permute-start.11 = (f32[128,128]{1,0:T(8,128)S(1)}, f32[128,128]{1,0:T(8,128)S(1)}, u32[]{:S(2)}, u32[]{:S(2)}) collective-permute-start(f32[128,128]{1,0:T(8,128)S(1)} %convert_multiply_fusion.own_ref.refs_8_.start_ref.refs_12_), channel_id=1, source_target_pairs={{64,0},{128,64},{192,128},{0,192},{65,1},{129,65},{193,129},{1,193... | collective-permute-start | bytes 196616 | tf_op jit(solution)/shard_map/ppermute | solution.py:29
  18.4 1.0 %collective-permute-done.1 = f32[128,128]{1,0:T(8,128)S(1)} collective-permute-done((f32[128,128]{1,0:T(8,128)S(1)}, f32[128,128]{1,0:T(8,128)S(1)}, u32[]{:S(2)}, u32[]{:S(2)}) %collective-permute-start.1) | collective-permute-done | bytes 65568 | tf_op jit(solution)/shard_map/ppermute | solution.py:29
  19.4 2.6 %collective-permute-start.4 = (f32[128,128]{1,0:T(8,128)S(1)}, f32[128,128]{1,0:T(8,128)S(1)}, u32[]{:S(2)}, u32[]{:S(2)}) collective-permute-start(f32[128,128]{1,0:T(8,128)S(1)} %add_add_fusion.1.refs_0_), channel_id=1, source_target_pairs={{16,0},{32,16},{48,32},{0,48},{17,1},{33,17},{49,33},{1,49},{18,2}... | collective-permute-start | bytes 196616 | tf_op jit(solution)/shard_map/ppermute | solution.py:29
  22.0 0.5 collective-permute-start.5
  22.5 0.6 collective-permute-start.6
  23.1 1.3 %collective-permute-start.13 = (f32[128,128]{1,0:T(8,128)S(1)}, f32[128,128]{1,0:T(8,128)S(1)}, u32[]{:S(2)}, u32[]{:S(2)}) collective-permute-start(f32[128,128]{1,0:T(8,128)S(1)} %convert_multiply_fusion.own_ref.refs_8_.start_ref.refs_12_), channel_id=1, source_target_pairs={{192,0},{0,64},{64,128},{128,192},{193,1},{1,65},{65,129},{129,193... | collective-permute-start | bytes 196616 | tf_op jit(solution)/shard_map/ppermute | solution.py:29
  24.4 4.1 %collective-permute-start.7 = (f32[128,128]{1,0:T(8,128)S(1)}, f32[128,128]{1,0:T(8,128)S(1)}, u32[]{:S(2)}, u32[]{:S(2)}) collective-permute-start(f32[128,128]{1,0:T(8,128)S(1)} %add_add_fusion.1.refs_0_), channel_id=1, source_target_pairs={{0,8},{8,0},{1,9},{9,1},{2,10},{10,2},{3,11},{11,3},{4,12},{12,4},... | collective-permute-start | bytes 196616 | tf_op jit(solution)/shard_map/ppermute | solution.py:44
  28.6 2.4 %collective-permute-start.9 = (f32[128,128]{1,0:T(8,128)S(1)}, f32[128,128]{1,0:T(8,128)S(1)}, u32[]{:S(2)}, u32[]{:S(2)}) collective-permute-start(f32[128,128]{1,0:T(8,128)S(1)} %collective-permute-done.5.refs_2_), channel_id=1, source_target_pairs={{0,8},{8,0},{1,9},{9,1},{2,10},{10,2},{3,11},{11,3},{4,12},{12,4},... | collective-permute-start | bytes 196616 | tf_op jit(solution)/shard_map/ppermute | solution.py:44
  31.0 0.7 collective-permute-start.10
  31.6 2.7 %shard_map.88 = (bf16[512,1024]{1,0:T(8,128)(2,1)S(1)}, bf16[512,1024]{1,0:T(8,128)(2,1)S(1)}) custom-call(f32[2,4096]{1,0:T(2,128)S(1)} %copy-done.1), custom_call_target="tpu_custom_call" | custom-call | flops 209715200 | bytes 2129920 | tf_op jit(solution)/shard_map/pallas_call | solution.py:59
  34.4 1.0 %shard_map.89 = (f32[136,128]{1,0:T(8,128)S(1)}, f32[136,128]{1,0:T(8,128)S(1)}, f32[136,128]{1,0:T(8,128)S(1)}, f32[136,128]{1,0:T(8,128)S(1)}) custom-call(f32[128,128]{1,0:T(8,128)S(1)} %add_add_fusion.1.refs_0_, f32[128,128]{1,0:T(8,128)S(1)} %collective-permute-done.4.refs_1_, f32[128,128]{1,0:T(8,128)S(1)} %collective-permute-done.5.refs_2_, ...), custom_call_target="tpu_custom_call" | custom-call | flops 402653184 | bytes 3162624 | tf_op jit(solution)/shard_map/pallas_call | solution.py:59
  35.5 1.4 %collective-permute-start.14 = (f32[136,128]{1,0:T(8,128)S(1)}, f32[136,128]{1,0:T(8,128)S(1)}, u32[]{:S(2)}, u32[]{:S(2)}) collective-permute-start(f32[136,128]{1,0:T(8,128)S(1)} %get-tuple-element.41.refs_9_), channel_id=1, source_target_pairs={{192,0},{0,64},{64,128},{128,192},{193,1},{1,65},{65,129},{129,193... | collective-permute-start | bytes 208904 | tf_op jit(solution)/shard_map/ppermute | solution.py:29
  36.8 2.6 %collective-permute-start.15 = (f32[136,128]{1,0:T(8,128)S(1)}, f32[136,128]{1,0:T(8,128)S(1)}, u32[]{:S(2)}, u32[]{:S(2)}) collective-permute-start(f32[136,128]{1,0:T(8,128)S(1)} %get-tuple-element.42.refs_10_), channel_id=1, source_target_pairs={{128,0},{192,64},{0,128},{64,192},{129,1},{193,65},{1,129},{65,193... | collective-permute-start | bytes 208904 | tf_op jit(solution)/shard_map/ppermute | solution.py:29
  39.4 1.1 %collective-permute-start.16 = (f32[136,128]{1,0:T(8,128)S(1)}, f32[136,128]{1,0:T(8,128)S(1)}, u32[]{:S(2)}, u32[]{:S(2)}) collective-permute-start(f32[136,128]{1,0:T(8,128)S(1)} %get-tuple-element.43.refs_11_), channel_id=1, source_target_pairs={{64,0},{128,64},{192,128},{0,192},{65,1},{129,65},{193,129},{1,193... | collective-permute-start | bytes 208904 | tf_op jit(solution)/shard_map/ppermute | solution.py:29
  40.6 2.6 %collective-permute-done.15.c = f32[136,128]{1,0:T(8,128)S(1)} collective-permute-done((f32[136,128]{1,0:T(8,128)S(1)}, f32[136,128]{1,0:T(8,128)S(1)}, u32[]{:S(2)}, u32[]{:S(2)}) %collective-permute-start.15) | collective-permute-done | bytes 69664 | tf_op jit(solution)/shard_map/ppermute | solution.py:29
  43.2 0.8 collective-permute-start.17
  44.0 2.4 %collective-permute-done.17.other_ref = f32[136,128]{1,0:T(8,128)S(1)} collective-permute-done((f32[136,128]{1,0:T(8,128)S(1)}, f32[136,128]{1,0:T(8,128)S(1)}, u32[]{:S(2)}, u32[]{:S(2)}) %collective-permute-start.17) | collective-permute-done | bytes 69664 | tf_op jit(solution)/shard_map/ppermute | solution.py:40
  46.5 0.4 shard_map.91
  46.8 4.2 %collective-permute-start.19 = (f32[136,128]{1,0:T(8,128)S(1)}, f32[136,128]{1,0:T(8,128)S(1)}, u32[]{:S(2)}, u32[]{:S(2)}) collective-permute-start(f32[136,128]{1,0:T(8,128)S(1)} %get-tuple-element.46), channel_id=1, source_target_pairs={{2,0},{4,2},{6,4},{0,6},{3,1},{5,3},{7,5},{1,7},{10,8},{12,10},{14... | collective-permute-start | bytes 208904 | tf_op jit(solution)/shard_map/ppermute | solution.py:29
  51.1 2.7 %collective-permute-start.18 = (f32[136,128]{1,0:T(8,128)S(1)}, f32[136,128]{1,0:T(8,128)S(1)}, u32[]{:S(2)}, u32[]{:S(2)}) collective-permute-start(f32[136,128]{1,0:T(8,128)S(1)} %get-tuple-element.45), channel_id=1, source_target_pairs={{4,0},{6,2},{0,4},{2,6},{5,1},{7,3},{1,5},{3,7},{12,8},{14,10},{8,... | collective-permute-start | bytes 208904 | tf_op jit(solution)/shard_map/ppermute | solution.py:29
  53.7 1.7 %collective-permute-start.28 = (f32[136,128]{1,0:T(8,128)S(1)}, f32[136,128]{1,0:T(8,128)S(1)}, u32[]{:S(2)}, u32[]{:S(2)}) collective-permute-start(f32[136,128]{1,0:T(8,128)S(1)} %shard_map.90.own_ref.refs_16_.image_ref), channel_id=1, source_target_pairs={{64,0},{128,64},{192,128},{0,192},{65,1},{129,65},{193,129},{1,193... | collective-permute-start | bytes 208904 | tf_op jit(solution)/shard_map/ppermute | solution.py:29
  55.4 0.7 collective-permute-start.29
  56.4 2.2 %collective-permute-done.18 = f32[136,128]{1,0:T(8,128)S(1)} collective-permute-done((f32[136,128]{1,0:T(8,128)S(1)}, f32[136,128]{1,0:T(8,128)S(1)}, u32[]{:S(2)}, u32[]{:S(2)}) %collective-permute-start.18) | collective-permute-done | bytes 69664 | tf_op jit(solution)/shard_map/ppermute | solution.py:29
  58.8 1.0 %collective-permute-start.22 = (f32[136,128]{1,0:T(8,128)S(1)}, f32[136,128]{1,0:T(8,128)S(1)}, u32[]{:S(2)}, u32[]{:S(2)}) collective-permute-start(f32[136,128]{1,0:T(8,128)S(1)} %add_add_fusion.refs_0_), channel_id=1, source_target_pairs={{32,0},{48,16},{0,32},{16,48},{33,1},{49,17},{1,33},{17,49},{34,2}... | collective-permute-start | bytes 208904 | tf_op jit(solution)/shard_map/ppermute | solution.py:29
  59.8 0.8 collective-permute-start.23
  60.6 0.4 collective-permute-start.30
  61.0 5.1 %collective-permute-start.24 = (f32[136,128]{1,0:T(8,128)S(1)}, f32[136,128]{1,0:T(8,128)S(1)}, u32[]{:S(2)}, u32[]{:S(2)}) collective-permute-start(f32[136,128]{1,0:T(8,128)S(1)} %add_add_fusion.refs_0_), channel_id=1, source_target_pairs={{0,8},{8,0},{1,9},{9,1},{2,10},{10,2},{3,11},{11,3},{4,12},{12,4},... | collective-permute-start | bytes 208904 | tf_op jit(solution)/shard_map/ppermute | solution.py:44
  66.4 2.2 %collective-permute-start.26 = (f32[136,128]{1,0:T(8,128)S(1)}, f32[136,128]{1,0:T(8,128)S(1)}, u32[]{:S(2)}, u32[]{:S(2)}) collective-permute-start(f32[136,128]{1,0:T(8,128)S(1)} %collective-permute-done.22.refs_2_), channel_id=1, source_target_pairs={{0,8},{8,0},{1,9},{9,1},{2,10},{10,2},{3,11},{11,3},{4,12},{12,4},... | collective-permute-start | bytes 208904 | tf_op jit(solution)/shard_map/ppermute | solution.py:44
  68.6 0.7 collective-permute-start.27
  69.5 0.7 collective-permute-done.27.refs_7_
  70.3 1.9 %shard_map.92 = (f32[256,1,128]{2,1,0:T(1,128)}, f32[1,128]{1,0:T(1,128)S(1)}) custom-call(f32[136,128]{1,0:T(8,128)S(1)} %add_add_fusion.refs_0_, f32[136,128]{1,0:T(8,128)S(1)} %collective-permute-done.21.refs_1_, f32[136,128]{1,0:T(8,128)S(1)} %collective-permute-done.22.refs_2_, f32[136,128]{1,0:T(8,128)S(1)} %collective-permute-done.23.refs_3_, ...), custom_call_target="tpu_custom_call" | custom-call | flops 402653184 | bytes 3605504 | tf_op jit(solution)/shard_map/pallas_call | solution.py:59
  72.1 10.2 %all-to-all-start = ((f32[256,1,128]{2,1,0:T(1,128)}), f32[256,1,128]{2,1,0:T(1,128)S(1)}, u32[]{:S(2)}, u32[]{:S(2)}) async-start(f32[256,1,128]{2,1,0:T(1,128)} %get-tuple-element.48), calls=%async_computation | async-start | bytes 262144 | tf_op jit(solution)/shard_map/all_to_all | solution.py:300
  82.4 3.5 %shard_map.93 = (bf16[512,1024]{1,0:T(8,128)(2,1)S(1)}, bf16[512,1024]{1,0:T(8,128)(2,1)S(1)}) custom-call(f32[2,4096]{1,0:T(2,128)S(1)} %copy-done.1, f32[2,4096]{1,0:T(2,128)S(1)} %copy-done.2, s32[32,128]{1,0:T(8,128)S(1)} %bitcast.3), custom_call_target="tpu_custom_call" | custom-call | flops 314572800 | bytes 2179072 | tf_op jit(solution)/shard_map/pallas_call | solution.py:59
  85.9 1.0 %shard_map.94 = (f32[128,128]{1,0:T(8,128)S(1)}, f32[128,128]{1,0:T(8,128)S(1)}, f32[128,128]{1,0:T(8,128)S(1)}, f32[128,128]{1,0:T(8,128)S(1)}) custom-call(f32[128,128]{1,0:T(8,128)S(1)} %add_add_fusion.1.refs_0_, f32[128,128]{1,0:T(8,128)S(1)} %collective-permute-done.4.refs_1_, f32[128,128]{1,0:T(8,128)S(1)} %collective-permute-done.5.refs_2_, ...), custom_call_target="tpu_custom_call" | custom-call | flops 402653184 | bytes 2883584 | tf_op jit(solution)/shard_map/pallas_call | solution.py:59
  86.9 1.0 %shard_map.95 = (f32[128,256]{1,0:T(8,128)S(1)}, f32[128,256]{1,0:T(8,128)S(1)}, f32[128,256]{1,0:T(8,128)S(1)}, f32[128,256]{1,0:T(8,128)S(1)}) custom-call(f32[136,128]{1,0:T(8,128)S(1)} %add_add_fusion.refs_0_, f32[136,128]{1,0:T(8,128)S(1)} %collective-permute-done.21.refs_1_, f32[136,128]{1,0:T(8,128)S(1)} %collective-permute-done.22.refs_2_, ...), custom_call_target="tpu_custom_call" | custom-call | flops 402653184 | bytes 3440640 | tf_op jit(solution)/shard_map/pallas_call | solution.py:59
  87.9 1.4 %collective-permute-start.31 = (f32[128,256]{1,0:T(8,128)S(1)}, f32[128,256]{1,0:T(8,128)S(1)}, u32[]{:S(2)}, u32[]{:S(2)}) collective-permute-start(f32[128,256]{1,0:T(8,128)S(1)} %get-tuple-element.57), channel_id=1, source_target_pairs={{192,0},{0,64},{64,128},{128,192},{193,1},{1,65},{65,129},{129,193... | collective-permute-start | bytes 393224 | tf_op jit(solution)/shard_map/ppermute | solution.py:29
  89.4 2.5 %collective-permute-start.32 = (f32[128,256]{1,0:T(8,128)S(1)}, f32[128,256]{1,0:T(8,128)S(1)}, u32[]{:S(2)}, u32[]{:S(2)}) collective-permute-start(f32[128,256]{1,0:T(8,128)S(1)} %get-tuple-element.58), channel_id=1, source_target_pairs={{128,0},{192,64},{0,128},{64,192},{129,1},{193,65},{1,129},{65,193... | collective-permute-start | bytes 393224 | tf_op jit(solution)/shard_map/ppermute | solution.py:29
  91.8 1.1 %collective-permute-start.33 = (f32[128,256]{1,0:T(8,128)S(1)}, f32[128,256]{1,0:T(8,128)S(1)}, u32[]{:S(2)}, u32[]{:S(2)}) collective-permute-start(f32[128,256]{1,0:T(8,128)S(1)} %get-tuple-element.59), channel_id=1, source_target_pairs={{64,0},{128,64},{192,128},{0,192},{65,1},{129,65},{193,129},{1,193... | collective-permute-start | bytes 393224 | tf_op jit(solution)/shard_map/ppermute | solution.py:29
  93.0 0.7 collective-permute-done.31.refs_1_
  93.7 4.6 %collective-permute-done.32.refs_2_ = f32[128,256]{1,0:T(8,128)S(1)} collective-permute-done((f32[128,256]{1,0:T(8,128)S(1)}, f32[128,256]{1,0:T(8,128)S(1)}, u32[]{:S(2)}, u32[]{:S(2)}) %collective-permute-start.32) | collective-permute-done | bytes 131104 | tf_op jit(solution)/shard_map/ppermute | solution.py:29
  98.2 1.2 %shard_map.96 = (f32[128,128]{1,0:T(8,128)}, f32[128,128]{1,0:T(8,128)}) custom-call(f32[256,1,128]{2,1,0:T(1,128)S(1)} %all-to-all-done.sums_ref, f32[1,128]{1,0:T(1,128)S(1)} %get-tuple-element.49.known_ref, f32[128,128]{1,0:T(8,128)S(1)} %convert_multiply_fusion.own_ref.refs_8_.start_ref.refs_12_, f32[136,128]{1,0:T(8,128)S(1)} %shard_map.90.own_ref.refs_16_.image_ref, ...), custom_call_target="tpu_custom_call" | custom-call | flops 327680 | bytes 922112 | tf_op jit(solution)/shard_map/pallas_call | solution.py:59
  (48 shorter events, 1.9 us)
Async XLA Ops:
  0.6 3.4 %copy-start.4 = (f32[1024]{0:T(1024)S(1)}, f32[1024]{0:T(1024)}, u32[]{:S(2)}) copy-start(f32[1024]{0:T(1024)} %param.10) | copy-start | bytes 12292
  1.5 4.2 %collective-permute-start = (f32[128,128]{1,0:T(8,128)S(1)}, f32[128,128]{1,0:T(8,128)S(1)}, u32[]{:S(2)}, u32[]{:S(2)}) collective-permute-start(f32[128,128]{1,0:T(8,128)S(1)} %convert_multiply_fusion.own_ref.refs_8_.start_ref.refs_12_), channel_id=1, source_target_pairs={{0,1},{1,0},{2,3},{3,2},{4,5},{5,4},{6,7},{7,6},{8,9},{9,8},{10,11... | collective-permute-start | bytes 196616 | tf_op jit(solution)/shard_map/ppermute | solution.py:40
  4.1 0.7 copy-start.5
  6.1 12.3 %collective-permute-start.2 = (f32[128,128]{1,0:T(8,128)S(1)}, f32[128,128]{1,0:T(8,128)S(1)}, u32[]{:S(2)}, u32[]{:S(2)}) collective-permute-start(f32[128,128]{1,0:T(8,128)S(1)} %get-tuple-element.35), channel_id=1, source_target_pairs={{2,0},{4,2},{6,4},{0,6},{3,1},{5,3},{7,5},{1,7},{10,8},{12,10},{14... | collective-permute-start | bytes 196616 | tf_op jit(solution)/shard_map/ppermute | solution.py:29
  12.0 6.3 %collective-permute-start.3 = (f32[128,128]{1,0:T(8,128)S(1)}, f32[128,128]{1,0:T(8,128)S(1)}, u32[]{:S(2)}, u32[]{:S(2)}) collective-permute-start(f32[128,128]{1,0:T(8,128)S(1)} %get-tuple-element.36), channel_id=1, source_target_pairs={{6,0},{0,2},{2,4},{4,6},{7,1},{1,3},{3,5},{5,7},{14,8},{8,10},{10,... | collective-permute-start | bytes 196616 | tf_op jit(solution)/shard_map/ppermute | solution.py:29
  12.0 7.4 %collective-permute-start.1 = (f32[128,128]{1,0:T(8,128)S(1)}, f32[128,128]{1,0:T(8,128)S(1)}, u32[]{:S(2)}, u32[]{:S(2)}) collective-permute-start(f32[128,128]{1,0:T(8,128)S(1)} %get-tuple-element.34), channel_id=1, source_target_pairs={{4,0},{6,2},{0,4},{2,6},{5,1},{7,3},{1,5},{3,7},{12,8},{14,10},{8,... | collective-permute-start | bytes 196616 | tf_op jit(solution)/shard_map/ppermute | solution.py:29
  15.3 7.8 %collective-permute-start.11 = (f32[128,128]{1,0:T(8,128)S(1)}, f32[128,128]{1,0:T(8,128)S(1)}, u32[]{:S(2)}, u32[]{:S(2)}) collective-permute-start(f32[128,128]{1,0:T(8,128)S(1)} %convert_multiply_fusion.own_ref.refs_8_.start_ref.refs_12_), channel_id=1, source_target_pairs={{64,0},{128,64},{192,128},{0,192},{65,1},{129,65},{193,129},{1,193... | collective-permute-start | bytes 196616 | tf_op jit(solution)/shard_map/ppermute | solution.py:29
  18.0 6.4 %collective-permute-start.12 = (f32[128,128]{1,0:T(8,128)S(1)}, f32[128,128]{1,0:T(8,128)S(1)}, u32[]{:S(2)}, u32[]{:S(2)}) collective-permute-start(f32[128,128]{1,0:T(8,128)S(1)} %convert_multiply_fusion.own_ref.refs_8_.start_ref.refs_12_), channel_id=1, source_target_pairs={{128,0},{192,64},{0,128},{64,192},{129,1},{193,65},{1,129},{65,193... | collective-permute-start | bytes 196616 | tf_op jit(solution)/shard_map/ppermute | solution.py:29
  19.4 12.2 %copy-start.1 = (f32[2,4096]{1,0:T(2,128)S(1)}, f32[2,4096]{1,0:T(2,128)}, u32[]{:S(2)}) copy-start(f32[2,4096]{1,0:T(2,128)} %sites_ref.3) | copy-start | bytes 98308
  19.4 9.0 %collective-permute-start.4 = (f32[128,128]{1,0:T(8,128)S(1)}, f32[128,128]{1,0:T(8,128)S(1)}, u32[]{:S(2)}, u32[]{:S(2)}) collective-permute-start(f32[128,128]{1,0:T(8,128)S(1)} %add_add_fusion.1.refs_0_), channel_id=1, source_target_pairs={{16,0},{32,16},{48,32},{0,48},{17,1},{33,17},{49,33},{1,49},{18,2}... | collective-permute-start | bytes 196616 | tf_op jit(solution)/shard_map/ppermute | solution.py:29
  22.0 6.6 %collective-permute-start.5 = (f32[128,128]{1,0:T(8,128)S(1)}, f32[128,128]{1,0:T(8,128)S(1)}, u32[]{:S(2)}, u32[]{:S(2)}) collective-permute-start(f32[128,128]{1,0:T(8,128)S(1)} %add_add_fusion.1.refs_0_), channel_id=1, source_target_pairs={{32,0},{48,16},{0,32},{16,48},{33,1},{49,17},{1,33},{17,49},{34,2}... | collective-permute-start | bytes 196616 | tf_op jit(solution)/shard_map/ppermute | solution.py:29
  22.5 8.5 %collective-permute-start.6 = (f32[128,128]{1,0:T(8,128)S(1)}, f32[128,128]{1,0:T(8,128)S(1)}, u32[]{:S(2)}, u32[]{:S(2)}) collective-permute-start(f32[128,128]{1,0:T(8,128)S(1)} %add_add_fusion.1.refs_0_), channel_id=1, source_target_pairs={{48,0},{0,16},{16,32},{32,48},{49,1},{1,17},{17,33},{33,49},{50,2}... | collective-permute-start | bytes 196616 | tf_op jit(solution)/shard_map/ppermute | solution.py:29
  23.1 11.2 %collective-permute-start.13 = (f32[128,128]{1,0:T(8,128)S(1)}, f32[128,128]{1,0:T(8,128)S(1)}, u32[]{:S(2)}, u32[]{:S(2)}) collective-permute-start(f32[128,128]{1,0:T(8,128)S(1)} %convert_multiply_fusion.own_ref.refs_8_.start_ref.refs_12_), channel_id=1, source_target_pairs={{192,0},{0,64},{64,128},{128,192},{193,1},{1,65},{65,129},{129,193... | collective-permute-start | bytes 196616 | tf_op jit(solution)/shard_map/ppermute | solution.py:29
  24.4 10.0 %collective-permute-start.7 = (f32[128,128]{1,0:T(8,128)S(1)}, f32[128,128]{1,0:T(8,128)S(1)}, u32[]{:S(2)}, u32[]{:S(2)}) collective-permute-start(f32[128,128]{1,0:T(8,128)S(1)} %add_add_fusion.1.refs_0_), channel_id=1, source_target_pairs={{0,8},{8,0},{1,9},{9,1},{2,10},{10,2},{3,11},{11,3},{4,12},{12,4},... | collective-permute-start | bytes 196616 | tf_op jit(solution)/shard_map/ppermute | solution.py:44
  28.5 5.9 %collective-permute-start.8 = (f32[128,128]{1,0:T(8,128)S(1)}, f32[128,128]{1,0:T(8,128)S(1)}, u32[]{:S(2)}, u32[]{:S(2)}) collective-permute-start(f32[128,128]{1,0:T(8,128)S(1)} %collective-permute-done.4.refs_1_), channel_id=1, source_target_pairs={{0,8},{8,0},{1,9},{9,1},{2,10},{10,2},{3,11},{11,3},{4,12},{12,4},... | collective-permute-start | bytes 196616 | tf_op jit(solution)/shard_map/ppermute | solution.py:44
  28.6 5.8 %collective-permute-start.9 = (f32[128,128]{1,0:T(8,128)S(1)}, f32[128,128]{1,0:T(8,128)S(1)}, u32[]{:S(2)}, u32[]{:S(2)}) collective-permute-start(f32[128,128]{1,0:T(8,128)S(1)} %collective-permute-done.5.refs_2_), channel_id=1, source_target_pairs={{0,8},{8,0},{1,9},{9,1},{2,10},{10,2},{3,11},{11,3},{4,12},{12,4},... | collective-permute-start | bytes 196616 | tf_op jit(solution)/shard_map/ppermute | solution.py:44
  31.0 3.4 %collective-permute-start.10 = (f32[128,128]{1,0:T(8,128)S(1)}, f32[128,128]{1,0:T(8,128)S(1)}, u32[]{:S(2)}, u32[]{:S(2)}) collective-permute-start(f32[128,128]{1,0:T(8,128)S(1)} %collective-permute-done.6.refs_3_), channel_id=1, source_target_pairs={{0,8},{8,0},{1,9},{9,1},{2,10},{10,2},{3,11},{11,3},{4,12},{12,4},... | collective-permute-start | bytes 196616 | tf_op jit(solution)/shard_map/ppermute | solution.py:44
  34.4 8.8 %copy-start = (s32[128,128]{1,0:T(8,128)S(1)}, s32[128,128]{1,0:T(8,128)}, u32[]{:S(2)}) copy-start(s32[128,128]{1,0:T(8,128)} %mask_ref.1) | copy-start | bytes 196612
  35.5 5.1 %collective-permute-start.14 = (f32[136,128]{1,0:T(8,128)S(1)}, f32[136,128]{1,0:T(8,128)S(1)}, u32[]{:S(2)}, u32[]{:S(2)}) collective-permute-start(f32[136,128]{1,0:T(8,128)S(1)} %get-tuple-element.41.refs_9_), channel_id=1, source_target_pairs={{192,0},{0,64},{64,128},{128,192},{193,1},{1,65},{65,129},{129,193... | collective-permute-start | bytes 208904 | tf_op jit(solution)/shard_map/ppermute | solution.py:29
  36.8 6.3 %collective-permute-start.15 = (f32[136,128]{1,0:T(8,128)S(1)}, f32[136,128]{1,0:T(8,128)S(1)}, u32[]{:S(2)}, u32[]{:S(2)}) collective-permute-start(f32[136,128]{1,0:T(8,128)S(1)} %get-tuple-element.42.refs_10_), channel_id=1, source_target_pairs={{128,0},{192,64},{0,128},{64,192},{129,1},{193,65},{1,129},{65,193... | collective-permute-start | bytes 208904 | tf_op jit(solution)/shard_map/ppermute | solution.py:29
  39.4 3.7 %collective-permute-start.16 = (f32[136,128]{1,0:T(8,128)S(1)}, f32[136,128]{1,0:T(8,128)S(1)}, u32[]{:S(2)}, u32[]{:S(2)}) collective-permute-start(f32[136,128]{1,0:T(8,128)S(1)} %get-tuple-element.43.refs_11_), channel_id=1, source_target_pairs={{64,0},{128,64},{192,128},{0,192},{65,1},{129,65},{193,129},{1,193... | collective-permute-start | bytes 208904 | tf_op jit(solution)/shard_map/ppermute | solution.py:29
  43.2 3.2 %collective-permute-start.17 = (f32[136,128]{1,0:T(8,128)S(1)}, f32[136,128]{1,0:T(8,128)S(1)}, u32[]{:S(2)}, u32[]{:S(2)}) collective-permute-start(f32[136,128]{1,0:T(8,128)S(1)} %shard_map.90.own_ref.refs_16_.image_ref), channel_id=1, source_target_pairs={{0,1},{1,0},{2,3},{3,2},{4,5},{5,4},{6,7},{7,6},{8,9},{9,8},{10,11... | collective-permute-start | bytes 208904 | tf_op jit(solution)/shard_map/ppermute | solution.py:40
  46.8 9.4 %collective-permute-start.19 = (f32[136,128]{1,0:T(8,128)S(1)}, f32[136,128]{1,0:T(8,128)S(1)}, u32[]{:S(2)}, u32[]{:S(2)}) collective-permute-start(f32[136,128]{1,0:T(8,128)S(1)} %get-tuple-element.46), channel_id=1, source_target_pairs={{2,0},{4,2},{6,4},{0,6},{3,1},{5,3},{7,5},{1,7},{10,8},{12,10},{14... | collective-permute-start | bytes 208904 | tf_op jit(solution)/shard_map/ppermute | solution.py:29
  51.1 5.4 %collective-permute-start.20 = (f32[136,128]{1,0:T(8,128)S(1)}, f32[136,128]{1,0:T(8,128)S(1)}, u32[]{:S(2)}, u32[]{:S(2)}) collective-permute-start(f32[136,128]{1,0:T(8,128)S(1)} %get-tuple-element.47), channel_id=1, source_target_pairs={{6,0},{0,2},{2,4},{4,6},{7,1},{1,3},{3,5},{5,7},{14,8},{8,10},{10,... | collective-permute-start | bytes 208904 | tf_op jit(solution)/shard_map/ppermute | solution.py:29
  51.1 7.5 %collective-permute-start.18 = (f32[136,128]{1,0:T(8,128)S(1)}, f32[136,128]{1,0:T(8,128)S(1)}, u32[]{:S(2)}, u32[]{:S(2)}) collective-permute-start(f32[136,128]{1,0:T(8,128)S(1)} %get-tuple-element.45), channel_id=1, source_target_pairs={{4,0},{6,2},{0,4},{2,6},{5,1},{7,3},{1,5},{3,7},{12,8},{14,10},{8,... | collective-permute-start | bytes 208904 | tf_op jit(solution)/shard_map/ppermute | solution.py:29
  53.7 6.8 %collective-permute-start.28 = (f32[136,128]{1,0:T(8,128)S(1)}, f32[136,128]{1,0:T(8,128)S(1)}, u32[]{:S(2)}, u32[]{:S(2)}) collective-permute-start(f32[136,128]{1,0:T(8,128)S(1)} %shard_map.90.own_ref.refs_16_.image_ref), channel_id=1, source_target_pairs={{64,0},{128,64},{192,128},{0,192},{65,1},{129,65},{193,129},{1,193... | collective-permute-start | bytes 208904 | tf_op jit(solution)/shard_map/ppermute | solution.py:29
  55.4 5.5 %collective-permute-start.29 = (f32[136,128]{1,0:T(8,128)S(1)}, f32[136,128]{1,0:T(8,128)S(1)}, u32[]{:S(2)}, u32[]{:S(2)}) collective-permute-start(f32[136,128]{1,0:T(8,128)S(1)} %shard_map.90.own_ref.refs_16_.image_ref), channel_id=1, source_target_pairs={{128,0},{192,64},{0,128},{64,192},{129,1},{193,65},{1,129},{65,193... | collective-permute-start | bytes 208904 | tf_op jit(solution)/shard_map/ppermute | solution.py:29
  58.6 7.5 %collective-permute-start.21 = (f32[136,128]{1,0:T(8,128)S(1)}, f32[136,128]{1,0:T(8,128)S(1)}, u32[]{:S(2)}, u32[]{:S(2)}) collective-permute-start(f32[136,128]{1,0:T(8,128)S(1)} %add_add_fusion.refs_0_), channel_id=1, source_target_pairs={{16,0},{32,16},{48,32},{0,48},{17,1},{33,17},{49,33},{1,49},{18,2}... | collective-permute-start | bytes 208904 | tf_op jit(solution)/shard_map/ppermute | solution.py:29
  58.8 7.6 %collective-permute-start.22 = (f32[136,128]{1,0:T(8,128)S(1)}, f32[136,128]{1,0:T(8,128)S(1)}, u32[]{:S(2)}, u32[]{:S(2)}) collective-permute-start(f32[136,128]{1,0:T(8,128)S(1)} %add_add_fusion.refs_0_), channel_id=1, source_target_pairs={{32,0},{48,16},{0,32},{16,48},{33,1},{49,17},{1,33},{17,49},{34,2}... | collective-permute-start | bytes 208904 | tf_op jit(solution)/shard_map/ppermute | solution.py:29
  59.8 8.8 %collective-permute-start.23 = (f32[136,128]{1,0:T(8,128)S(1)}, f32[136,128]{1,0:T(8,128)S(1)}, u32[]{:S(2)}, u32[]{:S(2)}) collective-permute-start(f32[136,128]{1,0:T(8,128)S(1)} %add_add_fusion.refs_0_), channel_id=1, source_target_pairs={{48,0},{0,16},{16,32},{32,48},{49,1},{1,17},{17,33},{33,49},{50,2}... | collective-permute-start | bytes 208904 | tf_op jit(solution)/shard_map/ppermute | solution.py:29
  60.6 8.8 %collective-permute-start.30 = (f32[136,128]{1,0:T(8,128)S(1)}, f32[136,128]{1,0:T(8,128)S(1)}, u32[]{:S(2)}, u32[]{:S(2)}) collective-permute-start(f32[136,128]{1,0:T(8,128)S(1)} %shard_map.90.own_ref.refs_16_.image_ref), channel_id=1, source_target_pairs={{192,0},{0,64},{64,128},{128,192},{193,1},{1,65},{65,129},{129,193... | collective-permute-start | bytes 208904 | tf_op jit(solution)/shard_map/ppermute | solution.py:29
  61.0 8.4 %collective-permute-start.24 = (f32[136,128]{1,0:T(8,128)S(1)}, f32[136,128]{1,0:T(8,128)S(1)}, u32[]{:S(2)}, u32[]{:S(2)}) collective-permute-start(f32[136,128]{1,0:T(8,128)S(1)} %add_add_fusion.refs_0_), channel_id=1, source_target_pairs={{0,8},{8,0},{1,9},{9,1},{2,10},{10,2},{3,11},{11,3},{4,12},{12,4},... | collective-permute-start | bytes 208904 | tf_op jit(solution)/shard_map/ppermute | solution.py:44
  66.1 3.2 %collective-permute-start.25 = (f32[136,128]{1,0:T(8,128)S(1)}, f32[136,128]{1,0:T(8,128)S(1)}, u32[]{:S(2)}, u32[]{:S(2)}) collective-permute-start(f32[136,128]{1,0:T(8,128)S(1)} %collective-permute-done.21.refs_1_), channel_id=1, source_target_pairs={{0,8},{8,0},{1,9},{9,1},{2,10},{10,2},{3,11},{11,3},{4,12},{12,4},... | collective-permute-start | bytes 208904 | tf_op jit(solution)/shard_map/ppermute | solution.py:44
  66.4 3.1 %collective-permute-start.26 = (f32[136,128]{1,0:T(8,128)S(1)}, f32[136,128]{1,0:T(8,128)S(1)}, u32[]{:S(2)}, u32[]{:S(2)}) collective-permute-start(f32[136,128]{1,0:T(8,128)S(1)} %collective-permute-done.22.refs_2_), channel_id=1, source_target_pairs={{0,8},{8,0},{1,9},{9,1},{2,10},{10,2},{3,11},{11,3},{4,12},{12,4},... | collective-permute-start | bytes 208904 | tf_op jit(solution)/shard_map/ppermute | solution.py:44
  68.6 1.6 %collective-permute-start.27 = (f32[136,128]{1,0:T(8,128)S(1)}, f32[136,128]{1,0:T(8,128)S(1)}, u32[]{:S(2)}, u32[]{:S(2)}) collective-permute-start(f32[136,128]{1,0:T(8,128)S(1)} %collective-permute-done.23.refs_3_), channel_id=1, source_target_pairs={{0,8},{8,0},{1,9},{9,1},{2,10},{10,2},{3,11},{11,3},{4,12},{12,4},... | collective-permute-start | bytes 208904 | tf_op jit(solution)/shard_map/ppermute | solution.py:44
  72.1 10.3 %copy-start.2 = (f32[2,4096]{1,0:T(2,128)S(1)}, f32[2,4096]{1,0:T(2,128)}, u32[]{:S(2)}) copy-start(f32[2,4096]{1,0:T(2,128)} %tests_ref.1) | copy-start | bytes 98308
  72.1 10.3 %copy-start.3 = (s32[4096]{0:T(1024)S(1)}, s32[4096]{0:T(1024)}, u32[]{:S(2)}) copy-start(s32[4096]{0:T(1024)} %param.13) | copy-start | bytes 49156
  72.1 26.1 %all-to-all-start = ((f32[256,1,128]{2,1,0:T(1,128)}), f32[256,1,128]{2,1,0:T(1,128)S(1)}, u32[]{:S(2)}, u32[]{:S(2)}) async-start(f32[256,1,128]{2,1,0:T(1,128)} %get-tuple-element.48), calls=%async_computation | async-start | bytes 262144 | tf_op jit(solution)/shard_map/all_to_all | solution.py:300
  87.9 5.7 %collective-permute-start.31 = (f32[128,256]{1,0:T(8,128)S(1)}, f32[128,256]{1,0:T(8,128)S(1)}, u32[]{:S(2)}, u32[]{:S(2)}) collective-permute-start(f32[128,256]{1,0:T(8,128)S(1)} %get-tuple-element.57), channel_id=1, source_target_pairs={{192,0},{0,64},{64,128},{128,192},{193,1},{1,65},{65,129},{129,193... | collective-permute-start | bytes 393224 | tf_op jit(solution)/shard_map/ppermute | solution.py:29
  89.4 8.9 %collective-permute-start.32 = (f32[128,256]{1,0:T(8,128)S(1)}, f32[128,256]{1,0:T(8,128)S(1)}, u32[]{:S(2)}, u32[]{:S(2)}) collective-permute-start(f32[128,256]{1,0:T(8,128)S(1)} %get-tuple-element.58), channel_id=1, source_target_pairs={{128,0},{192,64},{0,128},{64,192},{129,1},{193,65},{1,129},{65,193... | collective-permute-start | bytes 393224 | tf_op jit(solution)/shard_map/ppermute | solution.py:29
  91.8 6.4 %collective-permute-start.33 = (f32[128,256]{1,0:T(8,128)S(1)}, f32[128,256]{1,0:T(8,128)S(1)}, u32[]{:S(2)}, u32[]{:S(2)}) collective-permute-start(f32[128,256]{1,0:T(8,128)S(1)} %get-tuple-element.59), channel_id=1, source_target_pairs={{64,0},{128,64},{192,128},{0,192},{65,1},{129,65},{193,129},{1,193... | collective-permute-start | bytes 393224 | tf_op jit(solution)/shard_map/ppermute | solution.py:29

commit v3 on v2

--- a/solution.py
+++ b/solution.py
@@ -24,24 +24,21 @@
 VMEM = pl.BlockSpec(memory_space=pltpu.VMEM)
 
 
-def ahead(block, axis, shift):
-    size = lax.axis_size(axis)
-    return lax.ppermute(block, axis, [((i + shift) % size, i) for i in range(size)])
-
-
-def gathered(block, axis, order):
-    held = {0: block}
-    for shift in order:
-        held[shift] = ahead(block, axis, shift)
-    return [held[shift] for shift in range(len(held))]
+def paired(block, axis, flip):
+    return lax.ppermute(block, axis, [(i, i ^ flip) for i in range(lax.axis_size(axis))])
+
+
+def everyones(block, axis):
+    second, third, first = [paired(block, axis, flip) for flip in (2, 3, 1)]
+    return [block, first, second, third]
 
 
 def neighbours(block):
-    return lax.ppermute(block, "tm_1", [(0, 1), (1, 0)])
+    return paired(block, "tm_1", 1)
 
 
 def swapped(block):
-    return lax.ppermute(block, "loc_2", [(0, 1), (1, 0)])
+    return paired(block, "loc_2", 1)
 
 
 def halves(value):
@@ -86,12 +83,12 @@
 
 def row_places():
     y, x, c = (lax.axis_index(axis) for axis in LOC)
-    return [((((y + s) & 3) * 4) + x) * 2 + c for s in range(4)]
+    return [((y ^ s) * 4 + x) * 2 + c for s in range(4)]
 
 
 def column_places():
     y, x, c = (lax.axis_index(axis) for axis in LOC)
-    return [(y * 4 + ((x + s) & 3)) * 2 + (c ^ other) for other in range(2) for s in range(4)]
+    return [(y * 4 + (x ^ s)) * 2 + (c ^ other) for other in range(2) for s in range(4)]
 
 
 def fill(points_ref, at_ref, length, high_ref, low_ref):
@@ -110,11 +107,12 @@
 
 def time_kernel(stamps_ref, noise_ref, high_ref, low_ref, noise_out_ref, *, length):
     noise_out_ref[...] = noise_ref[...]
-    own = 2 * lax.axis_index("tm_0") + lax.axis_index("tm_1")
+    place, parity = lax.axis_index("tm_0"), lax.axis_index("tm_1")
+    own = 2 * place + parity
     columns = upright(jnp.concatenate([stamps_ref[pl.ds(t, 1), :] for t in (own, own ^ 1)], 0))
     for s in range(2):
         for t in range(4):
-            line = stamps_ref[pl.ds((own + 2 * t) & 7, 1), :]
+            line = stamps_ref[pl.ds(2 * (place ^ t) + parity, 1), :]
             apart = jnp.abs(columns[:, s : s + 1] - line)
             high, low = halves(matern(apart * (root_three / length)))
             high_ref[s * TILE : (s + 1) * TILE, t * TILE : (t + 1) * TILE] = high
@@ -300,7 +298,7 @@
         return lax.all_to_all(copies, axes, split_axis=0, concat_axis=0, tiled=True)
 
     start = observed_mask.astype(f32) * observed
-    start_rows = gathered(start, "loc_0", (2, 1, 3))
+    start_rows = everyones(start, "loc_0")
 
     time_high, time_low, noise = call(
         functools.partial(time_kernel, length=time_reach / times),
@@ -327,15 +325,15 @@
             time_low,
             flops=6 * TILE * 8 * TILE * TILE,
         )
-        parts = [parts[0]] + [ahead(parts[k], "tm_0", -k) for k in (2, 3, 1)]
-        return (parts[0] + parts[1]) + (parts[2] + parts[3])
+        others = [paired(parts[k], "tm_0", k) for k in (2, 3, 1)]
+        return (parts[0] + others[0]) + (others[1] + others[2])
 
     def columns(block):
-        held = gathered(block, "loc_1", (2, 1, 3))
+        held = everyones(block, "loc_1")
         return held + [swapped(piece) for piece in held]
 
     def to_owners(parts):
-        return [parts[0]] + [ahead(parts[s], "loc_0", -s) for s in (1, 2, 3)]
+        return [parts[0]] + [paired(parts[s], "loc_0", s) for s in (2, 3, 1)]
 
     other = neighbours(start)
     start_fold = folded(start, other)
@@ -372,7 +370,7 @@
         flops=10 * TILE * TILE,
     )
     other = neighbours(image)
-    image_rows = gathered(image, "loc_0", (2, 1, 3))
+    image_rows = everyones(image, "loc_0")
     image_fold = folded(image, other)
     start_fields = call(
         field_kernel,

time: 99.7 us -> 101 us (1.013)
  waiting for transfers between devices: 15.4 us -> 17.6 us
  starting transfers between devices: 68.2 us -> 66.8 us
    ppermute x34, waiting for transfers between devices: 15.4 us -> 17.6 us  [paired(): lax.ppermute(block, axis, [(i, i ^ flip) for i in range(lax.axis_size(axi...]
    ppermute x34, starting transfers between devices: 58 us -> 56.3 us  [paired(): lax.ppermute(block, axis, [(i, i ^ flip) for i in range(lax.axis_size(axi...]
  transfers between devices with their start and end apart: 35 -> 35, of which waited for: 11 -> 8; matrix products, arithmetic and copies ran while one was open for 0% -> 0% of each run, Pallas kernels for 9% -> 9%
where the time goes in v3:
time: 101 us; the launch traced here: 100 us
  starting transfers between devices  66.8 us (66%)
  waiting for transfers between devices  17.6 us (17%)
  Pallas kernels  13.4 us (13%)
    ppermute x34, starting transfers between devices, paired(): lax.ppermute(block, axis, [(i, i ^ flip) for i in range(lax.axis_size(axi...  56.3 us
    ppermute x34, waiting for transfers between devices, paired(): lax.ppermute(block, axis, [(i, i ^ flip) for i in range(lax.axis_size(axi...  17.6 us
    pallas_call x11, Pallas kernels, call(): pl.pallas_call(kernel, out_shape=shapes, in_specs=[VMEM] * len(args), out...  13.4 us
    all_to_all x1, starting transfers between devices, exchanged(): return lax.all_to_all(copies, axes, split_axis=0, concat_axis=0, tiled=True)  10.5 us
  transfers between devices with their start and end apart: 35, of which 8 were waited for; matrix products, arithmetic and copies ran while one was open for 0% of the time, Pallas kernels for 9%

profile of v3, /device:TPU:1, one launch (start us, length us, event | category | flops | bytes accessed | tf_op | source)
XLA Modules:
  0.0 100.3 jit_solution(13203060989792411120)
XLA Ops:
  0.6 0.9 convert_multiply_fusion.own_ref.refs_8_.start_ref.refs_12_
  1.5 2.5 %collective-permute-start = (f32[128,128]{1,0:T(8,128)S(1)}, f32[128,128]{1,0:T(8,128)S(1)}, u32[]{:S(2)}, u32[]{:S(2)}) collective-permute-start(f32[128,128]{1,0:T(8,128)S(1)} %convert_multiply_fusion.own_ref.refs_8_.start_ref.refs_12_), channel_id=1, source_target_pairs={{0,1},{1,0},{2,3},{3,2},{4,5},{5,4},{6,7},{7,6},{8,9},{9,8},{10,11... | collective-permute-start | bytes 196616 | tf_op jit(solution)/shard_map/ppermute | solution.py:28
  4.1 0.7 copy-done.5
  5.1 0.6 collective-permute-done.other_ref
  5.7 0.4 shard_map.87
  6.1 5.9 %collective-permute-start.2 = (f32[128,128]{1,0:T(8,128)S(1)}, f32[128,128]{1,0:T(8,128)S(1)}, u32[]{:S(2)}, u32[]{:S(2)}) collective-permute-start(f32[128,128]{1,0:T(8,128)S(1)} %get-tuple-element.35), channel_id=1, source_target_pairs={{0,6},{2,4},{4,2},{6,0},{1,7},{3,5},{5,3},{7,1},{8,14},{10,12},{12... | collective-permute-start | bytes 196616 | tf_op jit(solution)/shard_map/ppermute | solution.py:28
  12.0 1.2 %collective-permute-start.3 = (f32[128,128]{1,0:T(8,128)S(1)}, f32[128,128]{1,0:T(8,128)S(1)}, u32[]{:S(2)}, u32[]{:S(2)}) collective-permute-start(f32[128,128]{1,0:T(8,128)S(1)} %get-tuple-element.36), channel_id=1, source_target_pairs={{0,2},{2,0},{4,6},{6,4},{1,3},{3,1},{5,7},{7,5},{8,10},{10,8},{12,... | collective-permute-start | bytes 196616 | tf_op jit(solution)/shard_map/ppermute | solution.py:28
  13.2 1.0 %collective-permute-start.1 = (f32[128,128]{1,0:T(8,128)S(1)}, f32[128,128]{1,0:T(8,128)S(1)}, u32[]{:S(2)}, u32[]{:S(2)}) collective-permute-start(f32[128,128]{1,0:T(8,128)S(1)} %get-tuple-element.34), channel_id=1, source_target_pairs={{0,4},{2,6},{4,0},{6,2},{1,5},{3,7},{5,1},{7,3},{8,12},{10,14},{12... | collective-permute-start | bytes 196616 | tf_op jit(solution)/shard_map/ppermute | solution.py:28
  14.2 1.3 %collective-permute-start.11 = (f32[128,128]{1,0:T(8,128)S(1)}, f32[128,128]{1,0:T(8,128)S(1)}, u32[]{:S(2)}, u32[]{:S(2)}) collective-permute-start(f32[128,128]{1,0:T(8,128)S(1)} %convert_multiply_fusion.own_ref.refs_8_.start_ref.refs_12_), channel_id=1, source_target_pairs={{0,64},{64,0},{128,192},{192,128},{1,65},{65,1},{129,193},{193,129... | collective-permute-start | bytes 196616 | tf_op jit(solution)/shard_map/ppermute | solution.py:28
  15.5 2.6 %collective-permute-start.12 = (f32[128,128]{1,0:T(8,128)S(1)}, f32[128,128]{1,0:T(8,128)S(1)}, u32[]{:S(2)}, u32[]{:S(2)}) collective-permute-start(f32[128,128]{1,0:T(8,128)S(1)} %convert_multiply_fusion.own_ref.refs_8_.start_ref.refs_12_), channel_id=1, source_target_pairs={{0,128},{64,192},{128,0},{192,64},{1,129},{65,193},{129,1},{193,65... | collective-permute-start | bytes 196616 | tf_op jit(solution)/shard_map/ppermute | solution.py:28
  18.1 2.7 %collective-permute-done.1 = f32[128,128]{1,0:T(8,128)S(1)} collective-permute-done((f32[128,128]{1,0:T(8,128)S(1)}, f32[128,128]{1,0:T(8,128)S(1)}, u32[]{:S(2)}, u32[]{:S(2)}) %collective-permute-start.1) | collective-permute-done | bytes 65568 | tf_op jit(solution)/shard_map/ppermute | solution.py:28
  20.9 1.3 %collective-permute-start.4 = (f32[128,128]{1,0:T(8,128)S(1)}, f32[128,128]{1,0:T(8,128)S(1)}, u32[]{:S(2)}, u32[]{:S(2)}) collective-permute-start(f32[128,128]{1,0:T(8,128)S(1)} %add_add_fusion.1.refs_0_), channel_id=1, source_target_pairs={{0,16},{16,0},{32,48},{48,32},{1,17},{17,1},{33,49},{49,33},{2,18}... | collective-permute-start | bytes 196616 | tf_op jit(solution)/shard_map/ppermute | solution.py:28
  22.2 2.4 %collective-permute-start.5 = (f32[128,128]{1,0:T(8,128)S(1)}, f32[128,128]{1,0:T(8,128)S(1)}, u32[]{:S(2)}, u32[]{:S(2)}) collective-permute-start(f32[128,128]{1,0:T(8,128)S(1)} %add_add_fusion.1.refs_0_), channel_id=1, source_target_pairs={{0,32},{16,48},{32,0},{48,16},{1,33},{17,49},{33,1},{49,17},{2,34}... | collective-permute-start | bytes 196616 | tf_op jit(solution)/shard_map/ppermute | solution.py:28
  24.8 2.7 %collective-permute-start.13 = (f32[128,128]{1,0:T(8,128)S(1)}, f32[128,128]{1,0:T(8,128)S(1)}, u32[]{:S(2)}, u32[]{:S(2)}) collective-permute-start(f32[128,128]{1,0:T(8,128)S(1)} %convert_multiply_fusion.own_ref.refs_8_.start_ref.refs_12_), channel_id=1, source_target_pairs={{0,192},{64,128},{128,64},{192,0},{1,193},{65,129},{129,65},{193,1... | collective-permute-start | bytes 196616 | tf_op jit(solution)/shard_map/ppermute | solution.py:28
  27.6 4.3 %collective-permute-start.7 = (f32[128,128]{1,0:T(8,128)S(1)}, f32[128,128]{1,0:T(8,128)S(1)}, u32[]{:S(2)}, u32[]{:S(2)}) collective-permute-start(f32[128,128]{1,0:T(8,128)S(1)} %add_add_fusion.1.refs_0_), channel_id=1, source_target_pairs={{0,8},{8,0},{1,9},{9,1},{2,10},{10,2},{3,11},{11,3},{4,12},{12,4},... | collective-permute-start | bytes 196616 | tf_op jit(solution)/shard_map/ppermute | solution.py:28
  32.0 0.4 collective-permute-start.9
  32.4 1.5 %collective-permute-start.10 = (f32[128,128]{1,0:T(8,128)S(1)}, f32[128,128]{1,0:T(8,128)S(1)}, u32[]{:S(2)}, u32[]{:S(2)}) collective-permute-start(f32[128,128]{1,0:T(8,128)S(1)} %collective-permute-done.6.refs_3_), channel_id=1, source_target_pairs={{0,8},{8,0},{1,9},{9,1},{2,10},{10,2},{3,11},{11,3},{4,12},{12,4},... | collective-permute-start | bytes 196616 | tf_op jit(solution)/shard_map/ppermute | solution.py:28
  33.9 2.7 %shard_map.88 = (bf16[512,1024]{1,0:T(8,128)(2,1)S(1)}, bf16[512,1024]{1,0:T(8,128)(2,1)S(1)}) custom-call(f32[2,4096]{1,0:T(2,128)S(1)} %copy-done.1), custom_call_target="tpu_custom_call" | custom-call | flops 209715200 | bytes 2129920 | tf_op jit(solution)/shard_map/pallas_call | solution.py:56
  36.7 1.0 %shard_map.89 = (f32[136,128]{1,0:T(8,128)S(1)}, f32[136,128]{1,0:T(8,128)S(1)}, f32[136,128]{1,0:T(8,128)S(1)}, f32[136,128]{1,0:T(8,128)S(1)}) custom-call(f32[128,128]{1,0:T(8,128)S(1)} %add_add_fusion.1.refs_0_, f32[128,128]{1,0:T(8,128)S(1)} %collective-permute-done.4.refs_1_, f32[128,128]{1,0:T(8,128)S(1)} %collective-permute-done.5.refs_2_, ...), custom_call_target="tpu_custom_call" | custom-call | flops 402653184 | bytes 3162624 | tf_op jit(solution)/shard_map/pallas_call | solution.py:56
  37.7 3.0 %collective-permute-start.14 = (f32[136,128]{1,0:T(8,128)S(1)}, f32[136,128]{1,0:T(8,128)S(1)}, u32[]{:S(2)}, u32[]{:S(2)}) collective-permute-start(f32[136,128]{1,0:T(8,128)S(1)} %get-tuple-element.41.refs_10_), channel_id=1, source_target_pairs={{0,128},{64,192},{128,0},{192,64},{1,129},{65,193},{129,1},{193,65... | collective-permute-start | bytes 208904 | tf_op jit(solution)/shard_map/ppermute | solution.py:28
  40.7 0.8 collective-permute-start.15
  41.5 1.5 %collective-permute-done.14.b = f32[136,128]{1,0:T(8,128)S(1)} collective-permute-done((f32[136,128]{1,0:T(8,128)S(1)}, f32[136,128]{1,0:T(8,128)S(1)}, u32[]{:S(2)}, u32[]{:S(2)}) %collective-permute-start.14) | collective-permute-done | bytes 69664 | tf_op jit(solution)/shard_map/ppermute | solution.py:28
  43.0 2.1 %collective-permute-done.15.c = f32[136,128]{1,0:T(8,128)S(1)} collective-permute-done((f32[136,128]{1,0:T(8,128)S(1)}, f32[136,128]{1,0:T(8,128)S(1)}, u32[]{:S(2)}, u32[]{:S(2)}) %collective-permute-start.15) | collective-permute-done | bytes 69664 | tf_op jit(solution)/shard_map/ppermute | solution.py:28
  45.1 0.7 collective-permute-start.17
  45.8 2.8 %collective-permute-done.17.other_ref = f32[136,128]{1,0:T(8,128)S(1)} collective-permute-done((f32[136,128]{1,0:T(8,128)S(1)}, f32[136,128]{1,0:T(8,128)S(1)}, u32[]{:S(2)}, u32[]{:S(2)}) %collective-permute-start.17) | collective-permute-done | bytes 69664 | tf_op jit(solution)/shard_map/ppermute | solution.py:28
  48.6 0.4 shard_map.91
  48.9 0.7 collective-permute-start.19
  49.6 0.5 collective-permute-start.20
  50.1 4.5 %collective-permute-start.18 = (f32[136,128]{1,0:T(8,128)S(1)}, f32[136,128]{1,0:T(8,128)S(1)}, u32[]{:S(2)}, u32[]{:S(2)}) collective-permute-start(f32[136,128]{1,0:T(8,128)S(1)} %get-tuple-element.45), channel_id=1, source_target_pairs={{0,4},{2,6},{4,0},{6,2},{1,5},{3,7},{5,1},{7,3},{8,12},{10,14},{12... | collective-permute-start | bytes 208904 | tf_op jit(solution)/shard_map/ppermute | solution.py:28
  54.7 1.1 %collective-permute-start.28 = (f32[136,128]{1,0:T(8,128)S(1)}, f32[136,128]{1,0:T(8,128)S(1)}, u32[]{:S(2)}, u32[]{:S(2)}) collective-permute-start(f32[136,128]{1,0:T(8,128)S(1)} %shard_map.90.own_ref.refs_16_.image_ref), channel_id=1, source_target_pairs={{0,64},{64,0},{128,192},{192,128},{1,65},{65,1},{129,193},{193,129... | collective-permute-start | bytes 208904 | tf_op jit(solution)/shard_map/ppermute | solution.py:28
  55.8 2.6 %collective-permute-start.29 = (f32[136,128]{1,0:T(8,128)S(1)}, f32[136,128]{1,0:T(8,128)S(1)}, u32[]{:S(2)}, u32[]{:S(2)}) collective-permute-start(f32[136,128]{1,0:T(8,128)S(1)} %shard_map.90.own_ref.refs_16_.image_ref), channel_id=1, source_target_pairs={{0,128},{64,192},{128,0},{192,64},{1,129},{65,193},{129,1},{193,65... | collective-permute-start | bytes 208904 | tf_op jit(solution)/shard_map/ppermute | solution.py:28
  58.6 1.4 %collective-permute-start.22 = (f32[136,128]{1,0:T(8,128)S(1)}, f32[136,128]{1,0:T(8,128)S(1)}, u32[]{:S(2)}, u32[]{:S(2)}) collective-permute-start(f32[136,128]{1,0:T(8,128)S(1)} %add_add_fusion.refs_0_), channel_id=1, source_target_pairs={{0,32},{16,48},{32,0},{48,16},{1,33},{17,49},{33,1},{49,17},{2,34}... | collective-permute-start | bytes 208904 | tf_op jit(solution)/shard_map/ppermute | solution.py:28
  59.9 2.5 %collective-permute-start.23 = (f32[136,128]{1,0:T(8,128)S(1)}, f32[136,128]{1,0:T(8,128)S(1)}, u32[]{:S(2)}, u32[]{:S(2)}) collective-permute-start(f32[136,128]{1,0:T(8,128)S(1)} %add_add_fusion.refs_0_), channel_id=1, source_target_pairs={{0,48},{16,32},{32,16},{48,0},{1,49},{17,33},{33,17},{49,1},{2,50}... | collective-permute-start | bytes 208904 | tf_op jit(solution)/shard_map/ppermute | solution.py:28
  62.4 2.1 %collective-permute-start.30 = (f32[136,128]{1,0:T(8,128)S(1)}, f32[136,128]{1,0:T(8,128)S(1)}, u32[]{:S(2)}, u32[]{:S(2)}) collective-permute-start(f32[136,128]{1,0:T(8,128)S(1)} %shard_map.90.own_ref.refs_16_.image_ref), channel_id=1, source_target_pairs={{0,192},{64,128},{128,64},{192,0},{1,193},{65,129},{129,65},{193,1... | collective-permute-start | bytes 208904 | tf_op jit(solution)/shard_map/ppermute | solution.py:28
  64.5 3.5 %collective-permute-start.24 = (f32[136,128]{1,0:T(8,128)S(1)}, f32[136,128]{1,0:T(8,128)S(1)}, u32[]{:S(2)}, u32[]{:S(2)}) collective-permute-start(f32[136,128]{1,0:T(8,128)S(1)} %add_add_fusion.refs_0_), channel_id=1, source_target_pairs={{0,8},{8,0},{1,9},{9,1},{2,10},{10,2},{3,11},{11,3},{4,12},{12,4},... | collective-permute-start | bytes 208904 | tf_op jit(solution)/shard_map/ppermute | solution.py:28
  68.1 0.4 collective-permute-start.26
  68.6 0.9 collective-permute-start.27
  69.5 0.9 collective-permute-done.27.refs_7_
  70.4 1.9 %shard_map.92 = (f32[256,1,128]{2,1,0:T(1,128)}, f32[1,128]{1,0:T(1,128)S(1)}) custom-call(f32[136,128]{1,0:T(8,128)S(1)} %add_add_fusion.refs_0_, f32[136,128]{1,0:T(8,128)S(1)} %collective-permute-done.21.refs_1_, f32[136,128]{1,0:T(8,128)S(1)} %collective-permute-done.22.refs_2_, f32[136,128]{1,0:T(8,128)S(1)} %collective-permute-done.23.refs_3_, ...), custom_call_target="tpu_custom_call" | custom-call | flops 402653184 | bytes 3605504 | tf_op jit(solution)/shard_map/pallas_call | solution.py:56
  72.3 10.5 %all-to-all-start = ((f32[256,1,128]{2,1,0:T(1,128)}), f32[256,1,128]{2,1,0:T(1,128)S(1)}, u32[]{:S(2)}, u32[]{:S(2)}) async-start(f32[256,1,128]{2,1,0:T(1,128)} %get-tuple-element.48), calls=%async_computation | async-start | bytes 262144 | tf_op jit(solution)/shard_map/all_to_all | solution.py:298
  82.7 3.5 %shard_map.93 = (bf16[512,1024]{1,0:T(8,128)(2,1)S(1)}, bf16[512,1024]{1,0:T(8,128)(2,1)S(1)}) custom-call(f32[2,4096]{1,0:T(2,128)S(1)} %copy-done.1, f32[2,4096]{1,0:T(2,128)S(1)} %copy-done.2, s32[32,128]{1,0:T(8,128)S(1)} %bitcast.3), custom_call_target="tpu_custom_call" | custom-call | flops 314572800 | bytes 2179072 | tf_op jit(solution)/shard_map/pallas_call | solution.py:56
  86.3 1.0 %shard_map.94 = (f32[128,128]{1,0:T(8,128)S(1)}, f32[128,128]{1,0:T(8,128)S(1)}, f32[128,128]{1,0:T(8,128)S(1)}, f32[128,128]{1,0:T(8,128)S(1)}) custom-call(f32[128,128]{1,0:T(8,128)S(1)} %add_add_fusion.1.refs_0_, f32[128,128]{1,0:T(8,128)S(1)} %collective-permute-done.4.refs_1_, f32[128,128]{1,0:T(8,128)S(1)} %collective-permute-done.5.refs_2_, ...), custom_call_target="tpu_custom_call" | custom-call | flops 402653184 | bytes 2883584 | tf_op jit(solution)/shard_map/pallas_call | solution.py:56
  87.3 1.0 %shard_map.95 = (f32[128,256]{1,0:T(8,128)S(1)}, f32[128,256]{1,0:T(8,128)S(1)}, f32[128,256]{1,0:T(8,128)S(1)}, f32[128,256]{1,0:T(8,128)S(1)}) custom-call(f32[136,128]{1,0:T(8,128)S(1)} %add_add_fusion.refs_0_, f32[136,128]{1,0:T(8,128)S(1)} %collective-permute-done.21.refs_1_, f32[136,128]{1,0:T(8,128)S(1)} %collective-permute-done.22.refs_2_, ...), custom_call_target="tpu_custom_call" | custom-call | flops 402653184 | bytes 3440640 | tf_op jit(solution)/shard_map/pallas_call | solution.py:56
  88.3 3.0 %collective-permute-start.31 = (f32[128,256]{1,0:T(8,128)S(1)}, f32[128,256]{1,0:T(8,128)S(1)}, u32[]{:S(2)}, u32[]{:S(2)}) collective-permute-start(f32[128,256]{1,0:T(8,128)S(1)} %get-tuple-element.57), channel_id=1, source_target_pairs={{0,128},{64,192},{128,0},{192,64},{1,129},{65,193},{129,1},{193,65... | collective-permute-start | bytes 393224 | tf_op jit(solution)/shard_map/ppermute | solution.py:28
  91.3 0.9 collective-permute-start.32
  92.1 2.1 %collective-permute-done.31.refs_1_ = f32[128,256]{1,0:T(8,128)S(1)} collective-permute-done((f32[128,256]{1,0:T(8,128)S(1)}, f32[128,256]{1,0:T(8,128)S(1)}, u32[]{:S(2)}, u32[]{:S(2)}) %collective-permute-start.31) | collective-permute-done | bytes 131104 | tf_op jit(solution)/shard_map/ppermute | solution.py:28
  94.3 4.8 %collective-permute-done.32.refs_2_ = f32[128,256]{1,0:T(8,128)S(1)} collective-permute-done((f32[128,256]{1,0:T(8,128)S(1)}, f32[128,256]{1,0:T(8,128)S(1)}, u32[]{:S(2)}, u32[]{:S(2)}) %collective-permute-start.32) | collective-permute-done | bytes 131104 | tf_op jit(solution)/shard_map/ppermute | solution.py:28
  99.1 1.2 %shard_map.96 = (f32[128,128]{1,0:T(8,128)}, f32[128,128]{1,0:T(8,128)}) custom-call(f32[256,1,128]{2,1,0:T(1,128)S(1)} %all-to-all-done.sums_ref, f32[1,128]{1,0:T(1,128)S(1)} %get-tuple-element.49.known_ref, f32[128,128]{1,0:T(8,128)S(1)} %convert_multiply_fusion.own_ref.refs_8_.start_ref.refs_12_, f32[136,128]{1,0:T(8,128)S(1)} %shard_map.90.own_ref.refs_16_.image_ref, ...), custom_call_target="tpu_custom_call" | custom-call | flops 327680 | bytes 922112 | tf_op jit(solution)/shard_map/pallas_call | solution.py:56
  (48 shorter events, 1.0 us)
Async XLA Ops:
  0.6 3.4 %copy-start.4 = (f32[1024]{0:T(1024)S(1)}, f32[1024]{0:T(1024)}, u32[]{:S(2)}) copy-start(f32[1024]{0:T(1024)} %param.10) | copy-start | bytes 12292
  1.5 4.2 %collective-permute-start = (f32[128,128]{1,0:T(8,128)S(1)}, f32[128,128]{1,0:T(8,128)S(1)}, u32[]{:S(2)}, u32[]{:S(2)}) collective-permute-start(f32[128,128]{1,0:T(8,128)S(1)} %convert_multiply_fusion.own_ref.refs_8_.start_ref.refs_12_), channel_id=1, source_target_pairs={{0,1},{1,0},{2,3},{3,2},{4,5},{5,4},{6,7},{7,6},{8,9},{9,8},{10,11... | collective-permute-start | bytes 196616 | tf_op jit(solution)/shard_map/ppermute | solution.py:28
  4.1 0.7 copy-start.5
  6.1 12.0 %collective-permute-start.2 = (f32[128,128]{1,0:T(8,128)S(1)}, f32[128,128]{1,0:T(8,128)S(1)}, u32[]{:S(2)}, u32[]{:S(2)}) collective-permute-start(f32[128,128]{1,0:T(8,128)S(1)} %get-tuple-element.35), channel_id=1, source_target_pairs={{0,6},{2,4},{4,2},{6,0},{1,7},{3,5},{5,3},{7,1},{8,14},{10,12},{12... | collective-permute-start | bytes 196616 | tf_op jit(solution)/shard_map/ppermute | solution.py:28
  12.0 6.1 %collective-permute-start.3 = (f32[128,128]{1,0:T(8,128)S(1)}, f32[128,128]{1,0:T(8,128)S(1)}, u32[]{:S(2)}, u32[]{:S(2)}) collective-permute-start(f32[128,128]{1,0:T(8,128)S(1)} %get-tuple-element.36), channel_id=1, source_target_pairs={{0,2},{2,0},{4,6},{6,4},{1,3},{3,1},{5,7},{7,5},{8,10},{10,8},{12,... | collective-permute-start | bytes 196616 | tf_op jit(solution)/shard_map/ppermute | solution.py:28
  13.2 7.7 %collective-permute-start.1 = (f32[128,128]{1,0:T(8,128)S(1)}, f32[128,128]{1,0:T(8,128)S(1)}, u32[]{:S(2)}, u32[]{:S(2)}) collective-permute-start(f32[128,128]{1,0:T(8,128)S(1)} %get-tuple-element.34), channel_id=1, source_target_pairs={{0,4},{2,6},{4,0},{6,2},{1,5},{3,7},{5,1},{7,3},{8,12},{10,14},{12... | collective-permute-start | bytes 196616 | tf_op jit(solution)/shard_map/ppermute | solution.py:28
  14.2 10.6 %collective-permute-start.11 = (f32[128,128]{1,0:T(8,128)S(1)}, f32[128,128]{1,0:T(8,128)S(1)}, u32[]{:S(2)}, u32[]{:S(2)}) collective-permute-start(f32[128,128]{1,0:T(8,128)S(1)} %convert_multiply_fusion.own_ref.refs_8_.start_ref.refs_12_), channel_id=1, source_target_pairs={{0,64},{64,0},{128,192},{192,128},{1,65},{65,1},{129,193},{193,129... | collective-permute-start | bytes 196616 | tf_op jit(solution)/shard_map/ppermute | solution.py:28
  15.5 12.1 %collective-permute-start.12 = (f32[128,128]{1,0:T(8,128)S(1)}, f32[128,128]{1,0:T(8,128)S(1)}, u32[]{:S(2)}, u32[]{:S(2)}) collective-permute-start(f32[128,128]{1,0:T(8,128)S(1)} %convert_multiply_fusion.own_ref.refs_8_.start_ref.refs_12_), channel_id=1, source_target_pairs={{0,128},{64,192},{128,0},{192,64},{1,129},{65,193},{129,1},{193,65... | collective-permute-start | bytes 196616 | tf_op jit(solution)/shard_map/ppermute | solution.py:28
  20.9 13.0 %copy-start.1 = (f32[2,4096]{1,0:T(2,128)S(1)}, f32[2,4096]{1,0:T(2,128)}, u32[]{:S(2)}) copy-start(f32[2,4096]{1,0:T(2,128)} %sites_ref.3) | copy-start | bytes 98308
  20.9 11.0 %collective-permute-start.4 = (f32[128,128]{1,0:T(8,128)S(1)}, f32[128,128]{1,0:T(8,128)S(1)}, u32[]{:S(2)}, u32[]{:S(2)}) collective-permute-start(f32[128,128]{1,0:T(8,128)S(1)} %add_add_fusion.1.refs_0_), channel_id=1, source_target_pairs={{0,16},{16,0},{32,48},{48,32},{1,17},{17,1},{33,49},{49,33},{2,18}... | collective-permute-start | bytes 196616 | tf_op jit(solution)/shard_map/ppermute | solution.py:28
  22.2 9.8 %collective-permute-start.5 = (f32[128,128]{1,0:T(8,128)S(1)}, f32[128,128]{1,0:T(8,128)S(1)}, u32[]{:S(2)}, u32[]{:S(2)}) collective-permute-start(f32[128,128]{1,0:T(8,128)S(1)} %add_add_fusion.1.refs_0_), channel_id=1, source_target_pairs={{0,32},{16,48},{32,0},{48,16},{1,33},{17,49},{33,1},{49,17},{2,34}... | collective-permute-start | bytes 196616 | tf_op jit(solution)/shard_map/ppermute | solution.py:28
  24.6 7.8 %collective-permute-start.6 = (f32[128,128]{1,0:T(8,128)S(1)}, f32[128,128]{1,0:T(8,128)S(1)}, u32[]{:S(2)}, u32[]{:S(2)}) collective-permute-start(f32[128,128]{1,0:T(8,128)S(1)} %add_add_fusion.1.refs_0_), channel_id=1, source_target_pairs={{0,48},{16,32},{32,16},{48,0},{1,49},{17,33},{33,17},{49,1},{2,50}... | collective-permute-start | bytes 196616 | tf_op jit(solution)/shard_map/ppermute | solution.py:28
  24.8 11.8 %collective-permute-start.13 = (f32[128,128]{1,0:T(8,128)S(1)}, f32[128,128]{1,0:T(8,128)S(1)}, u32[]{:S(2)}, u32[]{:S(2)}) collective-permute-start(f32[128,128]{1,0:T(8,128)S(1)} %convert_multiply_fusion.own_ref.refs_8_.start_ref.refs_12_), channel_id=1, source_target_pairs={{0,192},{64,128},{128,64},{192,0},{1,193},{65,129},{129,65},{193,1... | collective-permute-start | bytes 196616 | tf_op jit(solution)/shard_map/ppermute | solution.py:28
  27.6 9.0 %collective-permute-start.7 = (f32[128,128]{1,0:T(8,128)S(1)}, f32[128,128]{1,0:T(8,128)S(1)}, u32[]{:S(2)}, u32[]{:S(2)}) collective-permute-start(f32[128,128]{1,0:T(8,128)S(1)} %add_add_fusion.1.refs_0_), channel_id=1, source_target_pairs={{0,8},{8,0},{1,9},{9,1},{2,10},{10,2},{3,11},{11,3},{4,12},{12,4},... | collective-permute-start | bytes 196616 | tf_op jit(solution)/shard_map/ppermute | solution.py:28
  31.9 4.7 %collective-permute-start.8 = (f32[128,128]{1,0:T(8,128)S(1)}, f32[128,128]{1,0:T(8,128)S(1)}, u32[]{:S(2)}, u32[]{:S(2)}) collective-permute-start(f32[128,128]{1,0:T(8,128)S(1)} %collective-permute-done.4.refs_1_), channel_id=1, source_target_pairs={{0,8},{8,0},{1,9},{9,1},{2,10},{10,2},{3,11},{11,3},{4,12},{12,4},... | collective-permute-start | bytes 196616 | tf_op jit(solution)/shard_map/ppermute | solution.py:28
  32.0 4.6 %collective-permute-start.9 = (f32[128,128]{1,0:T(8,128)S(1)}, f32[128,128]{1,0:T(8,128)S(1)}, u32[]{:S(2)}, u32[]{:S(2)}) collective-permute-start(f32[128,128]{1,0:T(8,128)S(1)} %collective-permute-done.5.refs_2_), channel_id=1, source_target_pairs={{0,8},{8,0},{1,9},{9,1},{2,10},{10,2},{3,11},{11,3},{4,12},{12,4},... | collective-permute-start | bytes 196616 | tf_op jit(solution)/shard_map/ppermute | solution.py:28
  32.4 4.2 %collective-permute-start.10 = (f32[128,128]{1,0:T(8,128)S(1)}, f32[128,128]{1,0:T(8,128)S(1)}, u32[]{:S(2)}, u32[]{:S(2)}) collective-permute-start(f32[128,128]{1,0:T(8,128)S(1)} %collective-permute-done.6.refs_3_), channel_id=1, source_target_pairs={{0,8},{8,0},{1,9},{9,1},{2,10},{10,2},{3,11},{11,3},{4,12},{12,4},... | collective-permute-start | bytes 196616 | tf_op jit(solution)/shard_map/ppermute | solution.py:28
  36.6 8.4 %copy-start = (s32[128,128]{1,0:T(8,128)S(1)}, s32[128,128]{1,0:T(8,128)}, u32[]{:S(2)}) copy-start(s32[128,128]{1,0:T(8,128)} %mask_ref.1) | copy-start | bytes 196612
  37.7 5.3 %collective-permute-start.14 = (f32[136,128]{1,0:T(8,128)S(1)}, f32[136,128]{1,0:T(8,128)S(1)}, u32[]{:S(2)}, u32[]{:S(2)}) collective-permute-start(f32[136,128]{1,0:T(8,128)S(1)} %get-tuple-element.41.refs_10_), channel_id=1, source_target_pairs={{0,128},{64,192},{128,0},{192,64},{1,129},{65,193},{129,1},{193,65... | collective-permute-start | bytes 208904 | tf_op jit(solution)/shard_map/ppermute | solution.py:28
  40.7 4.4 %collective-permute-start.15 = (f32[136,128]{1,0:T(8,128)S(1)}, f32[136,128]{1,0:T(8,128)S(1)}, u32[]{:S(2)}, u32[]{:S(2)}) collective-permute-start(f32[136,128]{1,0:T(8,128)S(1)} %get-tuple-element.42.refs_11_), channel_id=1, source_target_pairs={{0,192},{64,128},{128,64},{192,0},{1,193},{65,129},{129,65},{193,1... | collective-permute-start | bytes 208904 | tf_op jit(solution)/shard_map/ppermute | solution.py:28
  41.5 3.6 %collective-permute-start.16 = (f32[136,128]{1,0:T(8,128)S(1)}, f32[136,128]{1,0:T(8,128)S(1)}, u32[]{:S(2)}, u32[]{:S(2)}) collective-permute-start(f32[136,128]{1,0:T(8,128)S(1)} %get-tuple-element.43.refs_9_), channel_id=1, source_target_pairs={{0,64},{64,0},{128,192},{192,128},{1,65},{65,1},{129,193},{193,129... | collective-permute-start | bytes 208904 | tf_op jit(solution)/shard_map/ppermute | solution.py:28
  45.1 3.4 %collective-permute-start.17 = (f32[136,128]{1,0:T(8,128)S(1)}, f32[136,128]{1,0:T(8,128)S(1)}, u32[]{:S(2)}, u32[]{:S(2)}) collective-permute-start(f32[136,128]{1,0:T(8,128)S(1)} %shard_map.90.own_ref.refs_16_.image_ref), channel_id=1, source_target_pairs={{0,1},{1,0},{2,3},{3,2},{4,5},{5,4},{6,7},{7,6},{8,9},{9,8},{10,11... | collective-permute-start | bytes 208904 | tf_op jit(solution)/shard_map/ppermute | solution.py:28
  48.9 9.5 %collective-permute-start.19 = (f32[136,128]{1,0:T(8,128)S(1)}, f32[136,128]{1,0:T(8,128)S(1)}, u32[]{:S(2)}, u32[]{:S(2)}) collective-permute-start(f32[136,128]{1,0:T(8,128)S(1)} %get-tuple-element.46), channel_id=1, source_target_pairs={{0,6},{2,4},{4,2},{6,0},{1,7},{3,5},{5,3},{7,1},{8,14},{10,12},{12... | collective-permute-start | bytes 208904 | tf_op jit(solution)/shard_map/ppermute | solution.py:28
  49.6 8.8 %collective-permute-start.20 = (f32[136,128]{1,0:T(8,128)S(1)}, f32[136,128]{1,0:T(8,128)S(1)}, u32[]{:S(2)}, u32[]{:S(2)}) collective-permute-start(f32[136,128]{1,0:T(8,128)S(1)} %get-tuple-element.47), channel_id=1, source_target_pairs={{0,2},{2,0},{4,6},{6,4},{1,3},{3,1},{5,7},{7,5},{8,10},{10,8},{12,... | collective-permute-start | bytes 208904 | tf_op jit(solution)/shard_map/ppermute | solution.py:28
  50.1 8.3 %collective-permute-start.18 = (f32[136,128]{1,0:T(8,128)S(1)}, f32[136,128]{1,0:T(8,128)S(1)}, u32[]{:S(2)}, u32[]{:S(2)}) collective-permute-start(f32[136,128]{1,0:T(8,128)S(1)} %get-tuple-element.45), channel_id=1, source_target_pairs={{0,4},{2,6},{4,0},{6,2},{1,5},{3,7},{5,1},{7,3},{8,12},{10,14},{12... | collective-permute-start | bytes 208904 | tf_op jit(solution)/shard_map/ppermute | solution.py:28
  54.7 7.7 %collective-permute-start.28 = (f32[136,128]{1,0:T(8,128)S(1)}, f32[136,128]{1,0:T(8,128)S(1)}, u32[]{:S(2)}, u32[]{:S(2)}) collective-permute-start(f32[136,128]{1,0:T(8,128)S(1)} %shard_map.90.own_ref.refs_16_.image_ref), channel_id=1, source_target_pairs={{0,64},{64,0},{128,192},{192,128},{1,65},{65,1},{129,193},{193,129... | collective-permute-start | bytes 208904 | tf_op jit(solution)/shard_map/ppermute | solution.py:28
  55.8 8.7 %collective-permute-start.29 = (f32[136,128]{1,0:T(8,128)S(1)}, f32[136,128]{1,0:T(8,128)S(1)}, u32[]{:S(2)}, u32[]{:S(2)}) collective-permute-start(f32[136,128]{1,0:T(8,128)S(1)} %shard_map.90.own_ref.refs_16_.image_ref), channel_id=1, source_target_pairs={{0,128},{64,192},{128,0},{192,64},{1,129},{65,193},{129,1},{193,65... | collective-permute-start | bytes 208904 | tf_op jit(solution)/shard_map/ppermute | solution.py:28
  58.5 9.6 %collective-permute-start.21 = (f32[136,128]{1,0:T(8,128)S(1)}, f32[136,128]{1,0:T(8,128)S(1)}, u32[]{:S(2)}, u32[]{:S(2)}) collective-permute-start(f32[136,128]{1,0:T(8,128)S(1)} %add_add_fusion.refs_0_), channel_id=1, source_target_pairs={{0,16},{16,0},{32,48},{48,32},{1,17},{17,1},{33,49},{49,33},{2,18}... | collective-permute-start | bytes 208904 | tf_op jit(solution)/shard_map/ppermute | solution.py:28
  58.6 9.6 %collective-permute-start.22 = (f32[136,128]{1,0:T(8,128)S(1)}, f32[136,128]{1,0:T(8,128)S(1)}, u32[]{:S(2)}, u32[]{:S(2)}) collective-permute-start(f32[136,128]{1,0:T(8,128)S(1)} %add_add_fusion.refs_0_), channel_id=1, source_target_pairs={{0,32},{16,48},{32,0},{48,16},{1,33},{17,49},{33,1},{49,17},{2,34}... | collective-permute-start | bytes 208904 | tf_op jit(solution)/shard_map/ppermute | solution.py:28
  59.9 8.6 %collective-permute-start.23 = (f32[136,128]{1,0:T(8,128)S(1)}, f32[136,128]{1,0:T(8,128)S(1)}, u32[]{:S(2)}, u32[]{:S(2)}) collective-permute-start(f32[136,128]{1,0:T(8,128)S(1)} %add_add_fusion.refs_0_), channel_id=1, source_target_pairs={{0,48},{16,32},{32,16},{48,0},{1,49},{17,33},{33,17},{49,1},{2,50}... | collective-permute-start | bytes 208904 | tf_op jit(solution)/shard_map/ppermute | solution.py:28
  62.4 7.1 %collective-permute-start.30 = (f32[136,128]{1,0:T(8,128)S(1)}, f32[136,128]{1,0:T(8,128)S(1)}, u32[]{:S(2)}, u32[]{:S(2)}) collective-permute-start(f32[136,128]{1,0:T(8,128)S(1)} %shard_map.90.own_ref.refs_16_.image_ref), channel_id=1, source_target_pairs={{0,192},{64,128},{128,64},{192,0},{1,193},{65,129},{129,65},{193,1... | collective-permute-start | bytes 208904 | tf_op jit(solution)/shard_map/ppermute | solution.py:28
  64.5 5.0 %collective-permute-start.24 = (f32[136,128]{1,0:T(8,128)S(1)}, f32[136,128]{1,0:T(8,128)S(1)}, u32[]{:S(2)}, u32[]{:S(2)}) collective-permute-start(f32[136,128]{1,0:T(8,128)S(1)} %add_add_fusion.refs_0_), channel_id=1, source_target_pairs={{0,8},{8,0},{1,9},{9,1},{2,10},{10,2},{3,11},{11,3},{4,12},{12,4},... | collective-permute-start | bytes 208904 | tf_op jit(solution)/shard_map/ppermute | solution.py:28
  68.1 1.4 %collective-permute-start.25 = (f32[136,128]{1,0:T(8,128)S(1)}, f32[136,128]{1,0:T(8,128)S(1)}, u32[]{:S(2)}, u32[]{:S(2)}) collective-permute-start(f32[136,128]{1,0:T(8,128)S(1)} %collective-permute-done.21.refs_1_), channel_id=1, source_target_pairs={{0,8},{8,0},{1,9},{9,1},{2,10},{10,2},{3,11},{11,3},{4,12},{12,4},... | collective-permute-start | bytes 208904 | tf_op jit(solution)/shard_map/ppermute | solution.py:28
  68.1 1.3 %collective-permute-start.26 = (f32[136,128]{1,0:T(8,128)S(1)}, f32[136,128]{1,0:T(8,128)S(1)}, u32[]{:S(2)}, u32[]{:S(2)}) collective-permute-start(f32[136,128]{1,0:T(8,128)S(1)} %collective-permute-done.22.refs_2_), channel_id=1, source_target_pairs={{0,8},{8,0},{1,9},{9,1},{2,10},{10,2},{3,11},{11,3},{4,12},{12,4},... | collective-permute-start | bytes 208904 | tf_op jit(solution)/shard_map/ppermute | solution.py:28
  68.6 1.8 %collective-permute-start.27 = (f32[136,128]{1,0:T(8,128)S(1)}, f32[136,128]{1,0:T(8,128)S(1)}, u32[]{:S(2)}, u32[]{:S(2)}) collective-permute-start(f32[136,128]{1,0:T(8,128)S(1)} %collective-permute-done.23.refs_3_), channel_id=1, source_target_pairs={{0,8},{8,0},{1,9},{9,1},{2,10},{10,2},{3,11},{11,3},{4,12},{12,4},... | collective-permute-start | bytes 208904 | tf_op jit(solution)/shard_map/ppermute | solution.py:28
  72.2 10.5 %copy-start.2 = (f32[2,4096]{1,0:T(2,128)S(1)}, f32[2,4096]{1,0:T(2,128)}, u32[]{:S(2)}) copy-start(f32[2,4096]{1,0:T(2,128)} %tests_ref.1) | copy-start | bytes 98308
  72.3 10.5 %copy-start.3 = (s32[4096]{0:T(1024)S(1)}, s32[4096]{0:T(1024)}, u32[]{:S(2)}) copy-start(s32[4096]{0:T(1024)} %param.13) | copy-start | bytes 49156
  72.3 26.8 %all-to-all-start = ((f32[256,1,128]{2,1,0:T(1,128)}), f32[256,1,128]{2,1,0:T(1,128)S(1)}, u32[]{:S(2)}, u32[]{:S(2)}) async-start(f32[256,1,128]{2,1,0:T(1,128)} %get-tuple-element.48), calls=%async_computation | async-start | bytes 262144 | tf_op jit(solution)/shard_map/all_to_all | solution.py:298
  88.3 6.0 %collective-permute-start.31 = (f32[128,256]{1,0:T(8,128)S(1)}, f32[128,256]{1,0:T(8,128)S(1)}, u32[]{:S(2)}, u32[]{:S(2)}) collective-permute-start(f32[128,256]{1,0:T(8,128)S(1)} %get-tuple-element.57), channel_id=1, source_target_pairs={{0,128},{64,192},{128,0},{192,64},{1,129},{65,193},{129,1},{193,65... | collective-permute-start | bytes 393224 | tf_op jit(solution)/shard_map/ppermute | solution.py:28
  91.3 7.8 %collective-permute-start.32 = (f32[128,256]{1,0:T(8,128)S(1)}, f32[128,256]{1,0:T(8,128)S(1)}, u32[]{:S(2)}, u32[]{:S(2)}) collective-permute-start(f32[128,256]{1,0:T(8,128)S(1)} %get-tuple-element.58), channel_id=1, source_target_pairs={{0,192},{64,128},{128,64},{192,0},{1,193},{65,129},{129,65},{193,1... | collective-permute-start | bytes 393224 | tf_op jit(solution)/shard_map/ppermute | solution.py:28
  92.1 6.9 %collective-permute-start.33 = (f32[128,256]{1,0:T(8,128)S(1)}, f32[128,256]{1,0:T(8,128)S(1)}, u32[]{:S(2)}, u32[]{:S(2)}) collective-permute-start(f32[128,256]{1,0:T(8,128)S(1)} %get-tuple-element.59), channel_id=1, source_target_pairs={{0,64},{64,0},{128,192},{192,128},{1,65},{65,1},{129,193},{193,129... | collective-permute-start | bytes 393224 | tf_op jit(solution)/shard_map/ppermute | solution.py:28

commit v4 on v2

--- a/solution.py
+++ b/solution.py
@@ -108,8 +108,7 @@
         low_ref[rows, :] = low
 
 
-def time_kernel(stamps_ref, noise_ref, high_ref, low_ref, noise_out_ref, *, length):
-    noise_out_ref[...] = noise_ref[...]
+def time_kernel(stamps_ref, high_ref, low_ref, *, length):
     own = 2 * lax.axis_index("tm_0") + lax.axis_index("tm_1")
     columns = upright(jnp.concatenate([stamps_ref[pl.ds(t, 1), :] for t in (own, own ^ 1)], 0))
     for s in range(2):
@@ -126,7 +125,9 @@
         points_ref[:, k * TILE : (k + 1) * TILE] = lanes(sites_ref, place)
 
 
-def site_kernel(sites_ref, high_ref, low_ref, points_ref, at_ref, *, length):
+def site_kernel(sites_ref, noise_ref, *refs, length):
+    high_ref, low_ref, noise_out_ref, points_ref, at_ref = refs
+    noise_out_ref[...] = noise_ref[...]
     set_columns(sites_ref, points_ref)
     lines = jnp.concatenate([lanes(sites_ref, place) for place in row_places()], 0)
     columns = upright(lines)
@@ -300,19 +301,19 @@
         return lax.all_to_all(copies, axes, split_axis=0, concat_axis=0, tiled=True)
 
     start = observed_mask.astype(f32) * observed
-    start_rows = gathered(start, "loc_0", (2, 1, 3))
-
-    time_high, time_low, noise = call(
+    start_rows = gathered(start, "loc_0", (3, 2, 1))
+
+    time_high, time_low = call(
         functools.partial(time_kernel, length=time_reach / times),
-        [((2 * TILE, 4 * TILE), bf16)] * 2 + [((1, TILE), f32)],
+        [((2 * TILE, 4 * TILE), bf16)] * 2,
         time_stamps.reshape(8, TILE),
+        flops=20 * 8 * TILE * TILE,
+    )
+    site_high, site_low, noise = call(
+        functools.partial(site_kernel, length=space_length),
+        split_pair + [((1, TILE), f32)],
+        training_site_positions,
         noise_var[None, :],
-        flops=20 * 8 * TILE * TILE,
-    )
-    site_high, site_low = call(
-        functools.partial(site_kernel, length=space_length),
-        split_pair,
-        training_site_positions,
         flops=400 * 4 * TILE * 8 * TILE,
         scratch=points,
     )
@@ -327,11 +328,11 @@
             time_low,
             flops=6 * TILE * 8 * TILE * TILE,
         )
-        parts = [parts[0]] + [ahead(parts[k], "tm_0", -k) for k in (2, 3, 1)]
-        return (parts[0] + parts[1]) + (parts[2] + parts[3])
+        parts = [parts[0]] + [ahead(parts[k], "tm_0", -k) for k in (1, 2, 3)]
+        return (parts[0] + parts[2]) + (parts[1] + parts[3])
 
     def columns(block):
-        held = gathered(block, "loc_1", (2, 1, 3))
+        held = gathered(block, "loc_1", (3, 2, 1))
         return held + [swapped(piece) for piece in held]
 
     def to_owners(parts):
@@ -372,7 +373,7 @@
         flops=10 * TILE * TILE,
     )
     other = neighbours(image)
-    image_rows = gathered(image, "loc_0", (2, 1, 3))
+    image_rows = gathered(image, "loc_0", (3, 2, 1))
     image_fold = folded(image, other)
     start_fields = call(
         field_kernel,

time: 99.7 us -> 100 us (level)
  starting transfers between devices: 68.2 us -> 71.8 us
  waiting for transfers between devices: 15.4 us -> 13.3 us
    ppermute x24, starting transfers between devices: 39 us -> 41.2 us  [ahead(): lax.ppermute(block, axis, [((i + shift) % size, i) for i in range(size)])]
    ppermute x24, waiting for transfers between devices: 11.4 us -> 9.38 us  [ahead(): lax.ppermute(block, axis, [((i + shift) % size, i) for i in range(size)])]
    ppermute x2, starting transfers between devices: 3.37 us -> 4.4 us  [neighbours(): return lax.ppermute(block, 'tm_1', [(0, 1), (1, 0)])]
where the time goes in v4:
time: 100 us
  starting transfers between devices  71.8 us (72%)
  Pallas kernels  13.5 us (14%)
  waiting for transfers between devices  13.3 us (13%)
    ppermute x24, starting transfers between devices, ahead(): lax.ppermute(block, axis, [((i + shift) % size, i) for i in range(size)])  41.2 us
    ppermute x8, starting transfers between devices, swapped(): return lax.ppermute(block, 'loc_2', [(0, 1), (1, 0)])  14.9 us
    pallas_call x11, Pallas kernels, call(): pl.pallas_call(kernel, out_shape=shapes, in_specs=[VMEM] * len(args), out...  13.5 us
    all_to_all x1, starting transfers between devices, exchanged(): return lax.all_to_all(copies, axes, split_axis=0, concat_axis=0, tiled=True)  11.2 us
    ppermute x24, waiting for transfers between devices, ahead(): lax.ppermute(block, axis, [((i + shift) % size, i) for i in range(size)])  9.38 us
    ppermute x2, starting transfers between devices, neighbours(): return lax.ppermute(block, 'tm_1', [(0, 1), (1, 0)])  4.4 us
    ppermute x2, waiting for transfers between devices, neighbours(): return lax.ppermute(block, 'tm_1', [(0, 1), (1, 0)])  2.99 us
  transfers between devices with their start and end apart: 35, of which 11 were waited for; matrix products, arithmetic and copies ran while one was open for 0% of the time, Pallas kernels for 9%

profile of v4, /device:TPU:1, one launch (start us, length us, event | category | flops | bytes accessed | tf_op | source)
XLA Modules:
  0.0 100.3 jit_solution(17741806887377159451)
XLA Ops:
  0.6 0.9 convert_multiply_fusion.own_ref.refs_8_.start_ref.refs_12_
  1.5 2.5 %collective-permute-start = (f32[128,128]{1,0:T(8,128)S(1)}, f32[128,128]{1,0:T(8,128)S(1)}, u32[]{:S(2)}, u32[]{:S(2)}) collective-permute-start(f32[128,128]{1,0:T(8,128)S(1)} %convert_multiply_fusion.own_ref.refs_8_.start_ref.refs_12_), channel_id=1, source_target_pairs={{0,1},{1,0},{2,3},{3,2},{4,5},{5,4},{6,7},{7,6},{8,9},{9,8},{10,11... | collective-permute-start | bytes 196616 | tf_op jit(solution)/shard_map/ppermute | solution.py:40
  4.4 1.3 %collective-permute-done.other_ref = f32[128,128]{1,0:T(8,128)S(1)} collective-permute-done((f32[128,128]{1,0:T(8,128)S(1)}, f32[128,128]{1,0:T(8,128)S(1)}, u32[]{:S(2)}, u32[]{:S(2)}) %collective-permute-start) | collective-permute-done | bytes 65568 | tf_op jit(solution)/shard_map/ppermute | solution.py:40
  5.7 0.4 shard_map.87
  6.1 3.1 %collective-permute-start.2 = (f32[128,128]{1,0:T(8,128)S(1)}, f32[128,128]{1,0:T(8,128)S(1)}, u32[]{:S(2)}, u32[]{:S(2)}) collective-permute-start(f32[128,128]{1,0:T(8,128)S(1)} %get-tuple-element.35), channel_id=1, source_target_pairs={{6,0},{0,2},{2,4},{4,6},{7,1},{1,3},{3,5},{5,7},{14,8},{8,10},{10,... | collective-permute-start | bytes 196616 | tf_op jit(solution)/shard_map/ppermute | solution.py:29
  9.2 2.9 %collective-permute-start.3 = (f32[128,128]{1,0:T(8,128)S(1)}, f32[128,128]{1,0:T(8,128)S(1)}, u32[]{:S(2)}, u32[]{:S(2)}) collective-permute-start(f32[128,128]{1,0:T(8,128)S(1)} %get-tuple-element.36), channel_id=1, source_target_pairs={{2,0},{4,2},{6,4},{0,6},{3,1},{5,3},{7,5},{1,7},{10,8},{12,10},{14... | collective-permute-start | bytes 196616 | tf_op jit(solution)/shard_map/ppermute | solution.py:29
  12.1 4.4 %collective-permute-start.1 = (f32[128,128]{1,0:T(8,128)S(1)}, f32[128,128]{1,0:T(8,128)S(1)}, u32[]{:S(2)}, u32[]{:S(2)}) collective-permute-start(f32[128,128]{1,0:T(8,128)S(1)} %get-tuple-element.34), channel_id=1, source_target_pairs={{4,0},{6,2},{0,4},{2,6},{5,1},{7,3},{1,5},{3,7},{12,8},{14,10},{8,... | collective-permute-start | bytes 196616 | tf_op jit(solution)/shard_map/ppermute | solution.py:29
  16.5 2.7 %collective-permute-start.11 = (f32[128,128]{1,0:T(8,128)S(1)}, f32[128,128]{1,0:T(8,128)S(1)}, u32[]{:S(2)}, u32[]{:S(2)}) collective-permute-start(f32[128,128]{1,0:T(8,128)S(1)} %convert_multiply_fusion.own_ref.refs_8_.start_ref.refs_12_), channel_id=1, source_target_pairs={{64,0},{128,64},{192,128},{0,192},{65,1},{129,65},{193,129},{1,193... | collective-permute-start | bytes 196616 | tf_op jit(solution)/shard_map/ppermute | solution.py:29
  19.7 2.6 %collective-permute-start.4 = (f32[128,128]{1,0:T(8,128)S(1)}, f32[128,128]{1,0:T(8,128)S(1)}, u32[]{:S(2)}, u32[]{:S(2)}) collective-permute-start(f32[128,128]{1,0:T(8,128)S(1)} %add_add_fusion.1.refs_0_), channel_id=1, source_target_pairs={{16,0},{32,16},{48,32},{0,48},{17,1},{33,17},{49,33},{1,49},{18,2}... | collective-permute-start | bytes 196616 | tf_op jit(solution)/shard_map/ppermute | solution.py:29
  22.3 0.5 collective-permute-start.5
  22.8 0.6 collective-permute-start.6
  23.4 1.3 %collective-permute-start.13 = (f32[128,128]{1,0:T(8,128)S(1)}, f32[128,128]{1,0:T(8,128)S(1)}, u32[]{:S(2)}, u32[]{:S(2)}) collective-permute-start(f32[128,128]{1,0:T(8,128)S(1)} %convert_multiply_fusion.own_ref.refs_8_.start_ref.refs_12_), channel_id=1, source_target_pairs={{192,0},{0,64},{64,128},{128,192},{193,1},{1,65},{65,129},{129,193... | collective-permute-start | bytes 196616 | tf_op jit(solution)/shard_map/ppermute | solution.py:29
  24.7 4.0 %collective-permute-start.7 = (f32[128,128]{1,0:T(8,128)S(1)}, f32[128,128]{1,0:T(8,128)S(1)}, u32[]{:S(2)}, u32[]{:S(2)}) collective-permute-start(f32[128,128]{1,0:T(8,128)S(1)} %add_add_fusion.1.refs_0_), channel_id=1, source_target_pairs={{0,8},{8,0},{1,9},{9,1},{2,10},{10,2},{3,11},{11,3},{4,12},{12,4},... | collective-permute-start | bytes 196616 | tf_op jit(solution)/shard_map/ppermute | solution.py:44
  28.7 2.7 %collective-permute-start.9 = (f32[128,128]{1,0:T(8,128)S(1)}, f32[128,128]{1,0:T(8,128)S(1)}, u32[]{:S(2)}, u32[]{:S(2)}) collective-permute-start(f32[128,128]{1,0:T(8,128)S(1)} %collective-permute-done.5.refs_2_), channel_id=1, source_target_pairs={{0,8},{8,0},{1,9},{9,1},{2,10},{10,2},{3,11},{11,3},{4,12},{12,4},... | collective-permute-start | bytes 196616 | tf_op jit(solution)/shard_map/ppermute | solution.py:44
  31.5 0.7 collective-permute-start.10
  32.2 2.7 %shard_map.88 = (bf16[512,1024]{1,0:T(8,128)(2,1)S(1)}, bf16[512,1024]{1,0:T(8,128)(2,1)S(1)}, f32[1,128]{1,0:T(1,128)S(1)}) custom-call(f32[2,4096]{1,0:T(2,128)S(1)} %copy-done.1, f32[1,128]{1,0:T(1,128)S(1)} %bitcast.5), custom_call_target="tpu_custom_call" | custom-call | flops 209715200 | bytes 2130944 | tf_op jit(solution)/shard_map/pallas_call | solution.py:59
  34.9 1.1 %shard_map.89 = (f32[136,128]{1,0:T(8,128)S(1)}, f32[136,128]{1,0:T(8,128)S(1)}, f32[136,128]{1,0:T(8,128)S(1)}, f32[136,128]{1,0:T(8,128)S(1)}) custom-call(f32[128,128]{1,0:T(8,128)S(1)} %add_add_fusion.1.refs_0_, f32[128,128]{1,0:T(8,128)S(1)} %collective-permute-done.4.refs_1_, f32[128,128]{1,0:T(8,128)S(1)} %collective-permute-done.5.refs_2_, ...), custom_call_target="tpu_custom_call" | custom-call | flops 402653184 | bytes 3162624 | tf_op jit(solution)/shard_map/pallas_call | solution.py:59
  36.0 1.1 %collective-permute-start.14 = (f32[136,128]{1,0:T(8,128)S(1)}, f32[136,128]{1,0:T(8,128)S(1)}, u32[]{:S(2)}, u32[]{:S(2)}) collective-permute-start(f32[136,128]{1,0:T(8,128)S(1)} %get-tuple-element.41.refs_9_), channel_id=1, source_target_pairs={{192,0},{0,64},{64,128},{128,192},{193,1},{1,65},{65,129},{129,193... | collective-permute-start | bytes 208904 | tf_op jit(solution)/shard_map/ppermute | solution.py:29
  37.1 2.6 %collective-permute-start.15 = (f32[136,128]{1,0:T(8,128)S(1)}, f32[136,128]{1,0:T(8,128)S(1)}, u32[]{:S(2)}, u32[]{:S(2)}) collective-permute-start(f32[136,128]{1,0:T(8,128)S(1)} %get-tuple-element.42.refs_10_), channel_id=1, source_target_pairs={{128,0},{192,64},{0,128},{64,192},{129,1},{193,65},{1,129},{65,193... | collective-permute-start | bytes 208904 | tf_op jit(solution)/shard_map/ppermute | solution.py:29
  39.7 1.1 %collective-permute-start.16 = (f32[136,128]{1,0:T(8,128)S(1)}, f32[136,128]{1,0:T(8,128)S(1)}, u32[]{:S(2)}, u32[]{:S(2)}) collective-permute-start(f32[136,128]{1,0:T(8,128)S(1)} %get-tuple-element.43.refs_11_), channel_id=1, source_target_pairs={{64,0},{128,64},{192,128},{0,192},{65,1},{129,65},{193,129},{1,193... | collective-permute-start | bytes 208904 | tf_op jit(solution)/shard_map/ppermute | solution.py:29
  41.0 2.4 %collective-permute-done.15.c = f32[136,128]{1,0:T(8,128)S(1)} collective-permute-done((f32[136,128]{1,0:T(8,128)S(1)}, f32[136,128]{1,0:T(8,128)S(1)}, u32[]{:S(2)}, u32[]{:S(2)}) %collective-permute-start.15) | collective-permute-done | bytes 69664 | tf_op jit(solution)/shard_map/ppermute | solution.py:29
  43.5 1.9 %collective-permute-start.17 = (f32[136,128]{1,0:T(8,128)S(1)}, f32[136,128]{1,0:T(8,128)S(1)}, u32[]{:S(2)}, u32[]{:S(2)}) collective-permute-start(f32[136,128]{1,0:T(8,128)S(1)} %shard_map.90.own_ref.refs_16_.image_ref), channel_id=1, source_target_pairs={{0,1},{1,0},{2,3},{3,2},{4,5},{5,4},{6,7},{7,6},{8,9},{9,8},{10,11... | collective-permute-start | bytes 208904 | tf_op jit(solution)/shard_map/ppermute | solution.py:40
  45.4 1.7 %collective-permute-done.17.other_ref = f32[136,128]{1,0:T(8,128)S(1)} collective-permute-done((f32[136,128]{1,0:T(8,128)S(1)}, f32[136,128]{1,0:T(8,128)S(1)}, u32[]{:S(2)}, u32[]{:S(2)}) %collective-permute-start.17) | collective-permute-done | bytes 69664 | tf_op jit(solution)/shard_map/ppermute | solution.py:40
  47.4 0.7 collective-permute-start.19
  48.1 2.9 %collective-permute-start.20 = (f32[136,128]{1,0:T(8,128)S(1)}, f32[136,128]{1,0:T(8,128)S(1)}, u32[]{:S(2)}, u32[]{:S(2)}) collective-permute-start(f32[136,128]{1,0:T(8,128)S(1)} %get-tuple-element.47), channel_id=1, source_target_pairs={{2,0},{4,2},{6,4},{0,6},{3,1},{5,3},{7,5},{1,7},{10,8},{12,10},{14... | collective-permute-start | bytes 208904 | tf_op jit(solution)/shard_map/ppermute | solution.py:29
  51.1 4.4 %collective-permute-start.18 = (f32[136,128]{1,0:T(8,128)S(1)}, f32[136,128]{1,0:T(8,128)S(1)}, u32[]{:S(2)}, u32[]{:S(2)}) collective-permute-start(f32[136,128]{1,0:T(8,128)S(1)} %get-tuple-element.45), channel_id=1, source_target_pairs={{4,0},{6,2},{0,4},{2,6},{5,1},{7,3},{1,5},{3,7},{12,8},{14,10},{8,... | collective-permute-start | bytes 208904 | tf_op jit(solution)/shard_map/ppermute | solution.py:29
  55.4 1.7 %collective-permute-start.28 = (f32[136,128]{1,0:T(8,128)S(1)}, f32[136,128]{1,0:T(8,128)S(1)}, u32[]{:S(2)}, u32[]{:S(2)}) collective-permute-start(f32[136,128]{1,0:T(8,128)S(1)} %shard_map.90.own_ref.refs_16_.image_ref), channel_id=1, source_target_pairs={{64,0},{128,64},{192,128},{0,192},{65,1},{129,65},{193,129},{1,193... | collective-permute-start | bytes 208904 | tf_op jit(solution)/shard_map/ppermute | solution.py:29
  57.1 0.8 collective-permute-start.29
  57.9 0.5 collective-permute-done.18
  58.6 0.9 collective-permute-start.22
  59.5 0.8 collective-permute-start.23
  60.3 0.6 collective-permute-start.30
  61.0 0.8 collective-permute-done.29.refs_18_
  61.8 5.6 %collective-permute-start.24 = (f32[136,128]{1,0:T(8,128)S(1)}, f32[136,128]{1,0:T(8,128)S(1)}, u32[]{:S(2)}, u32[]{:S(2)}) collective-permute-start(f32[136,128]{1,0:T(8,128)S(1)} %add_add_fusion.refs_0_), channel_id=1, source_target_pairs={{0,8},{8,0},{1,9},{9,1},{2,10},{10,2},{3,11},{11,3},{4,12},{12,4},... | collective-permute-start | bytes 208904 | tf_op jit(solution)/shard_map/ppermute | solution.py:44
  67.3 1.1 %collective-permute-start.26 = (f32[136,128]{1,0:T(8,128)S(1)}, f32[136,128]{1,0:T(8,128)S(1)}, u32[]{:S(2)}, u32[]{:S(2)}) collective-permute-start(f32[136,128]{1,0:T(8,128)S(1)} %collective-permute-done.22.refs_2_), channel_id=1, source_target_pairs={{0,8},{8,0},{1,9},{9,1},{2,10},{10,2},{3,11},{11,3},{4,12},{12,4},... | collective-permute-start | bytes 208904 | tf_op jit(solution)/shard_map/ppermute | solution.py:44
  68.5 0.7 collective-permute-start.27
  69.4 0.7 collective-permute-done.27.refs_7_
  70.1 1.9 %shard_map.92 = (f32[256,1,128]{2,1,0:T(1,128)}, f32[1,128]{1,0:T(1,128)S(1)}) custom-call(f32[136,128]{1,0:T(8,128)S(1)} %add_add_fusion.refs_0_, f32[136,128]{1,0:T(8,128)S(1)} %collective-permute-done.21.refs_1_, f32[136,128]{1,0:T(8,128)S(1)} %collective-permute-done.22.refs_2_, f32[136,128]{1,0:T(8,128)S(1)} %collective-permute-done.23.refs_3_, ...), custom_call_target="tpu_custom_call" | custom-call | flops 402653184 | bytes 3605504 | tf_op jit(solution)/shard_map/pallas_call | solution.py:59
  72.0 11.2 %all-to-all-start = ((f32[256,1,128]{2,1,0:T(1,128)}), f32[256,1,128]{2,1,0:T(1,128)S(1)}, u32[]{:S(2)}, u32[]{:S(2)}) async-start(f32[256,1,128]{2,1,0:T(1,128)} %get-tuple-element.48), calls=%async_computation | async-start | bytes 262144 | tf_op jit(solution)/shard_map/all_to_all | solution.py:301
  83.2 3.5 %shard_map.93 = (bf16[512,1024]{1,0:T(8,128)(2,1)S(1)}, bf16[512,1024]{1,0:T(8,128)(2,1)S(1)}) custom-call(f32[2,4096]{1,0:T(2,128)S(1)} %copy-done.1, f32[2,4096]{1,0:T(2,128)S(1)} %copy-done.2, s32[32,128]{1,0:T(8,128)S(1)} %bitcast.3), custom_call_target="tpu_custom_call" | custom-call | flops 314572800 | bytes 2179072 | tf_op jit(solution)/shard_map/pallas_call | solution.py:59
  86.7 1.0 %shard_map.94 = (f32[128,128]{1,0:T(8,128)S(1)}, f32[128,128]{1,0:T(8,128)S(1)}, f32[128,128]{1,0:T(8,128)S(1)}, f32[128,128]{1,0:T(8,128)S(1)}) custom-call(f32[128,128]{1,0:T(8,128)S(1)} %add_add_fusion.1.refs_0_, f32[128,128]{1,0:T(8,128)S(1)} %collective-permute-done.4.refs_1_, f32[128,128]{1,0:T(8,128)S(1)} %collective-permute-done.5.refs_2_, ...), custom_call_target="tpu_custom_call" | custom-call | flops 402653184 | bytes 2883584 | tf_op jit(solution)/shard_map/pallas_call | solution.py:59
  87.8 1.0 %shard_map.95 = (f32[128,256]{1,0:T(8,128)S(1)}, f32[128,256]{1,0:T(8,128)S(1)}, f32[128,256]{1,0:T(8,128)S(1)}, f32[128,256]{1,0:T(8,128)S(1)}) custom-call(f32[136,128]{1,0:T(8,128)S(1)} %add_add_fusion.refs_0_, f32[136,128]{1,0:T(8,128)S(1)} %collective-permute-done.21.refs_1_, f32[136,128]{1,0:T(8,128)S(1)} %collective-permute-done.22.refs_2_, ...), custom_call_target="tpu_custom_call" | custom-call | flops 402653184 | bytes 3440640 | tf_op jit(solution)/shard_map/pallas_call | solution.py:59
  88.8 1.4 %collective-permute-start.31 = (f32[128,256]{1,0:T(8,128)S(1)}, f32[128,256]{1,0:T(8,128)S(1)}, u32[]{:S(2)}, u32[]{:S(2)}) collective-permute-start(f32[128,256]{1,0:T(8,128)S(1)} %get-tuple-element.57), channel_id=1, source_target_pairs={{192,0},{0,64},{64,128},{128,192},{193,1},{1,65},{65,129},{129,193... | collective-permute-start | bytes 393224 | tf_op jit(solution)/shard_map/ppermute | solution.py:29
  90.2 2.5 %collective-permute-start.32 = (f32[128,256]{1,0:T(8,128)S(1)}, f32[128,256]{1,0:T(8,128)S(1)}, u32[]{:S(2)}, u32[]{:S(2)}) collective-permute-start(f32[128,256]{1,0:T(8,128)S(1)} %get-tuple-element.58), channel_id=1, source_target_pairs={{128,0},{192,64},{0,128},{64,192},{129,1},{193,65},{1,129},{65,193... | collective-permute-start | bytes 393224 | tf_op jit(solution)/shard_map/ppermute | solution.py:29
  92.7 1.1 %collective-permute-start.33 = (f32[128,256]{1,0:T(8,128)S(1)}, f32[128,256]{1,0:T(8,128)S(1)}, u32[]{:S(2)}, u32[]{:S(2)}) collective-permute-start(f32[128,256]{1,0:T(8,128)S(1)} %get-tuple-element.59), channel_id=1, source_target_pairs={{64,0},{128,64},{192,128},{0,192},{65,1},{129,65},{193,129},{1,193... | collective-permute-start | bytes 393224 | tf_op jit(solution)/shard_map/ppermute | solution.py:29
  93.8 0.7 collective-permute-done.31.refs_1_
  94.5 4.6 %collective-permute-done.32.refs_2_ = f32[128,256]{1,0:T(8,128)S(1)} collective-permute-done((f32[128,256]{1,0:T(8,128)S(1)}, f32[128,256]{1,0:T(8,128)S(1)}, u32[]{:S(2)}, u32[]{:S(2)}) %collective-permute-start.32) | collective-permute-done | bytes 131104 | tf_op jit(solution)/shard_map/ppermute | solution.py:29
  99.1 1.2 %shard_map.96 = (f32[128,128]{1,0:T(8,128)}, f32[128,128]{1,0:T(8,128)}) custom-call(f32[256,1,128]{2,1,0:T(1,128)S(1)} %all-to-all-done.sums_ref, f32[1,128]{1,0:T(1,128)S(1)} %get-tuple-element.49.known_ref, f32[128,128]{1,0:T(8,128)S(1)} %convert_multiply_fusion.own_ref.refs_8_.start_ref.refs_12_, f32[136,128]{1,0:T(8,128)S(1)} %shard_map.90.own_ref.refs_16_.image_ref, ...), custom_call_target="tpu_custom_call" | custom-call | flops 327680 | bytes 922112 | tf_op jit(solution)/shard_map/pallas_call | solution.py:59
  (48 shorter events, 2.1 us)
Async XLA Ops:
  0.6 3.4 %copy-start.4 = (f32[1024]{0:T(1024)S(1)}, f32[1024]{0:T(1024)}, u32[]{:S(2)}) copy-start(f32[1024]{0:T(1024)} %param.10) | copy-start | bytes 12292
  1.5 4.2 %collective-permute-start = (f32[128,128]{1,0:T(8,128)S(1)}, f32[128,128]{1,0:T(8,128)S(1)}, u32[]{:S(2)}, u32[]{:S(2)}) collective-permute-start(f32[128,128]{1,0:T(8,128)S(1)} %convert_multiply_fusion.own_ref.refs_8_.start_ref.refs_12_), channel_id=1, source_target_pairs={{0,1},{1,0},{2,3},{3,2},{4,5},{5,4},{6,7},{7,6},{8,9},{9,8},{10,11... | collective-permute-start | bytes 196616 | tf_op jit(solution)/shard_map/ppermute | solution.py:40
  6.1 13.5 %collective-permute-start.2 = (f32[128,128]{1,0:T(8,128)S(1)}, f32[128,128]{1,0:T(8,128)S(1)}, u32[]{:S(2)}, u32[]{:S(2)}) collective-permute-start(f32[128,128]{1,0:T(8,128)S(1)} %get-tuple-element.35), channel_id=1, source_target_pairs={{6,0},{0,2},{2,4},{4,6},{7,1},{1,3},{3,5},{5,7},{14,8},{8,10},{10,... | collective-permute-start | bytes 196616 | tf_op jit(solution)/shard_map/ppermute | solution.py:29
  9.2 10.4 %collective-permute-start.3 = (f32[128,128]{1,0:T(8,128)S(1)}, f32[128,128]{1,0:T(8,128)S(1)}, u32[]{:S(2)}, u32[]{:S(2)}) collective-permute-start(f32[128,128]{1,0:T(8,128)S(1)} %get-tuple-element.36), channel_id=1, source_target_pairs={{2,0},{4,2},{6,4},{0,6},{3,1},{5,3},{7,5},{1,7},{10,8},{12,10},{14... | collective-permute-start | bytes 196616 | tf_op jit(solution)/shard_map/ppermute | solution.py:29
  12.1 7.6 %collective-permute-start.1 = (f32[128,128]{1,0:T(8,128)S(1)}, f32[128,128]{1,0:T(8,128)S(1)}, u32[]{:S(2)}, u32[]{:S(2)}) collective-permute-start(f32[128,128]{1,0:T(8,128)S(1)} %get-tuple-element.34), channel_id=1, source_target_pairs={{4,0},{6,2},{0,4},{2,6},{5,1},{7,3},{1,5},{3,7},{12,8},{14,10},{8,... | collective-permute-start | bytes 196616 | tf_op jit(solution)/shard_map/ppermute | solution.py:29
  16.5 6.9 %collective-permute-start.11 = (f32[128,128]{1,0:T(8,128)S(1)}, f32[128,128]{1,0:T(8,128)S(1)}, u32[]{:S(2)}, u32[]{:S(2)}) collective-permute-start(f32[128,128]{1,0:T(8,128)S(1)} %convert_multiply_fusion.own_ref.refs_8_.start_ref.refs_12_), channel_id=1, source_target_pairs={{64,0},{128,64},{192,128},{0,192},{65,1},{129,65},{193,129},{1,193... | collective-permute-start | bytes 196616 | tf_op jit(solution)/shard_map/ppermute | solution.py:29
  19.2 5.5 %collective-permute-start.12 = (f32[128,128]{1,0:T(8,128)S(1)}, f32[128,128]{1,0:T(8,128)S(1)}, u32[]{:S(2)}, u32[]{:S(2)}) collective-permute-start(f32[128,128]{1,0:T(8,128)S(1)} %convert_multiply_fusion.own_ref.refs_8_.start_ref.refs_12_), channel_id=1, source_target_pairs={{128,0},{192,64},{0,128},{64,192},{129,1},{193,65},{1,129},{65,193... | collective-permute-start | bytes 196616 | tf_op jit(solution)/shard_map/ppermute | solution.py:29
  19.7 12.5 %copy-start.1 = (f32[2,4096]{1,0:T(2,128)S(1)}, f32[2,4096]{1,0:T(2,128)}, u32[]{:S(2)}) copy-start(f32[2,4096]{1,0:T(2,128)} %sites_ref.3) | copy-start | bytes 98308
  19.7 12.5 %copy-start.5 = (f32[128]{0:T(128)S(1)}, f32[128]{0:T(128)}, u32[]{:S(2)}) copy-start(f32[128]{0:T(128)} %param.11) | copy-start | bytes 1540
  19.7 8.9 %collective-permute-start.4 = (f32[128,128]{1,0:T(8,128)S(1)}, f32[128,128]{1,0:T(8,128)S(1)}, u32[]{:S(2)}, u32[]{:S(2)}) collective-permute-start(f32[128,128]{1,0:T(8,128)S(1)} %add_add_fusion.1.refs_0_), channel_id=1, source_target_pairs={{16,0},{32,16},{48,32},{0,48},{17,1},{33,17},{49,33},{1,49},{18,2}... | collective-permute-start | bytes 196616 | tf_op jit(solution)/shard_map/ppermute | solution.py:29
  22.3 6.5 %collective-permute-start.5 = (f32[128,128]{1,0:T(8,128)S(1)}, f32[128,128]{1,0:T(8,128)S(1)}, u32[]{:S(2)}, u32[]{:S(2)}) collective-permute-start(f32[128,128]{1,0:T(8,128)S(1)} %add_add_fusion.1.refs_0_), channel_id=1, source_target_pairs={{32,0},{48,16},{0,32},{16,48},{33,1},{49,17},{1,33},{17,49},{34,2}... | collective-permute-start | bytes 196616 | tf_op jit(solution)/shard_map/ppermute | solution.py:29
  22.8 8.7 %collective-permute-start.6 = (f32[128,128]{1,0:T(8,128)S(1)}, f32[128,128]{1,0:T(8,128)S(1)}, u32[]{:S(2)}, u32[]{:S(2)}) collective-permute-start(f32[128,128]{1,0:T(8,128)S(1)} %add_add_fusion.1.refs_0_), channel_id=1, source_target_pairs={{48,0},{0,16},{16,32},{32,48},{49,1},{1,17},{17,33},{33,49},{50,2}... | collective-permute-start | bytes 196616 | tf_op jit(solution)/shard_map/ppermute | solution.py:29
  23.4 11.5 %collective-permute-start.13 = (f32[128,128]{1,0:T(8,128)S(1)}, f32[128,128]{1,0:T(8,128)S(1)}, u32[]{:S(2)}, u32[]{:S(2)}) collective-permute-start(f32[128,128]{1,0:T(8,128)S(1)} %convert_multiply_fusion.own_ref.refs_8_.start_ref.refs_12_), channel_id=1, source_target_pairs={{192,0},{0,64},{64,128},{128,192},{193,1},{1,65},{65,129},{129,193... | collective-permute-start | bytes 196616 | tf_op jit(solution)/shard_map/ppermute | solution.py:29
  24.7 10.2 %collective-permute-start.7 = (f32[128,128]{1,0:T(8,128)S(1)}, f32[128,128]{1,0:T(8,128)S(1)}, u32[]{:S(2)}, u32[]{:S(2)}) collective-permute-start(f32[128,128]{1,0:T(8,128)S(1)} %add_add_fusion.1.refs_0_), channel_id=1, source_target_pairs={{0,8},{8,0},{1,9},{9,1},{2,10},{10,2},{3,11},{11,3},{4,12},{12,4},... | collective-permute-start | bytes 196616 | tf_op jit(solution)/shard_map/ppermute | solution.py:44
  28.7 6.2 %collective-permute-start.8 = (f32[128,128]{1,0:T(8,128)S(1)}, f32[128,128]{1,0:T(8,128)S(1)}, u32[]{:S(2)}, u32[]{:S(2)}) collective-permute-start(f32[128,128]{1,0:T(8,128)S(1)} %collective-permute-done.4.refs_1_), channel_id=1, source_target_pairs={{0,8},{8,0},{1,9},{9,1},{2,10},{10,2},{3,11},{11,3},{4,12},{12,4},... | collective-permute-start | bytes 196616 | tf_op jit(solution)/shard_map/ppermute | solution.py:44
  28.7 6.2 %collective-permute-start.9 = (f32[128,128]{1,0:T(8,128)S(1)}, f32[128,128]{1,0:T(8,128)S(1)}, u32[]{:S(2)}, u32[]{:S(2)}) collective-permute-start(f32[128,128]{1,0:T(8,128)S(1)} %collective-permute-done.5.refs_2_), channel_id=1, source_target_pairs={{0,8},{8,0},{1,9},{9,1},{2,10},{10,2},{3,11},{11,3},{4,12},{12,4},... | collective-permute-start | bytes 196616 | tf_op jit(solution)/shard_map/ppermute | solution.py:44
  31.5 3.4 %collective-permute-start.10 = (f32[128,128]{1,0:T(8,128)S(1)}, f32[128,128]{1,0:T(8,128)S(1)}, u32[]{:S(2)}, u32[]{:S(2)}) collective-permute-start(f32[128,128]{1,0:T(8,128)S(1)} %collective-permute-done.6.refs_3_), channel_id=1, source_target_pairs={{0,8},{8,0},{1,9},{9,1},{2,10},{10,2},{3,11},{11,3},{4,12},{12,4},... | collective-permute-start | bytes 196616 | tf_op jit(solution)/shard_map/ppermute | solution.py:44
  34.9 8.5 %copy-start = (s32[128,128]{1,0:T(8,128)S(1)}, s32[128,128]{1,0:T(8,128)}, u32[]{:S(2)}) copy-start(s32[128,128]{1,0:T(8,128)} %mask_ref.1) | copy-start | bytes 196612
  36.0 5.0 %collective-permute-start.14 = (f32[136,128]{1,0:T(8,128)S(1)}, f32[136,128]{1,0:T(8,128)S(1)}, u32[]{:S(2)}, u32[]{:S(2)}) collective-permute-start(f32[136,128]{1,0:T(8,128)S(1)} %get-tuple-element.41.refs_9_), channel_id=1, source_target_pairs={{192,0},{0,64},{64,128},{128,192},{193,1},{1,65},{65,129},{129,193... | collective-permute-start | bytes 208904 | tf_op jit(solution)/shard_map/ppermute | solution.py:29
  37.1 6.4 %collective-permute-start.15 = (f32[136,128]{1,0:T(8,128)S(1)}, f32[136,128]{1,0:T(8,128)S(1)}, u32[]{:S(2)}, u32[]{:S(2)}) collective-permute-start(f32[136,128]{1,0:T(8,128)S(1)} %get-tuple-element.42.refs_10_), channel_id=1, source_target_pairs={{128,0},{192,64},{0,128},{64,192},{129,1},{193,65},{1,129},{65,193... | collective-permute-start | bytes 208904 | tf_op jit(solution)/shard_map/ppermute | solution.py:29
  39.7 3.8 %collective-permute-start.16 = (f32[136,128]{1,0:T(8,128)S(1)}, f32[136,128]{1,0:T(8,128)S(1)}, u32[]{:S(2)}, u32[]{:S(2)}) collective-permute-start(f32[136,128]{1,0:T(8,128)S(1)} %get-tuple-element.43.refs_11_), channel_id=1, source_target_pairs={{64,0},{128,64},{192,128},{0,192},{65,1},{129,65},{193,129},{1,193... | collective-permute-start | bytes 208904 | tf_op jit(solution)/shard_map/ppermute | solution.py:29
  43.5 3.6 %collective-permute-start.17 = (f32[136,128]{1,0:T(8,128)S(1)}, f32[136,128]{1,0:T(8,128)S(1)}, u32[]{:S(2)}, u32[]{:S(2)}) collective-permute-start(f32[136,128]{1,0:T(8,128)S(1)} %shard_map.90.own_ref.refs_16_.image_ref), channel_id=1, source_target_pairs={{0,1},{1,0},{2,3},{3,2},{4,5},{5,4},{6,7},{7,6},{8,9},{9,8},{10,11... | collective-permute-start | bytes 208904 | tf_op jit(solution)/shard_map/ppermute | solution.py:40
  47.4 10.4 %collective-permute-start.19 = (f32[136,128]{1,0:T(8,128)S(1)}, f32[136,128]{1,0:T(8,128)S(1)}, u32[]{:S(2)}, u32[]{:S(2)}) collective-permute-start(f32[136,128]{1,0:T(8,128)S(1)} %get-tuple-element.46), channel_id=1, source_target_pairs={{6,0},{0,2},{2,4},{4,6},{7,1},{1,3},{3,5},{5,7},{14,8},{8,10},{10,... | collective-permute-start | bytes 208904 | tf_op jit(solution)/shard_map/ppermute | solution.py:29
  48.1 9.7 %collective-permute-start.20 = (f32[136,128]{1,0:T(8,128)S(1)}, f32[136,128]{1,0:T(8,128)S(1)}, u32[]{:S(2)}, u32[]{:S(2)}) collective-permute-start(f32[136,128]{1,0:T(8,128)S(1)} %get-tuple-element.47), channel_id=1, source_target_pairs={{2,0},{4,2},{6,4},{0,6},{3,1},{5,3},{7,5},{1,7},{10,8},{12,10},{14... | collective-permute-start | bytes 208904 | tf_op jit(solution)/shard_map/ppermute | solution.py:29
  51.1 7.3 %collective-permute-start.18 = (f32[136,128]{1,0:T(8,128)S(1)}, f32[136,128]{1,0:T(8,128)S(1)}, u32[]{:S(2)}, u32[]{:S(2)}) collective-permute-start(f32[136,128]{1,0:T(8,128)S(1)} %get-tuple-element.45), channel_id=1, source_target_pairs={{4,0},{6,2},{0,4},{2,6},{5,1},{7,3},{1,5},{3,7},{12,8},{14,10},{8,... | collective-permute-start | bytes 208904 | tf_op jit(solution)/shard_map/ppermute | solution.py:29
  55.4 4.9 %collective-permute-start.28 = (f32[136,128]{1,0:T(8,128)S(1)}, f32[136,128]{1,0:T(8,128)S(1)}, u32[]{:S(2)}, u32[]{:S(2)}) collective-permute-start(f32[136,128]{1,0:T(8,128)S(1)} %shard_map.90.own_ref.refs_16_.image_ref), channel_id=1, source_target_pairs={{64,0},{128,64},{192,128},{0,192},{65,1},{129,65},{193,129},{1,193... | collective-permute-start | bytes 208904 | tf_op jit(solution)/shard_map/ppermute | solution.py:29
  57.1 4.7 %collective-permute-start.29 = (f32[136,128]{1,0:T(8,128)S(1)}, f32[136,128]{1,0:T(8,128)S(1)}, u32[]{:S(2)}, u32[]{:S(2)}) collective-permute-start(f32[136,128]{1,0:T(8,128)S(1)} %shard_map.90.own_ref.refs_16_.image_ref), channel_id=1, source_target_pairs={{128,0},{192,64},{0,128},{64,192},{129,1},{193,65},{1,129},{65,193... | collective-permute-start | bytes 208904 | tf_op jit(solution)/shard_map/ppermute | solution.py:29
  58.3 9.0 %collective-permute-start.21 = (f32[136,128]{1,0:T(8,128)S(1)}, f32[136,128]{1,0:T(8,128)S(1)}, u32[]{:S(2)}, u32[]{:S(2)}) collective-permute-start(f32[136,128]{1,0:T(8,128)S(1)} %add_add_fusion.refs_0_), channel_id=1, source_target_pairs={{16,0},{32,16},{48,32},{0,48},{17,1},{33,17},{49,33},{1,49},{18,2}... | collective-permute-start | bytes 208904 | tf_op jit(solution)/shard_map/ppermute | solution.py:29
  58.6 8.7 %collective-permute-start.22 = (f32[136,128]{1,0:T(8,128)S(1)}, f32[136,128]{1,0:T(8,128)S(1)}, u32[]{:S(2)}, u32[]{:S(2)}) collective-permute-start(f32[136,128]{1,0:T(8,128)S(1)} %add_add_fusion.refs_0_), channel_id=1, source_target_pairs={{32,0},{48,16},{0,32},{16,48},{33,1},{49,17},{1,33},{17,49},{34,2}... | collective-permute-start | bytes 208904 | tf_op jit(solution)/shard_map/ppermute | solution.py:29
  59.5 8.9 %collective-permute-start.23 = (f32[136,128]{1,0:T(8,128)S(1)}, f32[136,128]{1,0:T(8,128)S(1)}, u32[]{:S(2)}, u32[]{:S(2)}) collective-permute-start(f32[136,128]{1,0:T(8,128)S(1)} %add_add_fusion.refs_0_), channel_id=1, source_target_pairs={{48,0},{0,16},{16,32},{32,48},{49,1},{1,17},{17,33},{33,49},{50,2}... | collective-permute-start | bytes 208904 | tf_op jit(solution)/shard_map/ppermute | solution.py:29
  60.3 8.9 %collective-permute-start.30 = (f32[136,128]{1,0:T(8,128)S(1)}, f32[136,128]{1,0:T(8,128)S(1)}, u32[]{:S(2)}, u32[]{:S(2)}) collective-permute-start(f32[136,128]{1,0:T(8,128)S(1)} %shard_map.90.own_ref.refs_16_.image_ref), channel_id=1, source_target_pairs={{192,0},{0,64},{64,128},{128,192},{193,1},{1,65},{65,129},{129,193... | collective-permute-start | bytes 208904 | tf_op jit(solution)/shard_map/ppermute | solution.py:29
  61.8 7.5 %collective-permute-start.24 = (f32[136,128]{1,0:T(8,128)S(1)}, f32[136,128]{1,0:T(8,128)S(1)}, u32[]{:S(2)}, u32[]{:S(2)}) collective-permute-start(f32[136,128]{1,0:T(8,128)S(1)} %add_add_fusion.refs_0_), channel_id=1, source_target_pairs={{0,8},{8,0},{1,9},{9,1},{2,10},{10,2},{3,11},{11,3},{4,12},{12,4},... | collective-permute-start | bytes 208904 | tf_op jit(solution)/shard_map/ppermute | solution.py:44
  67.3 1.9 %collective-permute-start.25 = (f32[136,128]{1,0:T(8,128)S(1)}, f32[136,128]{1,0:T(8,128)S(1)}, u32[]{:S(2)}, u32[]{:S(2)}) collective-permute-start(f32[136,128]{1,0:T(8,128)S(1)} %collective-permute-done.21.refs_1_), channel_id=1, source_target_pairs={{0,8},{8,0},{1,9},{9,1},{2,10},{10,2},{3,11},{11,3},{4,12},{12,4},... | collective-permute-start | bytes 208904 | tf_op jit(solution)/shard_map/ppermute | solution.py:44
  67.3 2.0 %collective-permute-start.26 = (f32[136,128]{1,0:T(8,128)S(1)}, f32[136,128]{1,0:T(8,128)S(1)}, u32[]{:S(2)}, u32[]{:S(2)}) collective-permute-start(f32[136,128]{1,0:T(8,128)S(1)} %collective-permute-done.22.refs_2_), channel_id=1, source_target_pairs={{0,8},{8,0},{1,9},{9,1},{2,10},{10,2},{3,11},{11,3},{4,12},{12,4},... | collective-permute-start | bytes 208904 | tf_op jit(solution)/shard_map/ppermute | solution.py:44
  68.5 1.7 %collective-permute-start.27 = (f32[136,128]{1,0:T(8,128)S(1)}, f32[136,128]{1,0:T(8,128)S(1)}, u32[]{:S(2)}, u32[]{:S(2)}) collective-permute-start(f32[136,128]{1,0:T(8,128)S(1)} %collective-permute-done.23.refs_3_), channel_id=1, source_target_pairs={{0,8},{8,0},{1,9},{9,1},{2,10},{10,2},{3,11},{11,3},{4,12},{12,4},... | collective-permute-start | bytes 208904 | tf_op jit(solution)/shard_map/ppermute | solution.py:44
  72.0 11.2 %copy-start.2 = (f32[2,4096]{1,0:T(2,128)S(1)}, f32[2,4096]{1,0:T(2,128)}, u32[]{:S(2)}) copy-start(f32[2,4096]{1,0:T(2,128)} %tests_ref.1) | copy-start | bytes 98308
  72.0 11.2 %copy-start.3 = (s32[4096]{0:T(1024)S(1)}, s32[4096]{0:T(1024)}, u32[]{:S(2)}) copy-start(s32[4096]{0:T(1024)} %param.13) | copy-start | bytes 49156
  72.0 27.1 %all-to-all-start = ((f32[256,1,128]{2,1,0:T(1,128)}), f32[256,1,128]{2,1,0:T(1,128)S(1)}, u32[]{:S(2)}, u32[]{:S(2)}) async-start(f32[256,1,128]{2,1,0:T(1,128)} %get-tuple-element.48), calls=%async_computation | async-start | bytes 262144 | tf_op jit(solution)/shard_map/all_to_all | solution.py:301
  88.8 5.7 %collective-permute-start.31 = (f32[128,256]{1,0:T(8,128)S(1)}, f32[128,256]{1,0:T(8,128)S(1)}, u32[]{:S(2)}, u32[]{:S(2)}) collective-permute-start(f32[128,256]{1,0:T(8,128)S(1)} %get-tuple-element.57), channel_id=1, source_target_pairs={{192,0},{0,64},{64,128},{128,192},{193,1},{1,65},{65,129},{129,193... | collective-permute-start | bytes 393224 | tf_op jit(solution)/shard_map/ppermute | solution.py:29
  90.2 8.9 %collective-permute-start.32 = (f32[128,256]{1,0:T(8,128)S(1)}, f32[128,256]{1,0:T(8,128)S(1)}, u32[]{:S(2)}, u32[]{:S(2)}) collective-permute-start(f32[128,256]{1,0:T(8,128)S(1)} %get-tuple-element.58), channel_id=1, source_target_pairs={{128,0},{192,64},{0,128},{64,192},{129,1},{193,65},{1,129},{65,193... | collective-permute-start | bytes 393224 | tf_op jit(solution)/shard_map/ppermute | solution.py:29
  92.7 6.4 %collective-permute-start.33 = (f32[128,256]{1,0:T(8,128)S(1)}, f32[128,256]{1,0:T(8,128)S(1)}, u32[]{:S(2)}, u32[]{:S(2)}) collective-permute-start(f32[128,256]{1,0:T(8,128)S(1)} %get-tuple-element.59), channel_id=1, source_target_pairs={{64,0},{128,64},{192,128},{0,192},{65,1},{129,65},{193,129},{1,193... | collective-permute-start | bytes 393224 | tf_op jit(solution)/shard_map/ppermute | solution.py:29

commit v5 on v4

--- a/solution.py
+++ b/solution.py
@@ -243,7 +243,19 @@
     known_ref[...] = side_by_side([step, norm, first])
 
 
-def field_kernel(*refs):
+def start_field_kernel(*refs):
+    folds, image_ref, high_ref, low_ref = refs[:8], *refs[8:11]
+    (own_ref, *outs), right_high, right_low = refs[11:15], *refs[15:]
+    stack(folds, right_high, right_low)
+    for r, out in enumerate([own_ref] + outs[::-1]):
+        rows = slice(r * TILE, (r + 1) * TILE)
+        part = applied(high_ref, low_ref, rows, right_high[...], right_low[...])
+        out[out.shape[0] - TILE :, :] = part
+        if r > 0:
+            out[: TILE + 8, :] = image_ref[...]
+
+
+def image_field_kernel(*refs):
     folds, high_ref, low_ref = refs[:8], *refs[8:10]
     outs, right_high, right_low = refs[10:14], *refs[14:]
     stack(folds, right_high, right_low)
@@ -252,18 +264,9 @@
         out[...] = applied(high_ref, low_ref, rows, right_high[...], right_low[...])
 
 
-def both_kernel(*refs):
-    folds, befores, high_ref, low_ref = refs[:8], refs[8:12], *refs[12:14]
-    outs, right_high, right_low = refs[14:18], *refs[18:]
-    stack(folds, right_high, right_low)
-    for r, out in enumerate(outs):
-        rows = slice(r * TILE, (r + 1) * TILE)
-        out[:, :TILE] = befores[r][...]
-        out[:, TILE:] = applied(high_ref, low_ref, rows, right_high[...], right_low[...])
-
-
 def last_kernel(sums_ref, known_ref, start_ref, image_ref, *refs):
-    (a, b, c, d), (estimate_ref, field_ref) = refs[:4], refs[4:]
+    (a, b, c, d), (e, f, g, h), (estimate_ref, field_ref) = refs[:4], refs[4:8], refs[8:]
+    tail = slice(TILE + 8, None)
     sums = jnp.sum(sums_ref[...], axis=0)
     norm_next, curved, crossed = sums[:, 0:1], sums[:, 1:2], sums[:, 2:3]
     step, norm, first = known_ref[:, 0:1], known_ref[:, 1:2], known_ref[:, 2:3]
@@ -272,8 +275,8 @@
     start, image = start_ref[...], image_ref[:TILE, :]
     direction = (start - step * image) + follow * start
     estimate_ref[...] = step * start + step_next * direction
-    fields = (a[...] + b[...]) + (c[...] + d[...])
-    of_start, of_image = fields[:, :TILE], fields[:, TILE:]
+    of_start = (a[...] + b[tail, :]) + (c[tail, :] + d[tail, :])
+    of_image = (e[...] + f[...]) + (g[...] + h[...])
     turned = (of_start - step * of_image) + follow * of_start
     field_ref[...] = (step * of_start + step_next * turned) * amplitude
 
@@ -373,17 +376,19 @@
         flops=10 * TILE * TILE,
     )
     other = neighbours(image)
-    image_rows = gathered(image, "loc_0", (3, 2, 1))
     image_fold = folded(image, other)
-    start_fields = call(
-        field_kernel,
-        [square] * 4,
+    start_field, *pieces = call(
+        start_field_kernel,
+        [square] + [((2 * TILE + 8, TILE), f32)] * 3,
         *start_folds,
+        image,
         test_high,
         test_low,
         flops=one_product,
         scratch=right,
     )
+    others = [ahead(piece, "loc_0", s) for s, piece in enumerate(pieces, 1)]
+    image_rows = [image] + others
     image_folds = columns(image_fold)
     size = lax.axis_size(EVERYONE)
     sums, known = call(
@@ -401,10 +406,9 @@
     )
     sums = exchanged(sums, EVERYONE)
     fields = call(
-        both_kernel,
-        [((TILE, 2 * TILE), f32)] * 4,
+        image_field_kernel,
+        [square] * 4,
         *image_folds,
-        *start_fields,
         test_high,
         test_low,
         flops=one_product,
@@ -418,6 +422,8 @@
             known,
             start,
             image,
+            start_field,
+            *others,
             *to_owners(fields),
             flops=20 * TILE * TILE,
         )

time: 100 us -> 98.6 us (0.986)
  starting transfers between devices: 71.8 us -> 66.3 us
  waiting for transfers between devices: 13.3 us -> 16.9 us
    all_to_all x1, waiting for transfers between devices: 0.01 us -> 4.33 us  [exchanged(): return lax.all_to_all(copies, axes, split_axis=0, concat_axis=0, tiled=True)]
    ppermute x8, starting transfers between devices: 14.9 us -> 11.3 us  [swapped(): return lax.ppermute(block, 'loc_2', [(0, 1), (1, 0)])]
    all_to_all x1, starting transfers between devices: 11.2 us -> 9.73 us  [exchanged(): return lax.all_to_all(copies, axes, split_axis=0, concat_axis=0, tiled=True)]
    ppermute x24, waiting for transfers between devices: 9.38 us -> 8.01 us  [ahead(): lax.ppermute(block, axis, [((i + shift) % size, i) for i in range(size)])]
  transfers between devices with their start and end apart: 35 -> 35, of which waited for: 11 -> 10; matrix products, arithmetic and copies ran while one was open for 0% -> 0% of each run, Pallas kernels for 9% -> 9%
where the time goes in v5:
time: 98.6 us; the launch traced here: 98.5 us
  starting transfers between devices  66.3 us (67%)
  waiting for transfers between devices  16.9 us (17%)
  Pallas kernels  13.4 us (14%)
    ppermute x24, starting transfers between devices, ahead(): lax.ppermute(block, axis, [((i + shift) % size, i) for i in range(size)])  41.9 us
    pallas_call x11, Pallas kernels, call(): pl.pallas_call(kernel, out_shape=shapes, in_specs=[VMEM] * len(args), out...  13.4 us
    ppermute x8, starting transfers between devices, swapped(): return lax.ppermute(block, 'loc_2', [(0, 1), (1, 0)])  11.3 us
    all_to_all x1, starting transfers between devices, exchanged(): return lax.all_to_all(copies, axes, split_axis=0, concat_axis=0, tiled=True)  9.73 us
    ppermute x24, waiting for transfers between devices, ahead(): lax.ppermute(block, axis, [((i + shift) % size, i) for i in range(size)])  8.01 us
    all_to_all x1, waiting for transfers between devices, exchanged(): return lax.all_to_all(copies, axes, split_axis=0, concat_axis=0, tiled=True)  4.33 us
    ppermute x2, waiting for transfers between devices, neighbours(): return lax.ppermute(block, 'tm_1', [(0, 1), (1, 0)])  3.65 us
    ppermute x2, starting transfers between devices, neighbours(): return lax.ppermute(block, 'tm_1', [(0, 1), (1, 0)])  3.43 us
  transfers between devices with their start and end apart: 35, of which 10 were waited for; matrix products, arithmetic and copies ran while one was open for 0% of the time, Pallas kernels for 9%

profile of v5, /device:TPU:1, one launch (start us, length us, event | category | flops | bytes accessed | tf_op | source)
XLA Modules:
  0.0 98.5 jit_solution(5710121560723302244)
XLA Ops:
  0.6 0.9 convert_multiply_fusion.own_ref.refs_8_.start_ref.refs_12_
  1.5 2.5 %collective-permute-start = (f32[128,128]{1,0:T(8,128)S(1)}, f32[128,128]{1,0:T(8,128)S(1)}, u32[]{:S(2)}, u32[]{:S(2)}) collective-permute-start(f32[128,128]{1,0:T(8,128)S(1)} %convert_multiply_fusion.own_ref.refs_8_.start_ref.refs_12_), channel_id=1, source_target_pairs={{0,1},{1,0},{2,3},{3,2},{4,5},{5,4},{6,7},{7,6},{8,9},{9,8},{10,11... | collective-permute-start | bytes 196616 | tf_op jit(solution)/shard_map/ppermute | solution.py:40
  4.1 0.4 shard_map.86
  4.4 1.3 %collective-permute-done.other_ref = f32[128,128]{1,0:T(8,128)S(1)} collective-permute-done((f32[128,128]{1,0:T(8,128)S(1)}, f32[128,128]{1,0:T(8,128)S(1)}, u32[]{:S(2)}, u32[]{:S(2)}) %collective-permute-start) | collective-permute-done | bytes 65568 | tf_op jit(solution)/shard_map/ppermute | solution.py:40
  5.7 0.4 shard_map.87
  6.1 6.8 %collective-permute-start.1 = (f32[128,128]{1,0:T(8,128)S(1)}, f32[128,128]{1,0:T(8,128)S(1)}, u32[]{:S(2)}, u32[]{:S(2)}) collective-permute-start(f32[128,128]{1,0:T(8,128)S(1)} %get-tuple-element.34), channel_id=1, source_target_pairs={{4,0},{6,2},{0,4},{2,6},{5,1},{7,3},{1,5},{3,7},{12,8},{14,10},{8,... | collective-permute-start | bytes 196616 | tf_op jit(solution)/shard_map/ppermute | solution.py:29
  12.9 1.2 %collective-permute-start.2 = (f32[128,128]{1,0:T(8,128)S(1)}, f32[128,128]{1,0:T(8,128)S(1)}, u32[]{:S(2)}, u32[]{:S(2)}) collective-permute-start(f32[128,128]{1,0:T(8,128)S(1)} %get-tuple-element.35), channel_id=1, source_target_pairs={{6,0},{0,2},{2,4},{4,6},{7,1},{1,3},{3,5},{5,7},{14,8},{8,10},{10,... | collective-permute-start | bytes 196616 | tf_op jit(solution)/shard_map/ppermute | solution.py:29
  14.1 2.4 %collective-permute-start.3 = (f32[128,128]{1,0:T(8,128)S(1)}, f32[128,128]{1,0:T(8,128)S(1)}, u32[]{:S(2)}, u32[]{:S(2)}) collective-permute-start(f32[128,128]{1,0:T(8,128)S(1)} %get-tuple-element.36), channel_id=1, source_target_pairs={{2,0},{4,2},{6,4},{0,6},{3,1},{5,3},{7,5},{1,7},{10,8},{12,10},{14... | collective-permute-start | bytes 196616 | tf_op jit(solution)/shard_map/ppermute | solution.py:29
  16.5 1.3 %collective-permute-start.13 = (f32[128,128]{1,0:T(8,128)S(1)}, f32[128,128]{1,0:T(8,128)S(1)}, u32[]{:S(2)}, u32[]{:S(2)}) collective-permute-start(f32[128,128]{1,0:T(8,128)S(1)} %convert_multiply_fusion.own_ref.refs_8_.start_ref.refs_12_), channel_id=1, source_target_pairs={{192,0},{0,64},{64,128},{128,192},{193,1},{1,65},{65,129},{129,193... | collective-permute-start | bytes 196616 | tf_op jit(solution)/shard_map/ppermute | solution.py:29
  17.8 2.6 %collective-permute-start.12 = (f32[128,128]{1,0:T(8,128)S(1)}, f32[128,128]{1,0:T(8,128)S(1)}, u32[]{:S(2)}, u32[]{:S(2)}) collective-permute-start(f32[128,128]{1,0:T(8,128)S(1)} %convert_multiply_fusion.own_ref.refs_8_.start_ref.refs_12_), channel_id=1, source_target_pairs={{128,0},{192,64},{0,128},{64,192},{129,1},{193,65},{1,129},{65,193... | collective-permute-start | bytes 196616 | tf_op jit(solution)/shard_map/ppermute | solution.py:29
  20.5 1.3 %collective-permute-start.6 = (f32[128,128]{1,0:T(8,128)S(1)}, f32[128,128]{1,0:T(8,128)S(1)}, u32[]{:S(2)}, u32[]{:S(2)}) collective-permute-start(f32[128,128]{1,0:T(8,128)S(1)} %add_add_fusion.1.refs_0_), channel_id=1, source_target_pairs={{48,0},{0,16},{16,32},{32,48},{49,1},{1,17},{17,33},{33,49},{50,2}... | collective-permute-start | bytes 196616 | tf_op jit(solution)/shard_map/ppermute | solution.py:29
  21.8 2.4 %collective-permute-start.5 = (f32[128,128]{1,0:T(8,128)S(1)}, f32[128,128]{1,0:T(8,128)S(1)}, u32[]{:S(2)}, u32[]{:S(2)}) collective-permute-start(f32[128,128]{1,0:T(8,128)S(1)} %add_add_fusion.1.refs_0_), channel_id=1, source_target_pairs={{32,0},{48,16},{0,32},{16,48},{33,1},{49,17},{1,33},{17,49},{34,2}... | collective-permute-start | bytes 196616 | tf_op jit(solution)/shard_map/ppermute | solution.py:29
  24.2 1.2 %collective-permute-start.4 = (f32[128,128]{1,0:T(8,128)S(1)}, f32[128,128]{1,0:T(8,128)S(1)}, u32[]{:S(2)}, u32[]{:S(2)}) collective-permute-start(f32[128,128]{1,0:T(8,128)S(1)} %add_add_fusion.1.refs_0_), channel_id=1, source_target_pairs={{16,0},{32,16},{48,32},{0,48},{17,1},{33,17},{49,33},{1,49},{18,2}... | collective-permute-start | bytes 196616 | tf_op jit(solution)/shard_map/ppermute | solution.py:29
  25.4 2.1 %collective-permute-start.11 = (f32[128,128]{1,0:T(8,128)S(1)}, f32[128,128]{1,0:T(8,128)S(1)}, u32[]{:S(2)}, u32[]{:S(2)}) collective-permute-start(f32[128,128]{1,0:T(8,128)S(1)} %convert_multiply_fusion.own_ref.refs_8_.start_ref.refs_12_), channel_id=1, source_target_pairs={{64,0},{128,64},{192,128},{0,192},{65,1},{129,65},{193,129},{1,193... | collective-permute-start | bytes 196616 | tf_op jit(solution)/shard_map/ppermute | solution.py:29
  27.5 3.3 %collective-permute-start.7 = (f32[128,128]{1,0:T(8,128)S(1)}, f32[128,128]{1,0:T(8,128)S(1)}, u32[]{:S(2)}, u32[]{:S(2)}) collective-permute-start(f32[128,128]{1,0:T(8,128)S(1)} %add_add_fusion.1.refs_0_), channel_id=1, source_target_pairs={{0,8},{8,0},{1,9},{9,1},{2,10},{10,2},{3,11},{11,3},{4,12},{12,4},... | collective-permute-start | bytes 196616 | tf_op jit(solution)/shard_map/ppermute | solution.py:44
  30.9 0.4 collective-permute-start.9
  31.3 0.9 collective-permute-start.8
  32.3 2.7 %shard_map.88 = (bf16[512,1024]{1,0:T(8,128)(2,1)S(1)}, bf16[512,1024]{1,0:T(8,128)(2,1)S(1)}, f32[1,128]{1,0:T(1,128)S(1)}) custom-call(f32[2,4096]{1,0:T(2,128)S(1)} %copy-done.1, f32[1,128]{1,0:T(1,128)S(1)} %bitcast.5), custom_call_target="tpu_custom_call" | custom-call | flops 209715200 | bytes 2130944 | tf_op jit(solution)/shard_map/pallas_call | solution.py:59
  35.0 1.1 %shard_map.89 = (f32[136,128]{1,0:T(8,128)S(1)}, f32[136,128]{1,0:T(8,128)S(1)}, f32[136,128]{1,0:T(8,128)S(1)}, f32[136,128]{1,0:T(8,128)S(1)}) custom-call(f32[128,128]{1,0:T(8,128)S(1)} %add_add_fusion.1.refs_0_, f32[128,128]{1,0:T(8,128)S(1)} %collective-permute-done.4.refs_1_, f32[128,128]{1,0:T(8,128)S(1)} %collective-permute-done.5.refs_2_, ...), custom_call_target="tpu_custom_call" | custom-call | flops 402653184 | bytes 3162624 | tf_op jit(solution)/shard_map/pallas_call | solution.py:59
  36.2 2.2 %collective-permute-start.15 = (f32[136,128]{1,0:T(8,128)S(1)}, f32[136,128]{1,0:T(8,128)S(1)}, u32[]{:S(2)}, u32[]{:S(2)}) collective-permute-start(f32[136,128]{1,0:T(8,128)S(1)} %get-tuple-element.42.refs_10_), channel_id=1, source_target_pairs={{128,0},{192,64},{0,128},{64,192},{129,1},{193,65},{1,129},{65,193... | collective-permute-start | bytes 208904 | tf_op jit(solution)/shard_map/ppermute | solution.py:29
  38.4 1.0 %collective-permute-start.16 = (f32[136,128]{1,0:T(8,128)S(1)}, f32[136,128]{1,0:T(8,128)S(1)}, u32[]{:S(2)}, u32[]{:S(2)}) collective-permute-start(f32[136,128]{1,0:T(8,128)S(1)} %get-tuple-element.43.refs_11_), channel_id=1, source_target_pairs={{64,0},{128,64},{192,128},{0,192},{65,1},{129,65},{193,129},{1,193... | collective-permute-start | bytes 208904 | tf_op jit(solution)/shard_map/ppermute | solution.py:29
  39.4 2.1 %collective-permute-done.14.b = f32[136,128]{1,0:T(8,128)S(1)} collective-permute-done((f32[136,128]{1,0:T(8,128)S(1)}, f32[136,128]{1,0:T(8,128)S(1)}, u32[]{:S(2)}, u32[]{:S(2)}) %collective-permute-start.14) | collective-permute-done | bytes 69664 | tf_op jit(solution)/shard_map/ppermute | solution.py:29
  41.5 0.6 collective-permute-done.15.c
  42.2 0.7 collective-permute-done.16.d
  43.0 0.9 collective-permute-start.17
  43.9 2.4 %collective-permute-done.17.other_ref = f32[136,128]{1,0:T(8,128)S(1)} collective-permute-done((f32[136,128]{1,0:T(8,128)S(1)}, f32[136,128]{1,0:T(8,128)S(1)}, u32[]{:S(2)}, u32[]{:S(2)}) %collective-permute-start.17) | collective-permute-done | bytes 69664 | tf_op jit(solution)/shard_map/ppermute | solution.py:40
  46.2 0.4 shard_map.91
  46.6 2.6 %collective-permute-start.18 = (f32[136,128]{1,0:T(8,128)S(1)}, f32[136,128]{1,0:T(8,128)S(1)}, u32[]{:S(2)}, u32[]{:S(2)}) collective-permute-start(f32[136,128]{1,0:T(8,128)S(1)} %get-tuple-element.45), channel_id=1, source_target_pairs={{4,0},{6,2},{0,4},{2,6},{5,1},{7,3},{1,5},{3,7},{12,8},{14,10},{8,... | collective-permute-start | bytes 208904 | tf_op jit(solution)/shard_map/ppermute | solution.py:29
  49.2 3.3 %collective-permute-start.19 = (f32[136,128]{1,0:T(8,128)S(1)}, f32[136,128]{1,0:T(8,128)S(1)}, u32[]{:S(2)}, u32[]{:S(2)}) collective-permute-start(f32[136,128]{1,0:T(8,128)S(1)} %get-tuple-element.46), channel_id=1, source_target_pairs={{6,0},{0,2},{2,4},{4,6},{7,1},{1,3},{3,5},{5,7},{14,8},{8,10},{10,... | collective-permute-start | bytes 208904 | tf_op jit(solution)/shard_map/ppermute | solution.py:29
  52.7 3.5 %shard_map.92 = (bf16[512,1024]{1,0:T(8,128)(2,1)S(1)}, bf16[512,1024]{1,0:T(8,128)(2,1)S(1)}) custom-call(f32[2,4096]{1,0:T(2,128)S(1)} %copy-done.1, f32[2,4096]{1,0:T(2,128)S(1)} %copy-done.2, s32[32,128]{1,0:T(8,128)S(1)} %bitcast.3), custom_call_target="tpu_custom_call" | custom-call | flops 314572800 | bytes 2179072 | tf_op jit(solution)/shard_map/pallas_call | solution.py:59
  56.2 1.0 %shard_map.93 = (f32[128,128]{1,0:T(8,128)S(1)}, f32[264,128]{1,0:T(8,128)S(1)}, f32[264,128]{1,0:T(8,128)S(1)}, f32[264,128]{1,0:T(8,128)S(1)}) custom-call(f32[128,128]{1,0:T(8,128)S(1)} %add_add_fusion.1.refs_0_, f32[128,128]{1,0:T(8,128)S(1)} %collective-permute-done.4.refs_1_, f32[128,128]{1,0:T(8,128)S(1)} %collective-permute-done.5.refs_2_, ...), custom_call_target="tpu_custom_call" | custom-call | flops 402653184 | bytes 3162112 | tf_op jit(solution)/shard_map/pallas_call | solution.py:59
  57.3 2.6 %collective-permute-start.28 = (f32[264,128]{1,0:T(8,128)S(1)}, f32[264,128]{1,0:T(8,128)S(1)}, u32[]{:S(2)}, u32[]{:S(2)}) collective-permute-start(f32[264,128]{1,0:T(8,128)S(1)} %get-tuple-element.50), channel_id=1, source_target_pairs={{64,0},{128,64},{192,128},{0,192},{65,1},{129,65},{193,129},{1,193... | collective-permute-start | bytes 405512 | tf_op jit(solution)/shard_map/ppermute | solution.py:29
  59.9 0.6 collective-permute-start.29
  60.7 2.3 %collective-permute-start.22 = (f32[136,128]{1,0:T(8,128)S(1)}, f32[136,128]{1,0:T(8,128)S(1)}, u32[]{:S(2)}, u32[]{:S(2)}) collective-permute-start(f32[136,128]{1,0:T(8,128)S(1)} %add_add_fusion.refs_0_), channel_id=1, source_target_pairs={{32,0},{48,16},{0,32},{16,48},{33,1},{49,17},{1,33},{17,49},{34,2}... | collective-permute-start | bytes 208904 | tf_op jit(solution)/shard_map/ppermute | solution.py:29
  63.4 1.8 %collective-permute-done.29.refs_18_.refs_2_ = f32[264,128]{1,0:T(8,128)S(1)} collective-permute-done((f32[264,128]{1,0:T(8,128)S(1)}, f32[264,128]{1,0:T(8,128)S(1)}, u32[]{:S(2)}, u32[]{:S(2)}) %collective-permute-start.29) | collective-permute-done | bytes 135200 | tf_op jit(solution)/shard_map/ppermute | solution.py:29
  65.2 4.7 %collective-permute-start.24 = (f32[136,128]{1,0:T(8,128)S(1)}, f32[136,128]{1,0:T(8,128)S(1)}, u32[]{:S(2)}, u32[]{:S(2)}) collective-permute-start(f32[136,128]{1,0:T(8,128)S(1)} %add_add_fusion.refs_0_), channel_id=1, source_target_pairs={{0,8},{8,0},{1,9},{9,1},{2,10},{10,2},{3,11},{11,3},{4,12},{12,4},... | collective-permute-start | bytes 208904 | tf_op jit(solution)/shard_map/ppermute | solution.py:44
  69.9 0.6 collective-permute-start.26
  70.5 1.3 %collective-permute-start.25 = (f32[136,128]{1,0:T(8,128)S(1)}, f32[136,128]{1,0:T(8,128)S(1)}, u32[]{:S(2)}, u32[]{:S(2)}) collective-permute-start(f32[136,128]{1,0:T(8,128)S(1)} %collective-permute-done.21.refs_1_), channel_id=1, source_target_pairs={{0,8},{8,0},{1,9},{9,1},{2,10},{10,2},{3,11},{11,3},{4,12},{12,4},... | collective-permute-start | bytes 208904 | tf_op jit(solution)/shard_map/ppermute | solution.py:44
  71.8 0.9 collective-permute-done.25.refs_5_
  72.7 1.9 %shard_map.94 = (f32[256,1,128]{2,1,0:T(1,128)}, f32[1,128]{1,0:T(1,128)S(1)}) custom-call(f32[136,128]{1,0:T(8,128)S(1)} %add_add_fusion.refs_0_, f32[136,128]{1,0:T(8,128)S(1)} %collective-permute-done.21.refs_1_, f32[136,128]{1,0:T(8,128)S(1)} %collective-permute-done.22.refs_2_, f32[136,128]{1,0:T(8,128)S(1)} %collective-permute-done.23.refs_3_, ...), custom_call_target="tpu_custom_call" | custom-call | flops 402653184 | bytes 3802112 | tf_op jit(solution)/shard_map/pallas_call | solution.py:59
  74.6 9.7 %all-to-all-start = ((f32[256,1,128]{2,1,0:T(1,128)}), f32[256,1,128]{2,1,0:T(1,128)S(1)}, u32[]{:S(2)}, u32[]{:S(2)}) async-start(f32[256,1,128]{2,1,0:T(1,128)} %get-tuple-element.53), calls=%async_computation | async-start | bytes 262144 | tf_op jit(solution)/shard_map/all_to_all | solution.py:304
  84.3 1.0 %shard_map.95 = (f32[128,128]{1,0:T(8,128)S(1)}, f32[128,128]{1,0:T(8,128)S(1)}, f32[128,128]{1,0:T(8,128)S(1)}, f32[128,128]{1,0:T(8,128)S(1)}) custom-call(f32[136,128]{1,0:T(8,128)S(1)} %add_add_fusion.refs_0_, f32[136,128]{1,0:T(8,128)S(1)} %collective-permute-done.21.refs_1_, f32[136,128]{1,0:T(8,128)S(1)} %collective-permute-done.22.refs_2_, ...), custom_call_target="tpu_custom_call" | custom-call | flops 402653184 | bytes 2916352 | tf_op jit(solution)/shard_map/pallas_call | solution.py:59
  85.3 1.4 %collective-permute-start.31 = (f32[128,128]{1,0:T(8,128)S(1)}, f32[128,128]{1,0:T(8,128)S(1)}, u32[]{:S(2)}, u32[]{:S(2)}) collective-permute-start(f32[128,128]{1,0:T(8,128)S(1)} %get-tuple-element.57), channel_id=1, source_target_pairs={{192,0},{0,64},{64,128},{128,192},{193,1},{1,65},{65,129},{129,193... | collective-permute-start | bytes 196616 | tf_op jit(solution)/shard_map/ppermute | solution.py:29
  86.8 2.5 %collective-permute-start.32 = (f32[128,128]{1,0:T(8,128)S(1)}, f32[128,128]{1,0:T(8,128)S(1)}, u32[]{:S(2)}, u32[]{:S(2)}) collective-permute-start(f32[128,128]{1,0:T(8,128)S(1)} %get-tuple-element.58), channel_id=1, source_target_pairs={{128,0},{192,64},{0,128},{64,192},{129,1},{193,65},{1,129},{65,193... | collective-permute-start | bytes 196616 | tf_op jit(solution)/shard_map/ppermute | solution.py:29
  89.2 1.1 %collective-permute-start.33 = (f32[128,128]{1,0:T(8,128)S(1)}, f32[128,128]{1,0:T(8,128)S(1)}, u32[]{:S(2)}, u32[]{:S(2)}) collective-permute-start(f32[128,128]{1,0:T(8,128)S(1)} %get-tuple-element.59), channel_id=1, source_target_pairs={{64,0},{128,64},{192,128},{0,192},{65,1},{129,65},{193,129},{1,193... | collective-permute-start | bytes 196616 | tf_op jit(solution)/shard_map/ppermute | solution.py:29
  90.3 2.6 %collective-permute-done.32.refs_6_ = f32[128,128]{1,0:T(8,128)S(1)} collective-permute-done((f32[128,128]{1,0:T(8,128)S(1)}, f32[128,128]{1,0:T(8,128)S(1)}, u32[]{:S(2)}, u32[]{:S(2)}) %collective-permute-start.32) | collective-permute-done | bytes 65568 | tf_op jit(solution)/shard_map/ppermute | solution.py:29
  93.0 4.3 %all-to-all-done.sums_ref = f32[256,1,128]{2,1,0:T(1,128)S(1)} async-done(((f32[256,1,128]{2,1,0:T(1,128)}), f32[256,1,128]{2,1,0:T(1,128)S(1)}, u32[]{:S(2)}, u32[]{:S(2)}) %all-to-all-start) | async-done | bytes 131104 | tf_op jit(solution)/shard_map/all_to_all | solution.py:304
  97.3 1.2 %shard_map.96 = (f32[128,128]{1,0:T(8,128)}, f32[128,128]{1,0:T(8,128)}) custom-call(f32[256,1,128]{2,1,0:T(1,128)S(1)} %all-to-all-done.sums_ref, f32[1,128]{1,0:T(1,128)S(1)} %get-tuple-element.54.known_ref, f32[128,128]{1,0:T(8,128)S(1)} %convert_multiply_fusion.own_ref.refs_8_.start_ref.refs_12_, ...), custom_call_target="tpu_custom_call" | custom-call | flops 327680 | bytes 1131008 | tf_op jit(solution)/shard_map/pallas_call | solution.py:59
  (48 shorter events, 1.3 us)
Async XLA Ops:
  0.6 3.4 %copy-start.4 = (f32[1024]{0:T(1024)S(1)}, f32[1024]{0:T(1024)}, u32[]{:S(2)}) copy-start(f32[1024]{0:T(1024)} %param.10) | copy-start | bytes 12292
  1.5 4.2 %collective-permute-start = (f32[128,128]{1,0:T(8,128)S(1)}, f32[128,128]{1,0:T(8,128)S(1)}, u32[]{:S(2)}, u32[]{:S(2)}) collective-permute-start(f32[128,128]{1,0:T(8,128)S(1)} %convert_multiply_fusion.own_ref.refs_8_.start_ref.refs_12_), channel_id=1, source_target_pairs={{0,1},{1,0},{2,3},{3,2},{4,5},{5,4},{6,7},{7,6},{8,9},{9,8},{10,11... | collective-permute-start | bytes 196616 | tf_op jit(solution)/shard_map/ppermute | solution.py:40
  6.1 14.3 %collective-permute-start.1 = (f32[128,128]{1,0:T(8,128)S(1)}, f32[128,128]{1,0:T(8,128)S(1)}, u32[]{:S(2)}, u32[]{:S(2)}) collective-permute-start(f32[128,128]{1,0:T(8,128)S(1)} %get-tuple-element.34), channel_id=1, source_target_pairs={{4,0},{6,2},{0,4},{2,6},{5,1},{7,3},{1,5},{3,7},{12,8},{14,10},{8,... | collective-permute-start | bytes 196616 | tf_op jit(solution)/shard_map/ppermute | solution.py:29
  12.9 7.5 %collective-permute-start.2 = (f32[128,128]{1,0:T(8,128)S(1)}, f32[128,128]{1,0:T(8,128)S(1)}, u32[]{:S(2)}, u32[]{:S(2)}) collective-permute-start(f32[128,128]{1,0:T(8,128)S(1)} %get-tuple-element.35), channel_id=1, source_target_pairs={{6,0},{0,2},{2,4},{4,6},{7,1},{1,3},{3,5},{5,7},{14,8},{8,10},{10,... | collective-permute-start | bytes 196616 | tf_op jit(solution)/shard_map/ppermute | solution.py:29
  14.1 6.3 %collective-permute-start.3 = (f32[128,128]{1,0:T(8,128)S(1)}, f32[128,128]{1,0:T(8,128)S(1)}, u32[]{:S(2)}, u32[]{:S(2)}) collective-permute-start(f32[128,128]{1,0:T(8,128)S(1)} %get-tuple-element.36), channel_id=1, source_target_pairs={{2,0},{4,2},{6,4},{0,6},{3,1},{5,3},{7,5},{1,7},{10,8},{12,10},{14... | collective-permute-start | bytes 196616 | tf_op jit(solution)/shard_map/ppermute | solution.py:29
  16.5 8.9 %collective-permute-start.13 = (f32[128,128]{1,0:T(8,128)S(1)}, f32[128,128]{1,0:T(8,128)S(1)}, u32[]{:S(2)}, u32[]{:S(2)}) collective-permute-start(f32[128,128]{1,0:T(8,128)S(1)} %convert_multiply_fusion.own_ref.refs_8_.start_ref.refs_12_), channel_id=1, source_target_pairs={{192,0},{0,64},{64,128},{128,192},{193,1},{1,65},{65,129},{129,193... | collective-permute-start | bytes 196616 | tf_op jit(solution)/shard_map/ppermute | solution.py:29
  17.8 9.7 %collective-permute-start.12 = (f32[128,128]{1,0:T(8,128)S(1)}, f32[128,128]{1,0:T(8,128)S(1)}, u32[]{:S(2)}, u32[]{:S(2)}) collective-permute-start(f32[128,128]{1,0:T(8,128)S(1)} %convert_multiply_fusion.own_ref.refs_8_.start_ref.refs_12_), channel_id=1, source_target_pairs={{128,0},{192,64},{0,128},{64,192},{129,1},{193,65},{1,129},{65,193... | collective-permute-start | bytes 196616 | tf_op jit(solution)/shard_map/ppermute | solution.py:29
  20.4 11.8 %copy-start.1 = (f32[2,4096]{1,0:T(2,128)S(1)}, f32[2,4096]{1,0:T(2,128)}, u32[]{:S(2)}) copy-start(f32[2,4096]{1,0:T(2,128)} %sites_ref.3) | copy-start | bytes 98308
  20.5 11.8 %copy-start.5 = (f32[128]{0:T(128)S(1)}, f32[128]{0:T(128)}, u32[]{:S(2)}) copy-start(f32[128]{0:T(128)} %param.11) | copy-start | bytes 1540
  20.5 10.3 %collective-permute-start.6 = (f32[128,128]{1,0:T(8,128)S(1)}, f32[128,128]{1,0:T(8,128)S(1)}, u32[]{:S(2)}, u32[]{:S(2)}) collective-permute-start(f32[128,128]{1,0:T(8,128)S(1)} %add_add_fusion.1.refs_0_), channel_id=1, source_target_pairs={{48,0},{0,16},{16,32},{32,48},{49,1},{1,17},{17,33},{33,49},{50,2}... | collective-permute-start | bytes 196616 | tf_op jit(solution)/shard_map/ppermute | solution.py:29
  21.8 9.1 %collective-permute-start.5 = (f32[128,128]{1,0:T(8,128)S(1)}, f32[128,128]{1,0:T(8,128)S(1)}, u32[]{:S(2)}, u32[]{:S(2)}) collective-permute-start(f32[128,128]{1,0:T(8,128)S(1)} %add_add_fusion.1.refs_0_), channel_id=1, source_target_pairs={{32,0},{48,16},{0,32},{16,48},{33,1},{49,17},{1,33},{17,49},{34,2}... | collective-permute-start | bytes 196616 | tf_op jit(solution)/shard_map/ppermute | solution.py:29
  24.2 7.1 %collective-permute-start.4 = (f32[128,128]{1,0:T(8,128)S(1)}, f32[128,128]{1,0:T(8,128)S(1)}, u32[]{:S(2)}, u32[]{:S(2)}) collective-permute-start(f32[128,128]{1,0:T(8,128)S(1)} %add_add_fusion.1.refs_0_), channel_id=1, source_target_pairs={{16,0},{32,16},{48,32},{0,48},{17,1},{33,17},{49,33},{1,49},{18,2}... | collective-permute-start | bytes 196616 | tf_op jit(solution)/shard_map/ppermute | solution.py:29
  25.4 9.6 %collective-permute-start.11 = (f32[128,128]{1,0:T(8,128)S(1)}, f32[128,128]{1,0:T(8,128)S(1)}, u32[]{:S(2)}, u32[]{:S(2)}) collective-permute-start(f32[128,128]{1,0:T(8,128)S(1)} %convert_multiply_fusion.own_ref.refs_8_.start_ref.refs_12_), channel_id=1, source_target_pairs={{64,0},{128,64},{192,128},{0,192},{65,1},{129,65},{193,129},{1,193... | collective-permute-start | bytes 196616 | tf_op jit(solution)/shard_map/ppermute | solution.py:29
  27.5 7.5 %collective-permute-start.7 = (f32[128,128]{1,0:T(8,128)S(1)}, f32[128,128]{1,0:T(8,128)S(1)}, u32[]{:S(2)}, u32[]{:S(2)}) collective-permute-start(f32[128,128]{1,0:T(8,128)S(1)} %add_add_fusion.1.refs_0_), channel_id=1, source_target_pairs={{0,8},{8,0},{1,9},{9,1},{2,10},{10,2},{3,11},{11,3},{4,12},{12,4},... | collective-permute-start | bytes 196616 | tf_op jit(solution)/shard_map/ppermute | solution.py:44
  30.8 4.2 %collective-permute-start.10 = (f32[128,128]{1,0:T(8,128)S(1)}, f32[128,128]{1,0:T(8,128)S(1)}, u32[]{:S(2)}, u32[]{:S(2)}) collective-permute-start(f32[128,128]{1,0:T(8,128)S(1)} %collective-permute-done.6.refs_3_), channel_id=1, source_target_pairs={{0,8},{8,0},{1,9},{9,1},{2,10},{10,2},{3,11},{11,3},{4,12},{12,4},... | collective-permute-start | bytes 196616 | tf_op jit(solution)/shard_map/ppermute | solution.py:44
  30.9 4.1 %collective-permute-start.9 = (f32[128,128]{1,0:T(8,128)S(1)}, f32[128,128]{1,0:T(8,128)S(1)}, u32[]{:S(2)}, u32[]{:S(2)}) collective-permute-start(f32[128,128]{1,0:T(8,128)S(1)} %collective-permute-done.5.refs_2_), channel_id=1, source_target_pairs={{0,8},{8,0},{1,9},{9,1},{2,10},{10,2},{3,11},{11,3},{4,12},{12,4},... | collective-permute-start | bytes 196616 | tf_op jit(solution)/shard_map/ppermute | solution.py:44
  31.3 3.7 %collective-permute-start.8 = (f32[128,128]{1,0:T(8,128)S(1)}, f32[128,128]{1,0:T(8,128)S(1)}, u32[]{:S(2)}, u32[]{:S(2)}) collective-permute-start(f32[128,128]{1,0:T(8,128)S(1)} %collective-permute-done.4.refs_1_), channel_id=1, source_target_pairs={{0,8},{8,0},{1,9},{9,1},{2,10},{10,2},{3,11},{11,3},{4,12},{12,4},... | collective-permute-start | bytes 196616 | tf_op jit(solution)/shard_map/ppermute | solution.py:44
  35.0 7.9 %copy-start = (s32[128,128]{1,0:T(8,128)S(1)}, s32[128,128]{1,0:T(8,128)}, u32[]{:S(2)}) copy-start(s32[128,128]{1,0:T(8,128)} %mask_ref.1) | copy-start | bytes 196612
  36.1 5.4 %collective-permute-start.14 = (f32[136,128]{1,0:T(8,128)S(1)}, f32[136,128]{1,0:T(8,128)S(1)}, u32[]{:S(2)}, u32[]{:S(2)}) collective-permute-start(f32[136,128]{1,0:T(8,128)S(1)} %get-tuple-element.41.refs_9_), channel_id=1, source_target_pairs={{192,0},{0,64},{64,128},{128,192},{193,1},{1,65},{65,129},{129,193... | collective-permute-start | bytes 208904 | tf_op jit(solution)/shard_map/ppermute | solution.py:29
  36.2 6.0 %collective-permute-start.15 = (f32[136,128]{1,0:T(8,128)S(1)}, f32[136,128]{1,0:T(8,128)S(1)}, u32[]{:S(2)}, u32[]{:S(2)}) collective-permute-start(f32[136,128]{1,0:T(8,128)S(1)} %get-tuple-element.42.refs_10_), channel_id=1, source_target_pairs={{128,0},{192,64},{0,128},{64,192},{129,1},{193,65},{1,129},{65,193... | collective-permute-start | bytes 208904 | tf_op jit(solution)/shard_map/ppermute | solution.py:29
  38.4 4.5 %collective-permute-start.16 = (f32[136,128]{1,0:T(8,128)S(1)}, f32[136,128]{1,0:T(8,128)S(1)}, u32[]{:S(2)}, u32[]{:S(2)}) collective-permute-start(f32[136,128]{1,0:T(8,128)S(1)} %get-tuple-element.43.refs_11_), channel_id=1, source_target_pairs={{64,0},{128,64},{192,128},{0,192},{65,1},{129,65},{193,129},{1,193... | collective-permute-start | bytes 208904 | tf_op jit(solution)/shard_map/ppermute | solution.py:29
  42.9 9.8 %copy-start.2 = (f32[2,4096]{1,0:T(2,128)S(1)}, f32[2,4096]{1,0:T(2,128)}, u32[]{:S(2)}) copy-start(f32[2,4096]{1,0:T(2,128)} %tests_ref.1) | copy-start | bytes 98308
  43.0 9.8 %copy-start.3 = (s32[4096]{0:T(1024)S(1)}, s32[4096]{0:T(1024)}, u32[]{:S(2)}) copy-start(s32[4096]{0:T(1024)} %param.13) | copy-start | bytes 49156
  43.0 3.2 %collective-permute-start.17 = (f32[136,128]{1,0:T(8,128)S(1)}, f32[136,128]{1,0:T(8,128)S(1)}, u32[]{:S(2)}, u32[]{:S(2)}) collective-permute-start(f32[136,128]{1,0:T(8,128)S(1)} %shard_map.90.own_ref.refs_8_.refs_16_.image_ref), channel_id=1, source_target_pairs={{0,1},{1,0},{2,3},{3,2},{4,5},{5,4},{6,7},{7,6},{8,9},{9,8},{10,11... | collective-permute-start | bytes 208904 | tf_op jit(solution)/shard_map/ppermute | solution.py:40
  46.6 13.8 %collective-permute-start.18 = (f32[136,128]{1,0:T(8,128)S(1)}, f32[136,128]{1,0:T(8,128)S(1)}, u32[]{:S(2)}, u32[]{:S(2)}) collective-permute-start(f32[136,128]{1,0:T(8,128)S(1)} %get-tuple-element.45), channel_id=1, source_target_pairs={{4,0},{6,2},{0,4},{2,6},{5,1},{7,3},{1,5},{3,7},{12,8},{14,10},{8,... | collective-permute-start | bytes 208904 | tf_op jit(solution)/shard_map/ppermute | solution.py:29
  49.2 11.3 %collective-permute-start.19 = (f32[136,128]{1,0:T(8,128)S(1)}, f32[136,128]{1,0:T(8,128)S(1)}, u32[]{:S(2)}, u32[]{:S(2)}) collective-permute-start(f32[136,128]{1,0:T(8,128)S(1)} %get-tuple-element.46), channel_id=1, source_target_pairs={{6,0},{0,2},{2,4},{4,6},{7,1},{1,3},{3,5},{5,7},{14,8},{8,10},{10,... | collective-permute-start | bytes 208904 | tf_op jit(solution)/shard_map/ppermute | solution.py:29
  52.4 8.0 %collective-permute-start.20 = (f32[136,128]{1,0:T(8,128)S(1)}, f32[136,128]{1,0:T(8,128)S(1)}, u32[]{:S(2)}, u32[]{:S(2)}) collective-permute-start(f32[136,128]{1,0:T(8,128)S(1)} %get-tuple-element.47), channel_id=1, source_target_pairs={{2,0},{4,2},{6,4},{0,6},{3,1},{5,3},{7,5},{1,7},{10,8},{12,10},{14... | collective-permute-start | bytes 208904 | tf_op jit(solution)/shard_map/ppermute | solution.py:29
  57.3 6.0 %collective-permute-start.28 = (f32[264,128]{1,0:T(8,128)S(1)}, f32[264,128]{1,0:T(8,128)S(1)}, u32[]{:S(2)}, u32[]{:S(2)}) collective-permute-start(f32[264,128]{1,0:T(8,128)S(1)} %get-tuple-element.50), channel_id=1, source_target_pairs={{64,0},{128,64},{192,128},{0,192},{65,1},{129,65},{193,129},{1,193... | collective-permute-start | bytes 405512 | tf_op jit(solution)/shard_map/ppermute | solution.py:29
  59.9 5.4 %collective-permute-start.29 = (f32[264,128]{1,0:T(8,128)S(1)}, f32[264,128]{1,0:T(8,128)S(1)}, u32[]{:S(2)}, u32[]{:S(2)}) collective-permute-start(f32[264,128]{1,0:T(8,128)S(1)} %get-tuple-element.51), channel_id=1, source_target_pairs={{128,0},{192,64},{0,128},{64,192},{129,1},{193,65},{1,129},{65,193... | collective-permute-start | bytes 405512 | tf_op jit(solution)/shard_map/ppermute | solution.py:29
  60.4 9.4 %collective-permute-start.23 = (f32[136,128]{1,0:T(8,128)S(1)}, f32[136,128]{1,0:T(8,128)S(1)}, u32[]{:S(2)}, u32[]{:S(2)}) collective-permute-start(f32[136,128]{1,0:T(8,128)S(1)} %add_add_fusion.refs_0_), channel_id=1, source_target_pairs={{48,0},{0,16},{16,32},{32,48},{49,1},{1,17},{17,33},{33,49},{50,2}... | collective-permute-start | bytes 208904 | tf_op jit(solution)/shard_map/ppermute | solution.py:29
  60.7 9.2 %collective-permute-start.22 = (f32[136,128]{1,0:T(8,128)S(1)}, f32[136,128]{1,0:T(8,128)S(1)}, u32[]{:S(2)}, u32[]{:S(2)}) collective-permute-start(f32[136,128]{1,0:T(8,128)S(1)} %add_add_fusion.refs_0_), channel_id=1, source_target_pairs={{32,0},{48,16},{0,32},{16,48},{33,1},{49,17},{1,33},{17,49},{34,2}... | collective-permute-start | bytes 208904 | tf_op jit(solution)/shard_map/ppermute | solution.py:29
  63.0 7.5 %collective-permute-start.21 = (f32[136,128]{1,0:T(8,128)S(1)}, f32[136,128]{1,0:T(8,128)S(1)}, u32[]{:S(2)}, u32[]{:S(2)}) collective-permute-start(f32[136,128]{1,0:T(8,128)S(1)} %add_add_fusion.refs_0_), channel_id=1, source_target_pairs={{16,0},{32,16},{48,32},{0,48},{17,1},{33,17},{49,33},{1,49},{18,2}... | collective-permute-start | bytes 208904 | tf_op jit(solution)/shard_map/ppermute | solution.py:29
  63.3 8.5 %collective-permute-start.30 = (f32[264,128]{1,0:T(8,128)S(1)}, f32[264,128]{1,0:T(8,128)S(1)}, u32[]{:S(2)}, u32[]{:S(2)}) collective-permute-start(f32[264,128]{1,0:T(8,128)S(1)} %get-tuple-element.52), channel_id=1, source_target_pairs={{192,0},{0,64},{64,128},{128,192},{193,1},{1,65},{65,129},{129,193... | collective-permute-start | bytes 405512 | tf_op jit(solution)/shard_map/ppermute | solution.py:29
  65.2 6.6 %collective-permute-start.24 = (f32[136,128]{1,0:T(8,128)S(1)}, f32[136,128]{1,0:T(8,128)S(1)}, u32[]{:S(2)}, u32[]{:S(2)}) collective-permute-start(f32[136,128]{1,0:T(8,128)S(1)} %add_add_fusion.refs_0_), channel_id=1, source_target_pairs={{0,8},{8,0},{1,9},{9,1},{2,10},{10,2},{3,11},{11,3},{4,12},{12,4},... | collective-permute-start | bytes 208904 | tf_op jit(solution)/shard_map/ppermute | solution.py:44
  69.9 1.9 %collective-permute-start.27 = (f32[136,128]{1,0:T(8,128)S(1)}, f32[136,128]{1,0:T(8,128)S(1)}, u32[]{:S(2)}, u32[]{:S(2)}) collective-permute-start(f32[136,128]{1,0:T(8,128)S(1)} %collective-permute-done.23.refs_3_), channel_id=1, source_target_pairs={{0,8},{8,0},{1,9},{9,1},{2,10},{10,2},{3,11},{11,3},{4,12},{12,4},... | collective-permute-start | bytes 208904 | tf_op jit(solution)/shard_map/ppermute | solution.py:44
  69.9 1.9 %collective-permute-start.26 = (f32[136,128]{1,0:T(8,128)S(1)}, f32[136,128]{1,0:T(8,128)S(1)}, u32[]{:S(2)}, u32[]{:S(2)}) collective-permute-start(f32[136,128]{1,0:T(8,128)S(1)} %collective-permute-done.22.refs_2_), channel_id=1, source_target_pairs={{0,8},{8,0},{1,9},{9,1},{2,10},{10,2},{3,11},{11,3},{4,12},{12,4},... | collective-permute-start | bytes 208904 | tf_op jit(solution)/shard_map/ppermute | solution.py:44
  70.5 2.2 %collective-permute-start.25 = (f32[136,128]{1,0:T(8,128)S(1)}, f32[136,128]{1,0:T(8,128)S(1)}, u32[]{:S(2)}, u32[]{:S(2)}) collective-permute-start(f32[136,128]{1,0:T(8,128)S(1)} %collective-permute-done.21.refs_1_), channel_id=1, source_target_pairs={{0,8},{8,0},{1,9},{9,1},{2,10},{10,2},{3,11},{11,3},{4,12},{12,4},... | collective-permute-start | bytes 208904 | tf_op jit(solution)/shard_map/ppermute | solution.py:44
  74.6 22.7 %all-to-all-start = ((f32[256,1,128]{2,1,0:T(1,128)}), f32[256,1,128]{2,1,0:T(1,128)S(1)}, u32[]{:S(2)}, u32[]{:S(2)}) async-start(f32[256,1,128]{2,1,0:T(1,128)} %get-tuple-element.53), calls=%async_computation | async-start | bytes 262144 | tf_op jit(solution)/shard_map/all_to_all | solution.py:304
  85.3 5.0 %collective-permute-start.31 = (f32[128,128]{1,0:T(8,128)S(1)}, f32[128,128]{1,0:T(8,128)S(1)}, u32[]{:S(2)}, u32[]{:S(2)}) collective-permute-start(f32[128,128]{1,0:T(8,128)S(1)} %get-tuple-element.57), channel_id=1, source_target_pairs={{192,0},{0,64},{64,128},{128,192},{193,1},{1,65},{65,129},{129,193... | collective-permute-start | bytes 196616 | tf_op jit(solution)/shard_map/ppermute | solution.py:29
  86.8 6.2 %collective-permute-start.32 = (f32[128,128]{1,0:T(8,128)S(1)}, f32[128,128]{1,0:T(8,128)S(1)}, u32[]{:S(2)}, u32[]{:S(2)}) collective-permute-start(f32[128,128]{1,0:T(8,128)S(1)} %get-tuple-element.58), channel_id=1, source_target_pairs={{128,0},{192,64},{0,128},{64,192},{129,1},{193,65},{1,129},{65,193... | collective-permute-start | bytes 196616 | tf_op jit(solution)/shard_map/ppermute | solution.py:29
  89.2 3.8 %collective-permute-start.33 = (f32[128,128]{1,0:T(8,128)S(1)}, f32[128,128]{1,0:T(8,128)S(1)}, u32[]{:S(2)}, u32[]{:S(2)}) collective-permute-start(f32[128,128]{1,0:T(8,128)S(1)} %get-tuple-element.59), channel_id=1, source_target_pairs={{64,0},{128,64},{192,128},{0,192},{65,1},{129,65},{193,129},{1,193... | collective-permute-start | bytes 196616 | tf_op jit(solution)/shard_map/ppermute | solution.py:29

commit v6 on v5

--- a/solution.py
+++ b/solution.py
@@ -13,6 +13,7 @@
 LOC = ("loc_0", "loc_1", "loc_2")
 TM = ("tm_0", "tm_1")
 EVERYONE = LOC + TM
+ONE_CORE = ("loc_0", "loc_1") + TM
 
 root_three = math.sqrt(3.0)
 space_reach = 2.5
@@ -238,8 +239,7 @@
             line = jnp.where(lane == k, jnp.sum(value, axis=1, keepdims=True), line)
         return line
 
-    line = side_by_side([squares, curved, crossed])
-    out_ref[...] = jnp.broadcast_to(line[None], out_ref.shape)
+    out_ref[...] = side_by_side([squares, curved, crossed])
     known_ref[...] = side_by_side([step, norm, first])
 
 
@@ -331,7 +331,9 @@
             time_low,
             flops=6 * TILE * 8 * TILE * TILE,
         )
-        parts = [parts[0]] + [ahead(parts[k], "tm_0", -k) for k in (1, 2, 3)]
+        parts = list(parts)
+        for k in (1, 2, 3):
+            parts[k] = ahead(parts[k], "tm_0", -k)
         return (parts[0] + parts[2]) + (parts[1] + parts[3])
 
     def columns(block):
@@ -390,10 +392,9 @@
     others = [ahead(piece, "loc_0", s) for s, piece in enumerate(pieces, 1)]
     image_rows = [image] + others
     image_folds = columns(image_fold)
-    size = lax.axis_size(EVERYONE)
     sums, known = call(
         curve_kernel,
-        [((size, 1, TILE), f32), ((1, TILE), f32)],
+        [((1, TILE), f32)] * 2,
         *image_folds,
         *outers,
         *start_rows,
@@ -404,7 +405,9 @@
         flops=one_product,
         scratch=right,
     )
-    sums = exchanged(sums, EVERYONE)
+    sums = sums + swapped(sums)
+    copies = jnp.broadcast_to(sums, (lax.axis_size(ONE_CORE), *sums.shape))
+    sums = exchanged(copies, ONE_CORE)
     fields = call(
         image_field_kernel,
         [square] * 4,

time: 98.6 us -> 98.2 us (level)
  waiting for transfers between devices: 16.9 us -> 15.7 us
    all_to_all x1, waiting for transfers between devices: 4.33 us -> 2 us  [exchanged(): return lax.all_to_all(copies, axes, split_axis=0, concat_axis=0, tiled=True)]
    ppermute x8 -> x9, starting transfers between devices: 11.3 us -> 12.4 us  [swapped(): return lax.ppermute(block, 'loc_2', [(0, 1), (1, 0)])]
  transfers between devices with their start and end apart: 35 -> 36, of which waited for: 10 -> 13; matrix products, arithmetic and copies ran while one was open for 0% -> 0% of each run, Pallas kernels for 9% -> 9%
where the time goes in v6:
time: 98.2 us; the launch traced here: 98 us
  starting transfers between devices  67.2 us (68%)
  waiting for transfers between devices  15.7 us (16%)
  Pallas kernels  12.6 us (13%)
    ppermute x24, starting transfers between devices, ahead(): lax.ppermute(block, axis, [((i + shift) % size, i) for i in range(size)])  41.4 us
    pallas_call x11, Pallas kernels, call(): pl.pallas_call(kernel, out_shape=shapes, in_specs=[VMEM] * len(args), out...  12.6 us
    ppermute x9, starting transfers between devices, swapped(): return lax.ppermute(block, 'loc_2', [(0, 1), (1, 0)])  12.4 us
    all_to_all x1, starting transfers between devices, exchanged(): return lax.all_to_all(copies, axes, split_axis=0, concat_axis=0, tiled=True)  9.95 us
    ppermute x24, waiting for transfers between devices, ahead(): lax.ppermute(block, axis, [((i + shift) % size, i) for i in range(size)])  8.32 us
    ppermute x2, waiting for transfers between devices, neighbours(): return lax.ppermute(block, 'tm_1', [(0, 1), (1, 0)])  3.66 us
    ppermute x2, starting transfers between devices, neighbours(): return lax.ppermute(block, 'tm_1', [(0, 1), (1, 0)])  3.42 us
    all_to_all x1, waiting for transfers between devices, exchanged(): return lax.all_to_all(copies, axes, split_axis=0, concat_axis=0, tiled=True)  2 us
  transfers between devices with their start and end apart: 36, of which 13 were waited for; matrix products, arithmetic and copies ran while one was open for 0% of the time, Pallas kernels for 9%

profile of v6, /device:TPU:1, one launch (start us, length us, event | category | flops | bytes accessed | tf_op | source)
XLA Modules:
  0.0 98.0 jit_solution(13222530403290774233)
XLA Ops:
  0.6 0.9 convert_multiply_fusion.own_ref.refs_8_.start_ref.refs_12_
  1.5 2.5 %collective-permute-start = (f32[128,128]{1,0:T(8,128)S(1)}, f32[128,128]{1,0:T(8,128)S(1)}, u32[]{:S(2)}, u32[]{:S(2)}) collective-permute-start(f32[128,128]{1,0:T(8,128)S(1)} %convert_multiply_fusion.own_ref.refs_8_.start_ref.refs_12_), channel_id=1, source_target_pairs={{0,1},{1,0},{2,3},{3,2},{4,5},{5,4},{6,7},{7,6},{8,9},{9,8},{10,11... | collective-permute-start | bytes 196616 | tf_op jit(solution)/shard_map/ppermute | solution.py:41
  4.4 1.3 %collective-permute-done.other_ref = f32[128,128]{1,0:T(8,128)S(1)} collective-permute-done((f32[128,128]{1,0:T(8,128)S(1)}, f32[128,128]{1,0:T(8,128)S(1)}, u32[]{:S(2)}, u32[]{:S(2)}) %collective-permute-start) | collective-permute-done | bytes 65568 | tf_op jit(solution)/shard_map/ppermute | solution.py:41
  6.1 6.8 %collective-permute-start.1 = (f32[128,128]{1,0:T(8,128)S(1)}, f32[128,128]{1,0:T(8,128)S(1)}, u32[]{:S(2)}, u32[]{:S(2)}) collective-permute-start(f32[128,128]{1,0:T(8,128)S(1)} %get-tuple-element.34), channel_id=1, source_target_pairs={{4,0},{6,2},{0,4},{2,6},{5,1},{7,3},{1,5},{3,7},{12,8},{14,10},{8,... | collective-permute-start | bytes 196616 | tf_op jit(solution)/shard_map/ppermute | solution.py:30
  12.9 1.2 %collective-permute-start.2 = (f32[128,128]{1,0:T(8,128)S(1)}, f32[128,128]{1,0:T(8,128)S(1)}, u32[]{:S(2)}, u32[]{:S(2)}) collective-permute-start(f32[128,128]{1,0:T(8,128)S(1)} %get-tuple-element.35), channel_id=1, source_target_pairs={{6,0},{0,2},{2,4},{4,6},{7,1},{1,3},{3,5},{5,7},{14,8},{8,10},{10,... | collective-permute-start | bytes 196616 | tf_op jit(solution)/shard_map/ppermute | solution.py:30
  14.1 2.4 %collective-permute-start.3 = (f32[128,128]{1,0:T(8,128)S(1)}, f32[128,128]{1,0:T(8,128)S(1)}, u32[]{:S(2)}, u32[]{:S(2)}) collective-permute-start(f32[128,128]{1,0:T(8,128)S(1)} %get-tuple-element.36), channel_id=1, source_target_pairs={{2,0},{4,2},{6,4},{0,6},{3,1},{5,3},{7,5},{1,7},{10,8},{12,10},{14... | collective-permute-start | bytes 196616 | tf_op jit(solution)/shard_map/ppermute | solution.py:30
  16.5 1.3 %collective-permute-start.13 = (f32[128,128]{1,0:T(8,128)S(1)}, f32[128,128]{1,0:T(8,128)S(1)}, u32[]{:S(2)}, u32[]{:S(2)}) collective-permute-start(f32[128,128]{1,0:T(8,128)S(1)} %convert_multiply_fusion.own_ref.refs_8_.start_ref.refs_12_), channel_id=1, source_target_pairs={{192,0},{0,64},{64,128},{128,192},{193,1},{1,65},{65,129},{129,193... | collective-permute-start | bytes 196616 | tf_op jit(solution)/shard_map/ppermute | solution.py:30
  17.8 2.6 %collective-permute-start.12 = (f32[128,128]{1,0:T(8,128)S(1)}, f32[128,128]{1,0:T(8,128)S(1)}, u32[]{:S(2)}, u32[]{:S(2)}) collective-permute-start(f32[128,128]{1,0:T(8,128)S(1)} %convert_multiply_fusion.own_ref.refs_8_.start_ref.refs_12_), channel_id=1, source_target_pairs={{128,0},{192,64},{0,128},{64,192},{129,1},{193,65},{1,129},{65,193... | collective-permute-start | bytes 196616 | tf_op jit(solution)/shard_map/ppermute | solution.py:30
  20.5 1.3 %collective-permute-start.6 = (f32[128,128]{1,0:T(8,128)S(1)}, f32[128,128]{1,0:T(8,128)S(1)}, u32[]{:S(2)}, u32[]{:S(2)}) collective-permute-start(f32[128,128]{1,0:T(8,128)S(1)} %add_add_fusion.1.refs_0_), channel_id=1, source_target_pairs={{48,0},{0,16},{16,32},{32,48},{49,1},{1,17},{17,33},{33,49},{50,2}... | collective-permute-start | bytes 196616 | tf_op jit(solution)/shard_map/ppermute | solution.py:30
  21.8 2.5 %collective-permute-start.5 = (f32[128,128]{1,0:T(8,128)S(1)}, f32[128,128]{1,0:T(8,128)S(1)}, u32[]{:S(2)}, u32[]{:S(2)}) collective-permute-start(f32[128,128]{1,0:T(8,128)S(1)} %add_add_fusion.1.refs_0_), channel_id=1, source_target_pairs={{32,0},{48,16},{0,32},{16,48},{33,1},{49,17},{1,33},{17,49},{34,2}... | collective-permute-start | bytes 196616 | tf_op jit(solution)/shard_map/ppermute | solution.py:30
  24.2 1.1 %collective-permute-start.4 = (f32[128,128]{1,0:T(8,128)S(1)}, f32[128,128]{1,0:T(8,128)S(1)}, u32[]{:S(2)}, u32[]{:S(2)}) collective-permute-start(f32[128,128]{1,0:T(8,128)S(1)} %add_add_fusion.1.refs_0_), channel_id=1, source_target_pairs={{16,0},{32,16},{48,32},{0,48},{17,1},{33,17},{49,33},{1,49},{18,2}... | collective-permute-start | bytes 196616 | tf_op jit(solution)/shard_map/ppermute | solution.py:30
  25.4 2.1 %collective-permute-start.11 = (f32[128,128]{1,0:T(8,128)S(1)}, f32[128,128]{1,0:T(8,128)S(1)}, u32[]{:S(2)}, u32[]{:S(2)}) collective-permute-start(f32[128,128]{1,0:T(8,128)S(1)} %convert_multiply_fusion.own_ref.refs_8_.start_ref.refs_12_), channel_id=1, source_target_pairs={{64,0},{128,64},{192,128},{0,192},{65,1},{129,65},{193,129},{1,193... | collective-permute-start | bytes 196616 | tf_op jit(solution)/shard_map/ppermute | solution.py:30
  27.5 3.3 %collective-permute-start.7 = (f32[128,128]{1,0:T(8,128)S(1)}, f32[128,128]{1,0:T(8,128)S(1)}, u32[]{:S(2)}, u32[]{:S(2)}) collective-permute-start(f32[128,128]{1,0:T(8,128)S(1)} %add_add_fusion.1.refs_0_), channel_id=1, source_target_pairs={{0,8},{8,0},{1,9},{9,1},{2,10},{10,2},{3,11},{11,3},{4,12},{12,4},... | collective-permute-start | bytes 196616 | tf_op jit(solution)/shard_map/ppermute | solution.py:45
  31.3 1.0 collective-permute-start.8
  32.3 2.7 %shard_map.88 = (bf16[512,1024]{1,0:T(8,128)(2,1)S(1)}, bf16[512,1024]{1,0:T(8,128)(2,1)S(1)}, f32[1,128]{1,0:T(1,128)S(1)}) custom-call(f32[2,4096]{1,0:T(2,128)S(1)} %copy-done.1, f32[1,128]{1,0:T(1,128)S(1)} %bitcast.7), custom_call_target="tpu_custom_call" | custom-call | flops 209715200 | bytes 2130944 | tf_op jit(solution)/shard_map/pallas_call | solution.py:60
  35.0 1.1 %shard_map.89 = (f32[136,128]{1,0:T(8,128)S(1)}, f32[136,128]{1,0:T(8,128)S(1)}, f32[136,128]{1,0:T(8,128)S(1)}, f32[136,128]{1,0:T(8,128)S(1)}) custom-call(f32[128,128]{1,0:T(8,128)S(1)} %add_add_fusion.1.refs_0_, f32[128,128]{1,0:T(8,128)S(1)} %collective-permute-done.4.refs_1_, f32[128,128]{1,0:T(8,128)S(1)} %collective-permute-done.5.refs_2_, ...), custom_call_target="tpu_custom_call" | custom-call | flops 402653184 | bytes 3162624 | tf_op jit(solution)/shard_map/pallas_call | solution.py:60
  36.2 2.2 %collective-permute-start.15 = (f32[136,128]{1,0:T(8,128)S(1)}, f32[136,128]{1,0:T(8,128)S(1)}, u32[]{:S(2)}, u32[]{:S(2)}) collective-permute-start(f32[136,128]{1,0:T(8,128)S(1)} %get-tuple-element.42.refs_10_), channel_id=1, source_target_pairs={{128,0},{192,64},{0,128},{64,192},{129,1},{193,65},{1,129},{65,193... | collective-permute-start | bytes 208904 | tf_op jit(solution)/shard_map/ppermute | solution.py:30
  38.4 1.0 %collective-permute-start.16 = (f32[136,128]{1,0:T(8,128)S(1)}, f32[136,128]{1,0:T(8,128)S(1)}, u32[]{:S(2)}, u32[]{:S(2)}) collective-permute-start(f32[136,128]{1,0:T(8,128)S(1)} %get-tuple-element.43.refs_11_), channel_id=1, source_target_pairs={{64,0},{128,64},{192,128},{0,192},{65,1},{129,65},{193,129},{1,193... | collective-permute-start | bytes 208904 | tf_op jit(solution)/shard_map/ppermute | solution.py:30
  39.5 2.0 %collective-permute-done.14.b = f32[136,128]{1,0:T(8,128)S(1)} collective-permute-done((f32[136,128]{1,0:T(8,128)S(1)}, f32[136,128]{1,0:T(8,128)S(1)}, u32[]{:S(2)}, u32[]{:S(2)}) %collective-permute-start.14) | collective-permute-done | bytes 69664 | tf_op jit(solution)/shard_map/ppermute | solution.py:30
  41.5 0.7 collective-permute-done.15.c
  42.2 0.7 collective-permute-done.16.d
  43.0 0.9 collective-permute-start.17
  43.8 2.4 %collective-permute-done.17.other_ref = f32[136,128]{1,0:T(8,128)S(1)} collective-permute-done((f32[136,128]{1,0:T(8,128)S(1)}, f32[136,128]{1,0:T(8,128)S(1)}, u32[]{:S(2)}, u32[]{:S(2)}) %collective-permute-start.17) | collective-permute-done | bytes 69664 | tf_op jit(solution)/shard_map/ppermute | solution.py:41
  46.6 2.6 %collective-permute-start.18 = (f32[136,128]{1,0:T(8,128)S(1)}, f32[136,128]{1,0:T(8,128)S(1)}, u32[]{:S(2)}, u32[]{:S(2)}) collective-permute-start(f32[136,128]{1,0:T(8,128)S(1)} %get-tuple-element.45), channel_id=1, source_target_pairs={{4,0},{6,2},{0,4},{2,6},{5,1},{7,3},{1,5},{3,7},{12,8},{14,10},{8,... | collective-permute-start | bytes 208904 | tf_op jit(solution)/shard_map/ppermute | solution.py:30
  49.2 3.3 %collective-permute-start.19 = (f32[136,128]{1,0:T(8,128)S(1)}, f32[136,128]{1,0:T(8,128)S(1)}, u32[]{:S(2)}, u32[]{:S(2)}) collective-permute-start(f32[136,128]{1,0:T(8,128)S(1)} %get-tuple-element.46), channel_id=1, source_target_pairs={{6,0},{0,2},{2,4},{4,6},{7,1},{1,3},{3,5},{5,7},{14,8},{8,10},{10,... | collective-permute-start | bytes 208904 | tf_op jit(solution)/shard_map/ppermute | solution.py:30
  52.8 3.5 %shard_map.92 = (bf16[512,1024]{1,0:T(8,128)(2,1)S(1)}, bf16[512,1024]{1,0:T(8,128)(2,1)S(1)}) custom-call(f32[2,4096]{1,0:T(2,128)S(1)} %copy-done.1, f32[2,4096]{1,0:T(2,128)S(1)} %copy-done.2, s32[32,128]{1,0:T(8,128)S(1)} %bitcast.5), custom_call_target="tpu_custom_call" | custom-call | flops 314572800 | bytes 2179072 | tf_op jit(solution)/shard_map/pallas_call | solution.py:60
  56.2 1.0 %shard_map.93 = (f32[128,128]{1,0:T(8,128)S(1)}, f32[264,128]{1,0:T(8,128)S(1)}, f32[264,128]{1,0:T(8,128)S(1)}, f32[264,128]{1,0:T(8,128)S(1)}) custom-call(f32[128,128]{1,0:T(8,128)S(1)} %add_add_fusion.1.refs_0_, f32[128,128]{1,0:T(8,128)S(1)} %collective-permute-done.4.refs_1_, f32[128,128]{1,0:T(8,128)S(1)} %collective-permute-done.5.refs_2_, ...), custom_call_target="tpu_custom_call" | custom-call | flops 402653184 | bytes 3162112 | tf_op jit(solution)/shard_map/pallas_call | solution.py:60
  57.3 2.6 %collective-permute-start.28 = (f32[264,128]{1,0:T(8,128)S(1)}, f32[264,128]{1,0:T(8,128)S(1)}, u32[]{:S(2)}, u32[]{:S(2)}) collective-permute-start(f32[264,128]{1,0:T(8,128)S(1)} %get-tuple-element.50), channel_id=1, source_target_pairs={{64,0},{128,64},{192,128},{0,192},{65,1},{129,65},{193,129},{1,193... | collective-permute-start | bytes 405512 | tf_op jit(solution)/shard_map/ppermute | solution.py:30
  59.9 0.5 collective-permute-start.29
  60.7 2.3 %collective-permute-start.22 = (f32[136,128]{1,0:T(8,128)S(1)}, f32[136,128]{1,0:T(8,128)S(1)}, u32[]{:S(2)}, u32[]{:S(2)}) collective-permute-start(f32[136,128]{1,0:T(8,128)S(1)} %add_add_fusion.refs_0_), channel_id=1, source_target_pairs={{32,0},{48,16},{0,32},{16,48},{33,1},{49,17},{1,33},{17,49},{34,2}... | collective-permute-start | bytes 208904 | tf_op jit(solution)/shard_map/ppermute | solution.py:30
  63.4 1.8 %collective-permute-done.29.refs_18_.refs_2_ = f32[264,128]{1,0:T(8,128)S(1)} collective-permute-done((f32[264,128]{1,0:T(8,128)S(1)}, f32[264,128]{1,0:T(8,128)S(1)}, u32[]{:S(2)}, u32[]{:S(2)}) %collective-permute-start.29) | collective-permute-done | bytes 135200 | tf_op jit(solution)/shard_map/ppermute | solution.py:30
  65.2 4.7 %collective-permute-start.24 = (f32[136,128]{1,0:T(8,128)S(1)}, f32[136,128]{1,0:T(8,128)S(1)}, u32[]{:S(2)}, u32[]{:S(2)}) collective-permute-start(f32[136,128]{1,0:T(8,128)S(1)} %add_add_fusion.refs_0_), channel_id=1, source_target_pairs={{0,8},{8,0},{1,9},{9,1},{2,10},{10,2},{3,11},{11,3},{4,12},{12,4},... | collective-permute-start | bytes 208904 | tf_op jit(solution)/shard_map/ppermute | solution.py:45
  69.9 0.6 collective-permute-start.26
  70.5 1.3 %collective-permute-start.25 = (f32[136,128]{1,0:T(8,128)S(1)}, f32[136,128]{1,0:T(8,128)S(1)}, u32[]{:S(2)}, u32[]{:S(2)}) collective-permute-start(f32[136,128]{1,0:T(8,128)S(1)} %collective-permute-done.21.refs_1_), channel_id=1, source_target_pairs={{0,8},{8,0},{1,9},{9,1},{2,10},{10,2},{3,11},{11,3},{4,12},{12,4},... | collective-permute-start | bytes 208904 | tf_op jit(solution)/shard_map/ppermute | solution.py:45
  71.8 0.9 collective-permute-done.25.refs_5_
  72.7 1.1 %shard_map.94 = (f32[1,128]{1,0:T(1,128)S(1)}, f32[1,128]{1,0:T(1,128)S(1)}) custom-call(f32[136,128]{1,0:T(8,128)S(1)} %add_add_fusion.refs_0_, f32[136,128]{1,0:T(8,128)S(1)} %collective-permute-done.21.refs_1_, f32[136,128]{1,0:T(8,128)S(1)} %collective-permute-done.22.refs_2_, f32[136,128]{1,0:T(8,128)S(1)} %collective-permute-done.23.refs_3_, ...), custom_call_target="tpu_custom_call" | custom-call | flops 402653184 | bytes 3671552 | tf_op jit(solution)/shard_map/pallas_call | solution.py:60
  73.9 1.1 %collective-permute-start.31 = (f32[1,128]{1,0:T(1,128)S(1)}, f32[1,128]{1,0:T(1,128)S(1)}, u32[]{:S(2)}, u32[]{:S(2)}) collective-permute-start(f32[1,128]{1,0:T(1,128)S(1)} %get-tuple-element.53), channel_id=1, source_target_pairs={{0,8},{8,0},{1,9},{9,1},{2,10},{10,2},{3,11},{11,3},{4,12},{12,4},... | collective-permute-start | bytes 1544 | tf_op jit(solution)/shard_map/ppermute | solution.py:45
  75.0 0.8 collective-permute-done.31
  75.8 0.7 broadcast_in_dim.7
  76.5 9.9 %all-to-all-start = ((f32[128,1,128]{2,1,0:T(1,128)}), f32[128,1,128]{2,1,0:T(1,128)S(1)}, u32[]{:S(2)}, u32[]{:S(2)}) async-start(f32[128,1,128]{2,1,0:T(1,128)} %broadcast_in_dim.7), calls=%async_computation | async-start | bytes 131072 | tf_op jit(solution)/shard_map/all_to_all | solution.py:304
  86.5 1.0 %shard_map.95 = (f32[128,128]{1,0:T(8,128)S(1)}, f32[128,128]{1,0:T(8,128)S(1)}, f32[128,128]{1,0:T(8,128)S(1)}, f32[128,128]{1,0:T(8,128)S(1)}) custom-call(f32[136,128]{1,0:T(8,128)S(1)} %add_add_fusion.refs_0_, f32[136,128]{1,0:T(8,128)S(1)} %collective-permute-done.21.refs_1_, f32[136,128]{1,0:T(8,128)S(1)} %collective-permute-done.22.refs_2_, ...), custom_call_target="tpu_custom_call" | custom-call | flops 402653184 | bytes 2916352 | tf_op jit(solution)/shard_map/pallas_call | solution.py:60
  87.5 0.7 collective-permute-start.32
  88.2 2.8 %collective-permute-start.33 = (f32[128,128]{1,0:T(8,128)S(1)}, f32[128,128]{1,0:T(8,128)S(1)}, u32[]{:S(2)}, u32[]{:S(2)}) collective-permute-start(f32[128,128]{1,0:T(8,128)S(1)} %get-tuple-element.58), channel_id=1, source_target_pairs={{128,0},{192,64},{0,128},{64,192},{129,1},{193,65},{1,129},{65,193... | collective-permute-start | bytes 196616 | tf_op jit(solution)/shard_map/ppermute | solution.py:30
  91.1 1.0 collective-permute-start.34
  92.2 1.9 %collective-permute-done.33.refs_6_ = f32[128,128]{1,0:T(8,128)S(1)} collective-permute-done((f32[128,128]{1,0:T(8,128)S(1)}, f32[128,128]{1,0:T(8,128)S(1)}, u32[]{:S(2)}, u32[]{:S(2)}) %collective-permute-start.33) | collective-permute-done | bytes 65568 | tf_op jit(solution)/shard_map/ppermute | solution.py:30
  94.1 0.8 collective-permute-done.34.refs_7_
  95.0 2.0 %all-to-all-done.sums_ref = f32[128,1,128]{2,1,0:T(1,128)S(1)} async-done(((f32[128,1,128]{2,1,0:T(1,128)}), f32[128,1,128]{2,1,0:T(1,128)S(1)}, u32[]{:S(2)}, u32[]{:S(2)}) %all-to-all-start) | async-done | bytes 65568 | tf_op jit(solution)/shard_map/all_to_all | solution.py:304
  97.0 1.0 %shard_map.96 = (f32[128,128]{1,0:T(8,128)}, f32[128,128]{1,0:T(8,128)}) custom-call(f32[128,1,128]{2,1,0:T(1,128)S(1)} %all-to-all-done.sums_ref, f32[1,128]{1,0:T(1,128)S(1)} %get-tuple-element.54.known_ref, f32[128,128]{1,0:T(8,128)S(1)} %convert_multiply_fusion.own_ref.refs_8_.start_ref.refs_12_, ...), custom_call_target="tpu_custom_call" | custom-call | flops 327680 | bytes 1065472 | tf_op jit(solution)/shard_map/pallas_call | solution.py:60
  (52 shorter events, 3.0 us)
Async XLA Ops:
  0.6 3.4 %copy-start.4 = (f32[1024]{0:T(1024)S(1)}, f32[1024]{0:T(1024)}, u32[]{:S(2)}) copy-start(f32[1024]{0:T(1024)} %param.10) | copy-start | bytes 12292
  1.5 4.2 %collective-permute-start = (f32[128,128]{1,0:T(8,128)S(1)}, f32[128,128]{1,0:T(8,128)S(1)}, u32[]{:S(2)}, u32[]{:S(2)}) collective-permute-start(f32[128,128]{1,0:T(8,128)S(1)} %convert_multiply_fusion.own_ref.refs_8_.start_ref.refs_12_), channel_id=1, source_target_pairs={{0,1},{1,0},{2,3},{3,2},{4,5},{5,4},{6,7},{7,6},{8,9},{9,8},{10,11... | collective-permute-start | bytes 196616 | tf_op jit(solution)/shard_map/ppermute | solution.py:41
  6.1 14.3 %collective-permute-start.1 = (f32[128,128]{1,0:T(8,128)S(1)}, f32[128,128]{1,0:T(8,128)S(1)}, u32[]{:S(2)}, u32[]{:S(2)}) collective-permute-start(f32[128,128]{1,0:T(8,128)S(1)} %get-tuple-element.34), channel_id=1, source_target_pairs={{4,0},{6,2},{0,4},{2,6},{5,1},{7,3},{1,5},{3,7},{12,8},{14,10},{8,... | collective-permute-start | bytes 196616 | tf_op jit(solution)/shard_map/ppermute | solution.py:30
  12.9 7.5 %collective-permute-start.2 = (f32[128,128]{1,0:T(8,128)S(1)}, f32[128,128]{1,0:T(8,128)S(1)}, u32[]{:S(2)}, u32[]{:S(2)}) collective-permute-start(f32[128,128]{1,0:T(8,128)S(1)} %get-tuple-element.35), channel_id=1, source_target_pairs={{6,0},{0,2},{2,4},{4,6},{7,1},{1,3},{3,5},{5,7},{14,8},{8,10},{10,... | collective-permute-start | bytes 196616 | tf_op jit(solution)/shard_map/ppermute | solution.py:30
  14.1 6.3 %collective-permute-start.3 = (f32[128,128]{1,0:T(8,128)S(1)}, f32[128,128]{1,0:T(8,128)S(1)}, u32[]{:S(2)}, u32[]{:S(2)}) collective-permute-start(f32[128,128]{1,0:T(8,128)S(1)} %get-tuple-element.36), channel_id=1, source_target_pairs={{2,0},{4,2},{6,4},{0,6},{3,1},{5,3},{7,5},{1,7},{10,8},{12,10},{14... | collective-permute-start | bytes 196616 | tf_op jit(solution)/shard_map/ppermute | solution.py:30
  16.5 8.9 %collective-permute-start.13 = (f32[128,128]{1,0:T(8,128)S(1)}, f32[128,128]{1,0:T(8,128)S(1)}, u32[]{:S(2)}, u32[]{:S(2)}) collective-permute-start(f32[128,128]{1,0:T(8,128)S(1)} %convert_multiply_fusion.own_ref.refs_8_.start_ref.refs_12_), channel_id=1, source_target_pairs={{192,0},{0,64},{64,128},{128,192},{193,1},{1,65},{65,129},{129,193... | collective-permute-start | bytes 196616 | tf_op jit(solution)/shard_map/ppermute | solution.py:30
  17.8 9.7 %collective-permute-start.12 = (f32[128,128]{1,0:T(8,128)S(1)}, f32[128,128]{1,0:T(8,128)S(1)}, u32[]{:S(2)}, u32[]{:S(2)}) collective-permute-start(f32[128,128]{1,0:T(8,128)S(1)} %convert_multiply_fusion.own_ref.refs_8_.start_ref.refs_12_), channel_id=1, source_target_pairs={{128,0},{192,64},{0,128},{64,192},{129,1},{193,65},{1,129},{65,193... | collective-permute-start | bytes 196616 | tf_op jit(solution)/shard_map/ppermute | solution.py:30
  20.4 11.8 %copy-start.1 = (f32[2,4096]{1,0:T(2,128)S(1)}, f32[2,4096]{1,0:T(2,128)}, u32[]{:S(2)}) copy-start(f32[2,4096]{1,0:T(2,128)} %sites_ref.3) | copy-start | bytes 98308
  20.5 11.8 %copy-start.5 = (f32[128]{0:T(128)S(1)}, f32[128]{0:T(128)}, u32[]{:S(2)}) copy-start(f32[128]{0:T(128)} %param.11) | copy-start | bytes 1540
  20.5 10.3 %collective-permute-start.6 = (f32[128,128]{1,0:T(8,128)S(1)}, f32[128,128]{1,0:T(8,128)S(1)}, u32[]{:S(2)}, u32[]{:S(2)}) collective-permute-start(f32[128,128]{1,0:T(8,128)S(1)} %add_add_fusion.1.refs_0_), channel_id=1, source_target_pairs={{48,0},{0,16},{16,32},{32,48},{49,1},{1,17},{17,33},{33,49},{50,2}... | collective-permute-start | bytes 196616 | tf_op jit(solution)/shard_map/ppermute | solution.py:30
  21.8 9.1 %collective-permute-start.5 = (f32[128,128]{1,0:T(8,128)S(1)}, f32[128,128]{1,0:T(8,128)S(1)}, u32[]{:S(2)}, u32[]{:S(2)}) collective-permute-start(f32[128,128]{1,0:T(8,128)S(1)} %add_add_fusion.1.refs_0_), channel_id=1, source_target_pairs={{32,0},{48,16},{0,32},{16,48},{33,1},{49,17},{1,33},{17,49},{34,2}... | collective-permute-start | bytes 196616 | tf_op jit(solution)/shard_map/ppermute | solution.py:30
  24.2 7.1 %collective-permute-start.4 = (f32[128,128]{1,0:T(8,128)S(1)}, f32[128,128]{1,0:T(8,128)S(1)}, u32[]{:S(2)}, u32[]{:S(2)}) collective-permute-start(f32[128,128]{1,0:T(8,128)S(1)} %add_add_fusion.1.refs_0_), channel_id=1, source_target_pairs={{16,0},{32,16},{48,32},{0,48},{17,1},{33,17},{49,33},{1,49},{18,2}... | collective-permute-start | bytes 196616 | tf_op jit(solution)/shard_map/ppermute | solution.py:30
  25.4 9.6 %collective-permute-start.11 = (f32[128,128]{1,0:T(8,128)S(1)}, f32[128,128]{1,0:T(8,128)S(1)}, u32[]{:S(2)}, u32[]{:S(2)}) collective-permute-start(f32[128,128]{1,0:T(8,128)S(1)} %convert_multiply_fusion.own_ref.refs_8_.start_ref.refs_12_), channel_id=1, source_target_pairs={{64,0},{128,64},{192,128},{0,192},{65,1},{129,65},{193,129},{1,193... | collective-permute-start | bytes 196616 | tf_op jit(solution)/shard_map/ppermute | solution.py:30
  27.5 7.5 %collective-permute-start.7 = (f32[128,128]{1,0:T(8,128)S(1)}, f32[128,128]{1,0:T(8,128)S(1)}, u32[]{:S(2)}, u32[]{:S(2)}) collective-permute-start(f32[128,128]{1,0:T(8,128)S(1)} %add_add_fusion.1.refs_0_), channel_id=1, source_target_pairs={{0,8},{8,0},{1,9},{9,1},{2,10},{10,2},{3,11},{11,3},{4,12},{12,4},... | collective-permute-start | bytes 196616 | tf_op jit(solution)/shard_map/ppermute | solution.py:45
  30.8 4.2 %collective-permute-start.10 = (f32[128,128]{1,0:T(8,128)S(1)}, f32[128,128]{1,0:T(8,128)S(1)}, u32[]{:S(2)}, u32[]{:S(2)}) collective-permute-start(f32[128,128]{1,0:T(8,128)S(1)} %collective-permute-done.6.refs_3_), channel_id=1, source_target_pairs={{0,8},{8,0},{1,9},{9,1},{2,10},{10,2},{3,11},{11,3},{4,12},{12,4},... | collective-permute-start | bytes 196616 | tf_op jit(solution)/shard_map/ppermute | solution.py:45
  30.9 4.1 %collective-permute-start.9 = (f32[128,128]{1,0:T(8,128)S(1)}, f32[128,128]{1,0:T(8,128)S(1)}, u32[]{:S(2)}, u32[]{:S(2)}) collective-permute-start(f32[128,128]{1,0:T(8,128)S(1)} %collective-permute-done.5.refs_2_), channel_id=1, source_target_pairs={{0,8},{8,0},{1,9},{9,1},{2,10},{10,2},{3,11},{11,3},{4,12},{12,4},... | collective-permute-start | bytes 196616 | tf_op jit(solution)/shard_map/ppermute | solution.py:45
  31.3 3.7 %collective-permute-start.8 = (f32[128,128]{1,0:T(8,128)S(1)}, f32[128,128]{1,0:T(8,128)S(1)}, u32[]{:S(2)}, u32[]{:S(2)}) collective-permute-start(f32[128,128]{1,0:T(8,128)S(1)} %collective-permute-done.4.refs_1_), channel_id=1, source_target_pairs={{0,8},{8,0},{1,9},{9,1},{2,10},{10,2},{3,11},{11,3},{4,12},{12,4},... | collective-permute-start | bytes 196616 | tf_op jit(solution)/shard_map/ppermute | solution.py:45
  35.0 7.9 %copy-start = (s32[128,128]{1,0:T(8,128)S(1)}, s32[128,128]{1,0:T(8,128)}, u32[]{:S(2)}) copy-start(s32[128,128]{1,0:T(8,128)} %mask_ref.1) | copy-start | bytes 196612
  36.1 5.4 %collective-permute-start.14 = (f32[136,128]{1,0:T(8,128)S(1)}, f32[136,128]{1,0:T(8,128)S(1)}, u32[]{:S(2)}, u32[]{:S(2)}) collective-permute-start(f32[136,128]{1,0:T(8,128)S(1)} %get-tuple-element.41.refs_9_), channel_id=1, source_target_pairs={{192,0},{0,64},{64,128},{128,192},{193,1},{1,65},{65,129},{129,193... | collective-permute-start | bytes 208904 | tf_op jit(solution)/shard_map/ppermute | solution.py:30
  36.2 6.0 %collective-permute-start.15 = (f32[136,128]{1,0:T(8,128)S(1)}, f32[136,128]{1,0:T(8,128)S(1)}, u32[]{:S(2)}, u32[]{:S(2)}) collective-permute-start(f32[136,128]{1,0:T(8,128)S(1)} %get-tuple-element.42.refs_10_), channel_id=1, source_target_pairs={{128,0},{192,64},{0,128},{64,192},{129,1},{193,65},{1,129},{65,193... | collective-permute-start | bytes 208904 | tf_op jit(solution)/shard_map/ppermute | solution.py:30
  38.4 4.5 %collective-permute-start.16 = (f32[136,128]{1,0:T(8,128)S(1)}, f32[136,128]{1,0:T(8,128)S(1)}, u32[]{:S(2)}, u32[]{:S(2)}) collective-permute-start(f32[136,128]{1,0:T(8,128)S(1)} %get-tuple-element.43.refs_11_), channel_id=1, source_target_pairs={{64,0},{128,64},{192,128},{0,192},{65,1},{129,65},{193,129},{1,193... | collective-permute-start | bytes 208904 | tf_op jit(solution)/shard_map/ppermute | solution.py:30
  42.9 9.8 %copy-start.2 = (f32[2,4096]{1,0:T(2,128)S(1)}, f32[2,4096]{1,0:T(2,128)}, u32[]{:S(2)}) copy-start(f32[2,4096]{1,0:T(2,128)} %tests_ref.1) | copy-start | bytes 98308
  43.0 9.8 %copy-start.3 = (s32[4096]{0:T(1024)S(1)}, s32[4096]{0:T(1024)}, u32[]{:S(2)}) copy-start(s32[4096]{0:T(1024)} %param.13) | copy-start | bytes 49156
  43.0 3.2 %collective-permute-start.17 = (f32[136,128]{1,0:T(8,128)S(1)}, f32[136,128]{1,0:T(8,128)S(1)}, u32[]{:S(2)}, u32[]{:S(2)}) collective-permute-start(f32[136,128]{1,0:T(8,128)S(1)} %shard_map.90.own_ref.refs_8_.refs_16_.image_ref), channel_id=1, source_target_pairs={{0,1},{1,0},{2,3},{3,2},{4,5},{5,4},{6,7},{7,6},{8,9},{9,8},{10,11... | collective-permute-start | bytes 208904 | tf_op jit(solution)/shard_map/ppermute | solution.py:41
  46.6 13.8 %collective-permute-start.18 = (f32[136,128]{1,0:T(8,128)S(1)}, f32[136,128]{1,0:T(8,128)S(1)}, u32[]{:S(2)}, u32[]{:S(2)}) collective-permute-start(f32[136,128]{1,0:T(8,128)S(1)} %get-tuple-element.45), channel_id=1, source_target_pairs={{4,0},{6,2},{0,4},{2,6},{5,1},{7,3},{1,5},{3,7},{12,8},{14,10},{8,... | collective-permute-start | bytes 208904 | tf_op jit(solution)/shard_map/ppermute | solution.py:30
  49.2 11.2 %collective-permute-start.19 = (f32[136,128]{1,0:T(8,128)S(1)}, f32[136,128]{1,0:T(8,128)S(1)}, u32[]{:S(2)}, u32[]{:S(2)}) collective-permute-start(f32[136,128]{1,0:T(8,128)S(1)} %get-tuple-element.46), channel_id=1, source_target_pairs={{6,0},{0,2},{2,4},{4,6},{7,1},{1,3},{3,5},{5,7},{14,8},{8,10},{10,... | collective-permute-start | bytes 208904 | tf_op jit(solution)/shard_map/ppermute | solution.py:30
  52.4 8.0 %collective-permute-start.20 = (f32[136,128]{1,0:T(8,128)S(1)}, f32[136,128]{1,0:T(8,128)S(1)}, u32[]{:S(2)}, u32[]{:S(2)}) collective-permute-start(f32[136,128]{1,0:T(8,128)S(1)} %get-tuple-element.47), channel_id=1, source_target_pairs={{2,0},{4,2},{6,4},{0,6},{3,1},{5,3},{7,5},{1,7},{10,8},{12,10},{14... | collective-permute-start | bytes 208904 | tf_op jit(solution)/shard_map/ppermute | solution.py:30
  57.3 6.0 %collective-permute-start.28 = (f32[264,128]{1,0:T(8,128)S(1)}, f32[264,128]{1,0:T(8,128)S(1)}, u32[]{:S(2)}, u32[]{:S(2)}) collective-permute-start(f32[264,128]{1,0:T(8,128)S(1)} %get-tuple-element.50), channel_id=1, source_target_pairs={{64,0},{128,64},{192,128},{0,192},{65,1},{129,65},{193,129},{1,193... | collective-permute-start | bytes 405512 | tf_op jit(solution)/shard_map/ppermute | solution.py:30
  59.9 5.4 %collective-permute-start.29 = (f32[264,128]{1,0:T(8,128)S(1)}, f32[264,128]{1,0:T(8,128)S(1)}, u32[]{:S(2)}, u32[]{:S(2)}) collective-permute-start(f32[264,128]{1,0:T(8,128)S(1)} %get-tuple-element.51), channel_id=1, source_target_pairs={{128,0},{192,64},{0,128},{64,192},{129,1},{193,65},{1,129},{65,193... | collective-permute-start | bytes 405512 | tf_op jit(solution)/shard_map/ppermute | solution.py:30
  60.4 9.5 %collective-permute-start.23 = (f32[136,128]{1,0:T(8,128)S(1)}, f32[136,128]{1,0:T(8,128)S(1)}, u32[]{:S(2)}, u32[]{:S(2)}) collective-permute-start(f32[136,128]{1,0:T(8,128)S(1)} %add_add_fusion.refs_0_), channel_id=1, source_target_pairs={{48,0},{0,16},{16,32},{32,48},{49,1},{1,17},{17,33},{33,49},{50,2}... | collective-permute-start | bytes 208904 | tf_op jit(solution)/shard_map/ppermute | solution.py:30
  60.7 9.2 %collective-permute-start.22 = (f32[136,128]{1,0:T(8,128)S(1)}, f32[136,128]{1,0:T(8,128)S(1)}, u32[]{:S(2)}, u32[]{:S(2)}) collective-permute-start(f32[136,128]{1,0:T(8,128)S(1)} %add_add_fusion.refs_0_), channel_id=1, source_target_pairs={{32,0},{48,16},{0,32},{16,48},{33,1},{49,17},{1,33},{17,49},{34,2}... | collective-permute-start | bytes 208904 | tf_op jit(solution)/shard_map/ppermute | solution.py:30
  63.0 7.5 %collective-permute-start.21 = (f32[136,128]{1,0:T(8,128)S(1)}, f32[136,128]{1,0:T(8,128)S(1)}, u32[]{:S(2)}, u32[]{:S(2)}) collective-permute-start(f32[136,128]{1,0:T(8,128)S(1)} %add_add_fusion.refs_0_), channel_id=1, source_target_pairs={{16,0},{32,16},{48,32},{0,48},{17,1},{33,17},{49,33},{1,49},{18,2}... | collective-permute-start | bytes 208904 | tf_op jit(solution)/shard_map/ppermute | solution.py:30
  63.3 8.5 %collective-permute-start.30 = (f32[264,128]{1,0:T(8,128)S(1)}, f32[264,128]{1,0:T(8,128)S(1)}, u32[]{:S(2)}, u32[]{:S(2)}) collective-permute-start(f32[264,128]{1,0:T(8,128)S(1)} %get-tuple-element.52), channel_id=1, source_target_pairs={{192,0},{0,64},{64,128},{128,192},{193,1},{1,65},{65,129},{129,193... | collective-permute-start | bytes 405512 | tf_op jit(solution)/shard_map/ppermute | solution.py:30
  65.2 6.6 %collective-permute-start.24 = (f32[136,128]{1,0:T(8,128)S(1)}, f32[136,128]{1,0:T(8,128)S(1)}, u32[]{:S(2)}, u32[]{:S(2)}) collective-permute-start(f32[136,128]{1,0:T(8,128)S(1)} %add_add_fusion.refs_0_), channel_id=1, source_target_pairs={{0,8},{8,0},{1,9},{9,1},{2,10},{10,2},{3,11},{11,3},{4,12},{12,4},... | collective-permute-start | bytes 208904 | tf_op jit(solution)/shard_map/ppermute | solution.py:45
  69.9 1.9 %collective-permute-start.27 = (f32[136,128]{1,0:T(8,128)S(1)}, f32[136,128]{1,0:T(8,128)S(1)}, u32[]{:S(2)}, u32[]{:S(2)}) collective-permute-start(f32[136,128]{1,0:T(8,128)S(1)} %collective-permute-done.23.refs_3_), channel_id=1, source_target_pairs={{0,8},{8,0},{1,9},{9,1},{2,10},{10,2},{3,11},{11,3},{4,12},{12,4},... | collective-permute-start | bytes 208904 | tf_op jit(solution)/shard_map/ppermute | solution.py:45
  69.9 1.9 %collective-permute-start.26 = (f32[136,128]{1,0:T(8,128)S(1)}, f32[136,128]{1,0:T(8,128)S(1)}, u32[]{:S(2)}, u32[]{:S(2)}) collective-permute-start(f32[136,128]{1,0:T(8,128)S(1)} %collective-permute-done.22.refs_2_), channel_id=1, source_target_pairs={{0,8},{8,0},{1,9},{9,1},{2,10},{10,2},{3,11},{11,3},{4,12},{12,4},... | collective-permute-start | bytes 208904 | tf_op jit(solution)/shard_map/ppermute | solution.py:45
  70.5 2.2 %collective-permute-start.25 = (f32[136,128]{1,0:T(8,128)S(1)}, f32[136,128]{1,0:T(8,128)S(1)}, u32[]{:S(2)}, u32[]{:S(2)}) collective-permute-start(f32[136,128]{1,0:T(8,128)S(1)} %collective-permute-done.21.refs_1_), channel_id=1, source_target_pairs={{0,8},{8,0},{1,9},{9,1},{2,10},{10,2},{3,11},{11,3},{4,12},{12,4},... | collective-permute-start | bytes 208904 | tf_op jit(solution)/shard_map/ppermute | solution.py:45
  73.9 2.0 %collective-permute-start.31 = (f32[1,128]{1,0:T(1,128)S(1)}, f32[1,128]{1,0:T(1,128)S(1)}, u32[]{:S(2)}, u32[]{:S(2)}) collective-permute-start(f32[1,128]{1,0:T(1,128)S(1)} %get-tuple-element.53), channel_id=1, source_target_pairs={{0,8},{8,0},{1,9},{9,1},{2,10},{10,2},{3,11},{11,3},{4,12},{12,4},... | collective-permute-start | bytes 1544 | tf_op jit(solution)/shard_map/ppermute | solution.py:45
  76.5 20.5 %all-to-all-start = ((f32[128,1,128]{2,1,0:T(1,128)}), f32[128,1,128]{2,1,0:T(1,128)S(1)}, u32[]{:S(2)}, u32[]{:S(2)}) async-start(f32[128,1,128]{2,1,0:T(1,128)} %broadcast_in_dim.7), calls=%async_computation | async-start | bytes 131072 | tf_op jit(solution)/shard_map/all_to_all | solution.py:304
  87.5 4.7 %collective-permute-start.32 = (f32[128,128]{1,0:T(8,128)S(1)}, f32[128,128]{1,0:T(8,128)S(1)}, u32[]{:S(2)}, u32[]{:S(2)}) collective-permute-start(f32[128,128]{1,0:T(8,128)S(1)} %get-tuple-element.57), channel_id=1, source_target_pairs={{192,0},{0,64},{64,128},{128,192},{193,1},{1,65},{65,129},{129,193... | collective-permute-start | bytes 196616 | tf_op jit(solution)/shard_map/ppermute | solution.py:30
  88.2 5.9 %collective-permute-start.33 = (f32[128,128]{1,0:T(8,128)S(1)}, f32[128,128]{1,0:T(8,128)S(1)}, u32[]{:S(2)}, u32[]{:S(2)}) collective-permute-start(f32[128,128]{1,0:T(8,128)S(1)} %get-tuple-element.58), channel_id=1, source_target_pairs={{128,0},{192,64},{0,128},{64,192},{129,1},{193,65},{1,129},{65,193... | collective-permute-start | bytes 196616 | tf_op jit(solution)/shard_map/ppermute | solution.py:30
  91.1 3.9 %collective-permute-start.34 = (f32[128,128]{1,0:T(8,128)S(1)}, f32[128,128]{1,0:T(8,128)S(1)}, u32[]{:S(2)}, u32[]{:S(2)}) collective-permute-start(f32[128,128]{1,0:T(8,128)S(1)} %get-tuple-element.59), channel_id=1, source_target_pairs={{64,0},{128,64},{192,128},{0,192},{65,1},{129,65},{193,129},{1,193... | collective-permute-start | bytes 196616 | tf_op jit(solution)/shard_map/ppermute | solution.py:30
